TPU v7x, 1024 devices: a whole 4x8x16 slice. The times are simulated.
1024 devices in a mesh: gx: 16 (over y, z_hi), gy: 16 (over z_lo, core), gz: 4 (over x).
Axes of the slice: x: 4, y: 8, z: 16 (z_hi: 2, z_lo: 8; z = z_hi * 8 + z_lo), core: 2. Of those that a mesh axis runs over, the one named last changes fastest.
Arguments:
- gas_state: float32 [5, 128, 256, 512], P(None, 'gx', 'gy', 'gz'), may hold values from -6 to 6, as said below
- section_start: float32 [5, 128, 256, 512], P(None, 'gx', 'gy', 'gz'), may hold values from -6 to 6
- drop_cell: int32 [16, 16, 4, 16, 128], P('gx', 'gy', 'gz'), may hold values from 0 to 8191
- block_tile: int32 [16, 16, 4, 16], P('gx', 'gy', 'gz'), may hold values from 0 to 1, as said below
- droplets_per_block: int32 [16, 16, 4, 16], P('gx', 'gy', 'gz'), may hold values from 0 to 128, as said below
- drop_frac: float32 [16, 16, 4, 3, 16, 128], P('gx', 'gy', 'gz'), may hold values from -0.5 to 0.5
- drop_vel: float32 [16, 16, 4, 3, 16, 128], P('gx', 'gy', 'gz'), may hold values from -6 to 6
- drop_mass: float32 [16, 16, 4, 16, 128], P('gx', 'gy', 'gz'), may hold values from 0.1 to 4
- drop_temp: float32 [16, 16, 4, 16, 128], P('gx', 'gy', 'gz'), may hold values from -6 to 6
Outputs:
- new_state: float32 [5, 128, 256, 512], P(None, 'gx', 'gy', 'gz')
Inputs may be any that keep to these rules, and one draw needn't show every extreme that they name: `gas_state`: component 0 (density) lies between 0.3 and 3.4. `drop_cell`: encodes the cell (x, y, z) within the block's tile as (x * 8 + y) * 128 + z. `block_tile`: nondecreasing along a device's blocks; blocks with count 0 carry tile 1 (the last tile). `droplets_per_block`: on each device the blocks with a positive count come first and every later block has count 0; each device has at least 4 live blocks, one of them with 128 droplets; some device has all 16 blocks live. Slot d of a block is live when d is below its count.
All inputs are finite; a program needn't handle non-finite values.
Results may differ from a plain program's by a relative error of at most 0.00057.
Values sent between devices are 32-bit elements; how exact they have to be, the bound alone decides.
No kernel may reach another device: no remote copies, remote signals or barrier semaphores. Data moves between devices by JAX's collectives and lax.ppermute only.
A program may use at most 32 MiB of HBM per device.

v0:
```python
import math

import jax
import jax.numpy as jnp
from jax import lax
from jax.sharding import PartitionSpec as P

TS = 8


PARCEL = 8.0
LATENT = 0.5
TIME_INCREMENT = 0.2
VISCOSITY = 0.5


def with_halo(cells, sides, width):
    for axis, dim in sides:
        count = lax.axis_size(axis)
        head = lax.slice_in_dim(cells, 0, width, axis=dim)
        tail = lax.slice_in_dim(cells, cells.shape[dim] - width, cells.shape[dim], axis=dim)
        cells = jnp.concatenate(
            [
                lax.ppermute(tail, axis, [(i, (i + 1) % count) for i in range(count)]),
                cells,
                lax.ppermute(head, axis, [((i + 1) % count, i) for i in range(count)]),
            ],
            axis=dim,
        )
    return cells


def cut_windows(values, tile_size):
    number = (values.shape[0] - 2) // tile_size
    trailing = values.shape[1:]
    rest_pad = [(0, 0)] * len(trailing)
    leading = values[: number * tile_size].reshape((number, tile_size) + trailing)
    upper_rows = jnp.pad(values[tile_size:], [(0, tile_size - 2)] + rest_pad)
    upper_rows = upper_rows.reshape((number, tile_size) + trailing)[:, :2]
    return jnp.concatenate([leading, upper_rows], axis=1)


def join_windows(values, tile_size):
    number = values.shape[0]
    trailing = values.shape[2:]
    rest_pad = [(0, 0)] * len(trailing)
    leading = values[:, :tile_size].reshape((number * tile_size,) + trailing)
    leading = jnp.pad(leading, [(0, 2)] + rest_pad)
    upper_rows = jnp.pad(values[:, tile_size:], [(0, 0), (0, tile_size - 2)] + rest_pad)
    upper_rows = upper_rows.reshape((number * tile_size,) + trailing)
    upper_rows = jnp.pad(upper_rows, [(tile_size, 0)] + rest_pad)[: number * tile_size + 2]
    return leading + upper_rows


def tile_footprints(padded, tile_size):
    arranged = cut_windows(jnp.moveaxis(padded, 1, 0), tile_size)
    arranged = cut_windows(jnp.moveaxis(arranged, 3, 0), tile_size)
    arranged = jnp.transpose(arranged, (2, 0, 4, 3, 1, 5))
    return arranged.reshape(arranged.shape[0] * arranged.shape[1], -1, arranged.shape[5])


def tiles_to_padded(tile_sums, tiles_x, tile_rows_along_y, components, tile_size):
    foot_width = tile_size + 2
    arranged = tile_sums.reshape(
        tiles_x, tile_rows_along_y, components, foot_width, foot_width, tile_sums.shape[2]
    )
    arranged = jnp.transpose(arranged, (0, 3, 1, 4, 2, 5))
    arranged = join_windows(arranged, tile_size)
    arranged = join_windows(jnp.moveaxis(arranged, 0, 2), tile_size)
    return jnp.transpose(arranged, (2, 1, 0, 3))


def spread(position, offset, length):
    places = jnp.arange(length, dtype=jnp.int32)[None, :, None]
    anchor = position[:, None, :]
    low_weight = (0.5 * (0.5 - offset) * (0.5 - offset))[:, None, :]
    middle = (0.75 - offset * offset)[:, None, :]
    higher = (0.5 * (0.5 + offset) * (0.5 + offset))[:, None, :]
    return (
        jnp.where(places == anchor, low_weight, 0.0)
        + jnp.where(places == anchor + 1, middle, 0.0)
        + jnp.where(places == anchor + 2, higher, 0.0)
    )


def block_weights(drop_cells, offsets, tile_size, cells_z):
    plane_size = tile_size * cells_z
    pos_x = drop_cells // plane_size
    pos_y = drop_cells // cells_z % tile_size
    pos_z = drop_cells % cells_z
    foot_width = tile_size + 2
    weight_x = spread(pos_x, offsets[0], foot_width)
    weight_y = spread(pos_y, offsets[1], foot_width)
    planar = (weight_x[:, :, None, :] * weight_y[:, None, :, :]).reshape(
        drop_cells.shape[0], foot_width * foot_width, drop_cells.shape[1]
    )
    upward_direction = spread(pos_z, offsets[2], cells_z + 2)
    return (planar, upward_direction)


def droplet_terms(gas_at, velocity, masses, temper, counts):
    slots = jnp.arange(masses.shape[1], dtype=jnp.int32)[None, :]
    alive_weight = jnp.where(slots < counts[:, None], PARCEL, 0.0)
    diameter = jnp.cbrt(masses)
    spalding = jax.nn.softplus(gas_at[:, 4] - temper)
    evaporation = diameter * jnp.log1p(spalding)
    drag_force = (diameter * gas_at[:, 0])[:, None, :] * (gas_at[:, 1:4] - velocity)
    heat_flux = diameter * (gas_at[:, 4] - temper)
    momentum = evaporation[:, None, :] * velocity - drag_force
    energy = -heat_flux - LATENT * evaporation
    stacked = jnp.concatenate([evaporation[:, None, :], momentum, energy[:, None, :]], axis=1)
    return stacked * alive_weight[:, None, :]


def neighbour(padded, dim_index, offset):
    slicer = [slice(None), slice(1, -1), slice(1, -1), slice(1, -1)]
    length = padded.shape[dim_index] - 2
    slicer[dim_index] = slice(1 + offset, 1 + offset + length)
    return padded[tuple(slicer)]


def advance(padded, gas_state, section_start, sources):
    laplace = -6.0 * gas_state
    advect = jnp.zeros_like(gas_state)
    for dim_index in (1, 2, 3):
        higher = neighbour(padded, dim_index, 1)
        lower_cells = neighbour(padded, dim_index, -1)
        laplace = laplace + higher + lower_cells
        advect = advect + gas_state[dim_index][None] * (higher - lower_cells) * 0.5
    return 0.75 * section_start + 0.25 * (
        gas_state + TIME_INCREMENT * (VISCOSITY * laplace - advect + sources)
    )


def fold_rim(values, dim_index):
    moved_axis = jnp.moveaxis(values, dim_index, 0)
    core_cells = moved_axis[2:-2].at[0].add(moved_axis[0]).at[-1].add(moved_axis[-1])
    return jnp.moveaxis(core_cells, 0, dim_index)


def local(
    gas_state,
    section_start,
    drop_cell,
    block_tile,
    droplets_per_block,
    drop_frac,
    drop_vel,
    drop_mass,
    drop_temp,
):
    components, cells_x, cells_y, cells_z = gas_state.shape
    padded = with_halo(gas_state, (("gx", 1), ("gy", 2), ("gz", 3)), 1)
    footprints = tile_footprints(padded.astype(jnp.bfloat16), TS)
    drop_cells = drop_cell.reshape(drop_cell.shape[3:])
    tile_ids = block_tile.reshape(block_tile.shape[3:])
    counts = droplets_per_block.reshape(droplets_per_block.shape[3:])
    offsets = drop_frac.reshape(drop_frac.shape[3:])
    velocity = drop_vel.reshape(drop_vel.shape[3:])
    masses = drop_mass.reshape(drop_mass.shape[3:])
    temper = drop_temp.reshape(drop_temp.shape[3:])
    blocks, block_size = drop_cells.shape
    group_size = math.gcd(blocks, 8)
    tile_count = footprints.shape[0]
    owners_table = jnp.arange(tile_count, dtype=jnp.int32)[None, :]

    def deposit_group(turn_index, running):
        first_block = turn_index * group_size

        def window(values, dim_index):
            return lax.dynamic_slice_in_dim(values, first_block, group_size, dim_index)

        group_ids = window(tile_ids, 0)
        planar, upward_direction = block_weights(
            window(drop_cells, 0), window(offsets, 1), TS, cells_z
        )
        planar = planar.astype(jnp.bfloat16)
        upward_direction = upward_direction.astype(jnp.bfloat16)
        source_portions = jnp.take(footprints, group_ids, axis=0)
        nearby_gas_values = jnp.einsum(
            "gsy,gyn->gsn", source_portions, upward_direction, preferred_element_type=jnp.float32
        )
        gas_at = jnp.sum(
            nearby_gas_values.reshape(group_size, components, -1, block_size) * planar[:, None],
            axis=2,
        )
        sources = droplet_terms(
            gas_at,
            jnp.transpose(window(velocity, 1), (1, 0, 2)),
            window(masses, 0),
            window(temper, 0),
            window(counts, 0),
        )
        weight_scaled_terms = (
            (planar[:, None] * sources[:, :, None, :])
            .astype(jnp.bfloat16)
            .reshape(group_size, -1, block_size)
        )
        spread_sources = jnp.einsum(
            "peh,pch->pec",
            weight_scaled_terms,
            upward_direction,
            preferred_element_type=jnp.float32,
        )
        owners = (group_ids[:, None] == owners_table).astype(jnp.float32)
        return running + jnp.einsum(
            "bt,bkz->tkz", owners, spread_sources, precision=lax.Precision.HIGHEST
        )

    start_sums = jnp.zeros((tile_count,) + footprints.shape[1:], jnp.float32)
    turn_count = blocks // group_size
    tile_sums = lax.fori_loop(0, turn_count, deposit_group, start_sums)
    spread_sources = tiles_to_padded(tile_sums, cells_x // TS, cells_y // TS, components, TS)
    folded = fold_rim(with_halo(spread_sources, (("gx", 1),), 1), 1)
    folded = fold_rim(with_halo(folded, (("gy", 2),), 1), 2)
    sources = fold_rim(with_halo(folded, (("gz", 3),), 1), 3)
    return advance(padded, gas_state, section_start, sources)


def solution(mesh):
    in_specs = (
        P(None, "gx", "gy", "gz"),
        P(None, "gx", "gy", "gz"),
        P("gx", "gy", "gz", None, None),
        P("gx", "gy", "gz", None),
        P("gx", "gy", "gz", None),
        P("gx", "gy", "gz", None, None, None),
        P("gx", "gy", "gz", None, None, None),
        P("gx", "gy", "gz", None, None),
        P("gx", "gy", "gz", None, None),
    )
    out_specs = P(None, "gx", "gy", "gz")
    return jax.shard_map(local, mesh=mesh, in_specs=in_specs, out_specs=out_specs, check_vma=False)
```

profile of v0, /device:TPU:6, one launch (start us, length us, event | category | flops | bytes accessed | tf_op | source)
XLA Modules:
  0.0 149.8 jit_solution(12793696086656706261)
XLA Ops:
  0.0 0.8 fusion.46
  0.8 19.3 %collective-permute-start.1 = (f32[5,1,16,128]{3,2,0,1:T(8,128)S(1)}, f32[5,1,16,128]{3,2,0,1:T(8,128)S(1)}, u32[]{:S(2)}, u32[]{:S(2)}) collective-permute-start(f32[5,1,16,128]{3,2,0,1:T(8,128)S(1)} %get-tuple-element.522), channel_id=1, source_target_pairs={{0,64},{64,128},{128,192},{192,256},{256,320},{320,384},{384,448},... | collective-permute-start | bytes 122888 | tf_op jit(solution)/shard_map/ppermute | solution.py:24
  20.2 4.8 %collective-permute-start = (f32[5,1,16,128]{3,2,0,1:T(8,128)S(1)}, f32[5,1,16,128]{3,2,0,1:T(8,128)S(1)}, u32[]{:S(2)}, u32[]{:S(2)}) collective-permute-start(f32[5,1,16,128]{3,2,0,1:T(8,128)S(1)} %get-tuple-element.521), channel_id=1, source_target_pairs={{64,0},{128,64},{192,128},{256,192},{320,256},{384,320},{448,384},... | collective-permute-start | bytes 122888 | tf_op jit(solution)/shard_map/ppermute | solution.py:26
  25.1 1.0 constant_dynamic-update-slice_fusion.1
  26.2 9.7 %collective-permute-done = f32[5,1,16,128]{3,2,0,1:T(8,128)S(1)} collective-permute-done((f32[5,1,16,128]{3,2,0,1:T(8,128)S(1)}, f32[5,1,16,128]{3,2,0,1:T(8,128)S(1)}, u32[]{:S(2)}, u32[]{:S(2)}) %collective-permute-start) | collective-permute-done | bytes 40992 | tf_op jit(solution)/shard_map/ppermute | solution.py:26
  36.0 6.6 %collective-permute-start.2 = (f32[5,10,1,128]{3,2,0,1:T(1,128)S(1)}, f32[5,10,1,128]{3,2,0,1:T(1,128)S(1)}, u32[]{:S(2)}, u32[]{:S(2)}) collective-permute-start(f32[5,10,1,128]{3,2,0,1:T(1,128)S(1)} %get-tuple-element.517), channel_id=1, source_target_pairs={{4,0},{8,4},{12,8},{16,12},{20,16},{24,20},{28,24},{32,28},{36,32}... | collective-permute-start | bytes 76808 | tf_op jit(solution)/shard_map/ppermute | solution.py:26
  42.6 1.9 %collective-permute-start.3 = (f32[5,10,1,128]{3,2,0,1:T(1,128)S(1)}, f32[5,10,1,128]{3,2,0,1:T(1,128)S(1)}, u32[]{:S(2)}, u32[]{:S(2)}) collective-permute-start(f32[5,10,1,128]{3,2,0,1:T(1,128)S(1)} %get-tuple-element.516), channel_id=1, source_target_pairs={{0,4},{4,8},{8,12},{12,16},{16,20},{20,24},{24,28},{28,32},{32,36}... | collective-permute-start | bytes 76808 | tf_op jit(solution)/shard_map/ppermute | solution.py:24
  44.5 9.8 %collective-permute-done.3 = f32[5,10,1,128]{3,2,0,1:T(1,128)S(1)} collective-permute-done((f32[5,10,1,128]{3,2,0,1:T(1,128)S(1)}, f32[5,10,1,128]{3,2,0,1:T(1,128)S(1)}, u32[]{:S(2)}, u32[]{:S(2)}) %collective-permute-start.3) | collective-permute-done | bytes 25632 | tf_op jit(solution)/shard_map/ppermute | solution.py:24
  55.1 2.4 %collective-permute-start.5 = (f32[5,10,18,1]{2,3,1,0:T(1,128)S(1)}, f32[5,10,18,1]{2,3,1,0:T(1,128)S(1)}, u32[]{:S(2)}, u32[]{:S(2)}) collective-permute-start(f32[5,10,18,1]{2,3,1,0:T(1,128)S(1)} %copy.77), channel_id=1, source_target_pairs={{0,1},{1,2},{2,3},{3,0},{4,5},{5,6},{6,7},{7,4},{8,9},{9,10},{10,1... | collective-permute-start | bytes 10808 | tf_op jit(solution)/shard_map/ppermute | solution.py:24
  57.9 3.4 %collective-permute-start.4 = (f32[5,10,18,1]{2,3,1,0:T(1,128)S(1)}, f32[5,10,18,1]{2,3,1,0:T(1,128)S(1)}, u32[]{:S(2)}, u32[]{:S(2)}) collective-permute-start(f32[5,10,18,1]{2,3,1,0:T(1,128)S(1)} %copy.75), channel_id=1, source_target_pairs={{1,0},{2,1},{3,2},{0,3},{5,4},{6,5},{7,6},{4,7},{9,8},{10,9},{11,1... | collective-permute-start | bytes 10808 | tf_op jit(solution)/shard_map/ppermute | solution.py:26
  61.5 0.4 copy.81
  61.9 2.9 %collective-permute-done.4 = f32[5,10,18,1]{2,3,1,0:T(1,128)S(1)} collective-permute-done((f32[5,10,18,1]{2,3,1,0:T(1,128)S(1)}, f32[5,10,18,1]{2,3,1,0:T(1,128)S(1)}, u32[]{:S(2)}, u32[]{:S(2)}) %collective-permute-start.4) | collective-permute-done | bytes 3632 | tf_op jit(solution)/shard_map/ppermute | solution.py:26
  64.8 0.6 copy-done.14
  65.4 0.4 copy.82
  67.2 0.7 pad_maximum_fusion.1
  68.1 12.6 %while.23 = (s32[]{:T(128)}, f32[2,500,130]{1,0,2:T(2,128)S(1)}, s32[16]{0:T(128)S(1)}, s32[16,128]{1,0:T(8,128)S(1)}, f32[3,16,128]{2,1,0:T(8,128)S(1)}, /*inde...) while((s32[]{:T(128)}, f32[2,500,130]{1,0,2:T(2,128)S(1)}, ...), condition=%wide.region_2.3_spmd.clone, body=%wide.region_0.2_spmd.clone.sunk | while | flops 284528960 | bytes 20749924 | solution.py:212
  68.4 0.7 gather_fusion
  69.0 0.8 fusion.61
  70.9 0.8 fusion.64
  71.8 2.7 %fusion.65 = f32[2,500,130]{1,0,2:T(2,128)S(1)} fusion(f32[8,500,130]{1,2,0:T(8,128)S(1)} %fusion.64, f32[2,500,130]{1,0,2:T(2,128)S(1)} %get-tuple-element.649, pred[]{:T(512)S(6)} %compare.65, s32[8]{0:T(128)S(1)} %get-tuple-element.609), kind=kOutput, calls=%fused_computation.9.clone.1 | convolution fusion | flops 12740016 | bytes 3120033 | tf_op jit(solution)/shard_map/while/body/eval_jaxpr/bt,bkz->tkz/dot_general | solution.py:206
  74.6 0.7 gather_fusion
  75.3 0.8 fusion.61
  77.2 0.8 fusion.64
  78.1 2.7 %fusion.65 = f32[2,500,130]{1,0,2:T(2,128)S(1)} fusion(f32[8,500,130]{1,2,0:T(8,128)S(1)} %fusion.64, f32[2,500,130]{1,0,2:T(2,128)S(1)} %get-tuple-element.649, pred[]{:T(512)S(6)} %compare.65, s32[8]{0:T(128)S(1)} %get-tuple-element.609), kind=kOutput, calls=%fused_computation.9.clone.1 | convolution fusion | flops 12740016 | bytes 3120033 | tf_op jit(solution)/shard_map/while/body/eval_jaxpr/bt,bkz->tkz/dot_general | solution.py:206
  80.7 1.3 copy.86
  82.1 0.5 slice_bitcast_fusion.2
  83.0 0.5 slice.437
  84.0 3.7 %collective-permute-start.6 = (f32[5,1,18,130]{3,2,0,1:T(8,128)S(1)}, f32[5,1,18,130]{3,2,0,1:T(8,128)S(1)}, u32[]{:S(2)}, u32[]{:S(2)}) collective-permute-start(f32[5,1,18,130]{3,2,0,1:T(8,128)S(1)} %get-tuple-element.508), channel_id=1, source_target_pairs={{0,64},{64,128},{128,192},{192,256},{256,320},{320,384},{384,448},... | collective-permute-start | bytes 140408 | tf_op jit(solution)/shard_map/ppermute | solution.py:24
  87.7 12.9 %collective-permute-start.7 = (f32[5,1,18,130]{3,2,0,1:T(8,128)S(1)}, f32[5,1,18,130]{3,2,0,1:T(8,128)S(1)}, u32[]{:S(2)}, u32[]{:S(2)}) collective-permute-start(f32[5,1,18,130]{3,2,0,1:T(8,128)S(1)} %get-tuple-element.509), channel_id=1, source_target_pairs={{64,0},{128,64},{192,128},{256,192},{320,256},{384,320},{448,384},... | collective-permute-start | bytes 140408 | tf_op jit(solution)/shard_map/ppermute | solution.py:26
  100.7 2.6 %collective-permute-done.6 = f32[5,1,18,130]{3,2,0,1:T(8,128)S(1)} collective-permute-done((f32[5,1,18,130]{3,2,0,1:T(8,128)S(1)}, f32[5,1,18,130]{3,2,0,1:T(8,128)S(1)}, u32[]{:S(2)}, u32[]{:S(2)}) %collective-permute-start.6) | collective-permute-done | bytes 46832 | tf_op jit(solution)/shard_map/ppermute | solution.py:24
  103.3 1.1 collective-permute-done.7
  104.7 1.9 %collective-permute-start.8 = (f32[5,8,1,130]{3,2,0,1:T(1,128)S(1)}, f32[5,8,1,130]{3,2,0,1:T(1,128)S(1)}, u32[]{:S(2)}, u32[]{:S(2)}) collective-permute-start(f32[5,8,1,130]{3,2,0,1:T(1,128)S(1)} %get-tuple-element.510), channel_id=1, source_target_pairs={{0,4},{4,8},{8,12},{12,16},{16,20},{20,24},{24,28},{28,32},{32,36}... | collective-permute-start | bytes 62408 | tf_op jit(solution)/shard_map/ppermute | solution.py:24
  106.7 10.6 %collective-permute-start.9 = (f32[5,8,1,130]{3,2,0,1:T(1,128)S(1)}, f32[5,8,1,130]{3,2,0,1:T(1,128)S(1)}, u32[]{:S(2)}, u32[]{:S(2)}) collective-permute-start(f32[5,8,1,130]{3,2,0,1:T(1,128)S(1)} %get-tuple-element.511), channel_id=1, source_target_pairs={{4,0},{8,4},{12,8},{16,12},{20,16},{24,20},{28,24},{32,28},{36,32}... | collective-permute-start | bytes 62408 | tf_op jit(solution)/shard_map/ppermute | solution.py:26
  117.3 1.5 collective-permute-done.9
  119.0 1.8 %scatter-add.24 = f32[16,5,8,130]{3,0,1,2:T(8,128)S(1)} dynamic-update-slice(f32[16,5,8,130]{3,0,1,2:T(8,128)S(1)} %slice.448, f32[1,5,8,130]{3,0,1,2:T(1,128)S(1)} %slice_add_fusion.5, s32[]{:T(128)} %constant.386.clone.1, s32[]{:T(128)} %constant.386.clone.1, s32[]{:T(128)} %constant.386.clone.1, s32[]{:T(128)} %constant.386.clone.1) | dynamic-update-slice | bytes 41604 | tf_op jit(solution)/shard_map/scatter-add | solution.py:137
  121.0 1.8 %scatter-add.25 = f32[16,5,8,130]{3,0,1,2:T(8,128)S(1)} dynamic-update-slice(f32[16,5,8,130]{3,0,1,2:T(8,128)S(1)} %scatter-add.24, f32[1,5,8,130]{3,0,1,2:T(1,128)S(1)} %slice_add_fusion.4, s32[]{:T(128)} %constant.390.clone.1, s32[]{:T(128)} %constant.386.clone.1, s32[]{:T(128)} %constant.386.clone.1, s32[]{:T(128)} %constant.386.clone.1) | dynamic-update-slice | bytes 41604 | tf_op jit(solution)/shard_map/scatter-add | solution.py:137
  123.0 4.1 %collective-permute-start.10 = (f32[5,8,16,1]{3,2,0,1:T(8,128)S(1)}, f32[5,8,16,1]{3,2,0,1:T(8,128)S(1)}, u32[]{:S(2)}, u32[]{:S(2)}) collective-permute-start(f32[5,8,16,1]{3,2,0,1:T(8,128)S(1)} %get-tuple-element.512), channel_id=1, source_target_pairs={{0,1},{1,2},{2,3},{3,0},{4,5},{5,6},{6,7},{7,4},{8,9},{9,10},{10,1... | collective-permute-start | bytes 7688 | tf_op jit(solution)/shard_map/ppermute | solution.py:24
  127.1 2.3 %collective-permute-start.11 = (f32[5,8,16,1]{3,2,0,1:T(8,128)S(1)}, f32[5,8,16,1]{3,2,0,1:T(8,128)}, u32[]{:S(2)}, u32[]{:S(2)}) collective-permute-start(f32[5,8,16,1]{3,2,0,1:T(8,128)S(1)} %get-tuple-element.513), channel_id=1, source_target_pairs={{1,0},{2,1},{3,2},{0,3},{5,4},{6,5},{7,6},{4,7},{9,8},{10,9},{11,1... | collective-permute-start | bytes 7688 | tf_op jit(solution)/shard_map/ppermute | solution.py:26
  129.4 0.7 slice_bitcast_fusion.7
  130.1 0.4 copy.76
  130.5 1.2 copy.78
  131.6 0.8 collective-permute-done.10
  132.5 4.9 %collective-permute-done.11 = f32[5,8,16,1]{3,2,0,1:T(8,128)} collective-permute-done((f32[5,8,16,1]{3,2,0,1:T(8,128)S(1)}, f32[5,8,16,1]{3,2,0,1:T(8,128)}, u32[]{:S(2)}, u32[]{:S(2)}) %collective-permute-start.11) | collective-permute-done | bytes 2592 | tf_op jit(solution)/shard_map/ppermute | solution.py:26
  137.4 1.3 maximum_bitcast_fusion.2
  139.0 2.8 %scatter-add.26 = f32[128,5,8,16]{0,3,1,2:T(8,128)S(1)} dynamic-update-slice(f32[128,5,8,16]{0,3,1,2:T(8,128)S(1)} %slice.455, f32[1,5,8,16]{0,3,1,2:T(8,128)S(1)} %slice_add_fusion.1, s32[]{:T(128)} %constant.386.clone.1, s32[]{:T(128)} %constant.386.clone.1, s32[]{:T(128)} %constant.386.clone.1, s32[]{:T(128)} %constant.386.clone.1) | dynamic-update-slice | bytes 5124 | tf_op jit(solution)/shard_map/scatter-add | solution.py:137
  142.1 5.3 %scatter-add.29 = f32[128,5,8,16]{0,3,1,2:T(8,128)S(1)} dynamic-update-slice(f32[128,5,8,16]{0,3,1,2:T(8,128)S(1)} %scatter-add.26, f32[1,5,8,16]{0,3,1,2:T(8,128)S(1)} %slice_add_fusion, s32[]{:T(128)} %constant.391.clone.1, s32[]{:T(128)} %constant.386.clone.1, s32[]{:T(128)} %constant.386.clone.1, s32[]{:T(128)} %constant.386.clone.1) | dynamic-update-slice | bytes 5124 | tf_op jit(solution)/shard_map/scatter-add | solution.py:137
  147.4 1.6 %fusion.36 = f32[5,8,16,128]{3,2,0,1:T(8,128)S(1)} fusion(f32[5,8,16,128]{3,2,0,1:T(8,128)S(1)} %copy.89, f32[128,5,8,16]{0,3,1,2:T(8,128)S(1)} %scatter-add.29, f32[5,8,16,128]{3,2,1,0:T(8,128)} %param.24, f32[5,10,1,128]{3,2,0,1:T(1,128)S(1)} %collective-permute-done.2, f32[5,10,16,128]{3,2,0,1:T(8,128)S(1)} %copy-done.1, ...), kind=kLoop, calls=%fused_computation.119 | loop fusion | flops 2785280 | bytes 2057248 | tf_op jit(solution)/shard_map/add | solution.py:130
  149.0 0.8 copy.90
  (131 shorter events, 7.4 us)
Async XLA Ops:
  0.8 24.3 %collective-permute-start.1 = (f32[5,1,16,128]{3,2,0,1:T(8,128)S(1)}, f32[5,1,16,128]{3,2,0,1:T(8,128)S(1)}, u32[]{:S(2)}, u32[]{:S(2)}) collective-permute-start(f32[5,1,16,128]{3,2,0,1:T(8,128)S(1)} %get-tuple-element.522), channel_id=1, source_target_pairs={{0,64},{64,128},{128,192},{192,256},{256,320},{320,384},{384,448},... | collective-permute-start | bytes 122888 | tf_op jit(solution)/shard_map/ppermute | solution.py:24
  20.2 15.7 %collective-permute-start = (f32[5,1,16,128]{3,2,0,1:T(8,128)S(1)}, f32[5,1,16,128]{3,2,0,1:T(8,128)S(1)}, u32[]{:S(2)}, u32[]{:S(2)}) collective-permute-start(f32[5,1,16,128]{3,2,0,1:T(8,128)S(1)} %get-tuple-element.521), channel_id=1, source_target_pairs={{64,0},{128,64},{192,128},{256,192},{320,256},{384,320},{448,384},... | collective-permute-start | bytes 122888 | tf_op jit(solution)/shard_map/ppermute | solution.py:26
  25.1 17.4 %copy-start.10 = (f32[5,1,16,128]{3,2,0,1:T(8,128)}, f32[5,1,16,128]{3,2,0,1:T(8,128)S(1)}, u32[]{:S(2)}) copy-start(f32[5,1,16,128]{3,2,0,1:T(8,128)S(1)} %collective-permute-done.1) | copy-start | bytes 122884
  35.9 6.7 %copy-start.11 = (f32[5,1,16,128]{3,2,0,1:T(8,128)}, f32[5,1,16,128]{3,2,0,1:T(8,128)S(1)}, u32[]{:S(2)}) copy-start(f32[5,1,16,128]{3,2,0,1:T(8,128)S(1)} %collective-permute-done) | copy-start | bytes 122884
  35.9 25.4 %copy-start = (f32[5,10,16,128]{3,2,0,1:T(8,128)}, f32[5,10,16,128]{3,2,0,1:T(8,128)S(1)}, u32[]{:S(2)}) copy-start(f32[5,10,16,128]{3,2,0,1:T(8,128)S(1)} %constant_dynamic-update-slice_fusion) | copy-start | bytes 1228804
  36.0 8.6 %collective-permute-start.2 = (f32[5,10,1,128]{3,2,0,1:T(1,128)S(1)}, f32[5,10,1,128]{3,2,0,1:T(1,128)S(1)}, u32[]{:S(2)}, u32[]{:S(2)}) collective-permute-start(f32[5,10,1,128]{3,2,0,1:T(1,128)S(1)} %get-tuple-element.517), channel_id=1, source_target_pairs={{4,0},{8,4},{12,8},{16,12},{20,16},{24,20},{28,24},{32,28},{36,32}... | collective-permute-start | bytes 76808 | tf_op jit(solution)/shard_map/ppermute | solution.py:26
  42.6 11.8 %collective-permute-start.3 = (f32[5,10,1,128]{3,2,0,1:T(1,128)S(1)}, f32[5,10,1,128]{3,2,0,1:T(1,128)S(1)}, u32[]{:S(2)}, u32[]{:S(2)}) collective-permute-start(f32[5,10,1,128]{3,2,0,1:T(1,128)S(1)} %get-tuple-element.516), channel_id=1, source_target_pairs={{0,4},{4,8},{8,12},{12,16},{16,20},{20,24},{24,28},{28,32},{32,36}... | collective-permute-start | bytes 76808 | tf_op jit(solution)/shard_map/ppermute | solution.py:24
  54.3 7.0 %copy-start.7 = (f32[5,10,1,128]{3,2,0,1:T(1,128)}, f32[5,10,1,128]{3,2,0,1:T(1,128)S(1)}, u32[]{:S(2)}) copy-start(f32[5,10,1,128]{3,2,0,1:T(1,128)S(1)} %collective-permute-done.3) | copy-start | bytes 76804
  55.1 6.4 %collective-permute-start.5 = (f32[5,10,18,1]{2,3,1,0:T(1,128)S(1)}, f32[5,10,18,1]{2,3,1,0:T(1,128)S(1)}, u32[]{:S(2)}, u32[]{:S(2)}) collective-permute-start(f32[5,10,18,1]{2,3,1,0:T(1,128)S(1)} %copy.77), channel_id=1, source_target_pairs={{0,1},{1,2},{2,3},{3,0},{4,5},{5,6},{6,7},{7,4},{8,9},{9,10},{10,1... | collective-permute-start | bytes 10808 | tf_op jit(solution)/shard_map/ppermute | solution.py:24
  57.9 6.9 %collective-permute-start.4 = (f32[5,10,18,1]{2,3,1,0:T(1,128)S(1)}, f32[5,10,18,1]{2,3,1,0:T(1,128)S(1)}, u32[]{:S(2)}, u32[]{:S(2)}) collective-permute-start(f32[5,10,18,1]{2,3,1,0:T(1,128)S(1)} %copy.75), channel_id=1, source_target_pairs={{1,0},{2,1},{3,2},{0,3},{5,4},{6,5},{7,6},{4,7},{9,8},{10,9},{11,1... | collective-permute-start | bytes 10808 | tf_op jit(solution)/shard_map/ppermute | solution.py:26
  61.5 4.9 %copy-start.13 = (f32[5,10,18,1]{2,3,1,0:T(1,128)}, f32[5,10,18,1]{2,3,1,0:T(1,128)S(1)}, u32[]{:S(2)}) copy-start(f32[5,10,18,1]{2,3,1,0:T(1,128)S(1)} %collective-permute-done.5) | copy-start | bytes 10804
  64.8 0.6 copy-start.14
  66.6 1.5 copy-start.3
  66.6 1.5 copy-start.9
  66.6 1.5 copy-start.12
  66.6 1.5 copy-start.16
  66.6 1.5 copy-start.17
  66.6 1.5 copy-start.18
  66.6 1.5 copy-start.19
  84.0 19.3 %collective-permute-start.6 = (f32[5,1,18,130]{3,2,0,1:T(8,128)S(1)}, f32[5,1,18,130]{3,2,0,1:T(8,128)S(1)}, u32[]{:S(2)}, u32[]{:S(2)}) collective-permute-start(f32[5,1,18,130]{3,2,0,1:T(8,128)S(1)} %get-tuple-element.508), channel_id=1, source_target_pairs={{0,64},{64,128},{128,192},{192,256},{256,320},{320,384},{384,448},... | collective-permute-start | bytes 140408 | tf_op jit(solution)/shard_map/ppermute | solution.py:24
  87.7 16.7 %collective-permute-start.7 = (f32[5,1,18,130]{3,2,0,1:T(8,128)S(1)}, f32[5,1,18,130]{3,2,0,1:T(8,128)S(1)}, u32[]{:S(2)}, u32[]{:S(2)}) collective-permute-start(f32[5,1,18,130]{3,2,0,1:T(8,128)S(1)} %get-tuple-element.509), channel_id=1, source_target_pairs={{64,0},{128,64},{192,128},{256,192},{320,256},{384,320},{448,384},... | collective-permute-start | bytes 140408 | tf_op jit(solution)/shard_map/ppermute | solution.py:26
  104.7 12.5 %collective-permute-start.8 = (f32[5,8,1,130]{3,2,0,1:T(1,128)S(1)}, f32[5,8,1,130]{3,2,0,1:T(1,128)S(1)}, u32[]{:S(2)}, u32[]{:S(2)}) collective-permute-start(f32[5,8,1,130]{3,2,0,1:T(1,128)S(1)} %get-tuple-element.510), channel_id=1, source_target_pairs={{0,4},{4,8},{8,12},{12,16},{16,20},{20,24},{24,28},{28,32},{32,36}... | collective-permute-start | bytes 62408 | tf_op jit(solution)/shard_map/ppermute | solution.py:24
  106.7 22.7 %copy-start.2 = (f32[5,8,16,128]{3,2,1,0:T(8,128)S(1)}, f32[5,8,16,128]{3,2,1,0:T(8,128)}, u32[]{:S(2)}) copy-start(f32[5,8,16,128]{3,2,1,0:T(8,128)} %param.23) | copy-start | bytes 983044
  106.7 12.0 %collective-permute-start.9 = (f32[5,8,1,130]{3,2,0,1:T(1,128)S(1)}, f32[5,8,1,130]{3,2,0,1:T(1,128)S(1)}, u32[]{:S(2)}, u32[]{:S(2)}) collective-permute-start(f32[5,8,1,130]{3,2,0,1:T(1,128)S(1)} %get-tuple-element.511), channel_id=1, source_target_pairs={{4,0},{8,4},{12,8},{16,12},{20,16},{24,20},{28,24},{32,28},{36,32}... | collective-permute-start | bytes 62408 | tf_op jit(solution)/shard_map/ppermute | solution.py:26
  118.9 11.2 %copy-start.15 = (f32[5,10,18,1]{2,3,1,0:T(1,128)S(1)}, f32[5,10,18,1]{2,3,1,0:T(1,128)}, u32[]{:S(2)}) copy-start(f32[5,10,18,1]{2,3,1,0:T(1,128)} %copy-done.14) | copy-start | bytes 10804
  123.0 9.5 %collective-permute-start.10 = (f32[5,8,16,1]{3,2,0,1:T(8,128)S(1)}, f32[5,8,16,1]{3,2,0,1:T(8,128)S(1)}, u32[]{:S(2)}, u32[]{:S(2)}) collective-permute-start(f32[5,8,16,1]{3,2,0,1:T(8,128)S(1)} %get-tuple-element.512), channel_id=1, source_target_pairs={{0,1},{1,2},{2,3},{3,0},{4,5},{5,6},{6,7},{7,4},{8,9},{9,10},{10,1... | collective-permute-start | bytes 7688 | tf_op jit(solution)/shard_map/ppermute | solution.py:24
  127.1 10.3 %collective-permute-start.11 = (f32[5,8,16,1]{3,2,0,1:T(8,128)S(1)}, f32[5,8,16,1]{3,2,0,1:T(8,128)}, u32[]{:S(2)}, u32[]{:S(2)}) collective-permute-start(f32[5,8,16,1]{3,2,0,1:T(8,128)S(1)} %get-tuple-element.513), channel_id=1, source_target_pairs={{1,0},{2,1},{3,2},{0,3},{5,4},{6,5},{7,6},{4,7},{9,8},{10,9},{11,1... | collective-permute-start | bytes 7688 | tf_op jit(solution)/shard_map/ppermute | solution.py:26
  138.7 8.7 %copy-start.1 = (f32[5,10,16,128]{3,2,0,1:T(8,128)S(1)}, f32[5,10,16,128]{3,2,0,1:T(8,128)}, u32[]{:S(2)}) copy-start(f32[5,10,16,128]{3,2,0,1:T(8,128)} %copy-done) | copy-start | bytes 1228804
  138.7 8.7 %copy-start.4 = (f32[8,16,128]{2,1,0:T(8,128)S(1)}, f32[8,16,128]{2,1,0:T(8,128)}, u32[]{:S(2)}) copy-start(f32[8,16,128]{2,1,0:T(8,128)} %get-tuple-element.518) | copy-start | bytes 196612
  138.7 8.7 %copy-start.5 = (f32[8,16,128]{2,1,0:T(8,128)S(1)}, f32[8,16,128]{2,1,0:T(8,128)}, u32[]{:S(2)}) copy-start(f32[8,16,128]{2,1,0:T(8,128)} %get-tuple-element.519) | copy-start | bytes 196612
  138.7 8.7 %copy-start.6 = (f32[8,16,128]{2,1,0:T(8,128)S(1)}, f32[8,16,128]{2,1,0:T(8,128)}, u32[]{:S(2)}) copy-start(f32[8,16,128]{2,1,0:T(8,128)} %get-tuple-element.520) | copy-start | bytes 196612
  138.7 8.7 %copy-start.8 = (f32[5,10,1,128]{3,2,0,1:T(1,128)S(1)}, f32[5,10,1,128]{3,2,0,1:T(1,128)}, u32[]{:S(2)}) copy-start(f32[5,10,1,128]{3,2,0,1:T(1,128)} %copy-done.7) | copy-start | bytes 76804
where the time goes:
time: 150 us
  starting transfers between devices  74 us (49%)
  waiting for transfers between devices  33.5 us (22%)
  local copies, waits for them, and re-layouts  25.5 us (17%)
  matrix products  8.55 us (6%)
  other arithmetic  7.18 us (5%)
    ppermute x6, starting transfers between devices, with_halo(): lax.ppermute(head, axis, [((i + 1) % count, i) for i in range(count)])  40.6 us
    ppermute x6, starting transfers between devices, with_halo(): lax.ppermute(tail, axis, [(i, (i + 1) % count) for i in range(count)])  33.4 us
    ppermute x6, waiting for transfers between devices, with_halo(): lax.ppermute(head, axis, [((i + 1) % count, i) for i in range(count)])  20.1 us
    ppermute x6, waiting for transfers between devices, with_halo(): lax.ppermute(tail, axis, [(i, (i + 1) % count) for i in range(count)])  13.4 us
    scatter-add x4, local copies, waits for them, and re-layouts, fold_rim(): moved_axis[2:-2].at[0].add(moved_axis[0]).at[-1].add(moved_axis[-1])  11.8 us
    dot_general x2, matrix products, deposit_group(): jnp.einsum('bt,bkz->tkz', owners, spread_sources, precision=lax.Precision...  5.32 us
  transfers between devices with their start and end apart: 12, of which 9 were waited for; matrix products, arithmetic and copies ran while one was open for 3% of the time, Pallas kernels for 0%

commit v1 on v0

v1 whole, which is shorter than its diff:
```python
import jax
import jax.numpy as jnp
from jax import lax
from jax.experimental import pallas as pl
from jax.experimental.pallas import tpu as pltpu
from jax.sharding import PartitionSpec as P

PARCEL = 8.0
LATENT = 0.5
TIME_INCREMENT = 0.2
VISCOSITY = 0.5

AXES = ("gx", "gy", "gz")
F32 = jnp.float32
BF16 = jnp.bfloat16
I32 = jnp.int32
FAR_AWAY = -100

OWN = 128
HALO = 64


def swaps(shape):
    nx, ny, nz = shape

    def pairs(target):
        out = []
        for i in range(nx):
            for j in range(ny):
                for k in range(nz):
                    a, b, c = target(i, j, k)
                    out.append(((i * ny + j) * nz + k, (a * ny + b) * nz + c))
        return out

    def d_side(i, j, k):
        if j == 0:
            return (i ^ 1, ny - 1, k)
        if j == ny - 1:
            return (i ^ 1, 0, k)
        return (i, ((j - 1) ^ 1) + 1, k)

    return {
        "A": pairs(lambda i, j, k: (i ^ 1, j, k)),
        "B": pairs(lambda i, j, k: ((i + 2) % nx if i % 2 == 0 else (i - 2) % nx, j, k)),
        "C": pairs(lambda i, j, k: (i, j ^ 1, k)),
        "D": pairs(d_side),
        "up": pairs(lambda i, j, k: (i, j, (k + 1) % nz)),
        "down": pairs(lambda i, j, k: (i, j, (k - 1) % nz)),
    }


def places():
    i, j = lax.axis_index("gx"), lax.axis_index("gy")
    odd_i, odd_j = lax.rem(i, 2), lax.rem(j, 2)
    wrap = jnp.logical_or(j == 0, j == lax.axis_size("gy") - 1)
    return odd_i, odd_j, wrap


def rows(start, size, unit):
    return pl.ds(pl.multiple_of(start, unit), size)


def choose(cond, yes, no):
    pl.when(cond)(yes)
    pl.when(jnp.logical_not(cond))(no)


def pack_y(gas, to_c, to_d):
    _, odd_j, _ = places()

    def put(ref, y):
        for c in range(5):
            ref[c * 8 : c * 8 + 8, :] = gas[pl.ds(c * OWN + y, 8, stride=16), :]

    def even():
        put(to_c, 15)
        put(to_d, 0)

    def odd():
        put(to_c, 0)
        put(to_d, 15)

    choose(odd_j == 0, even, odd)


def pack_a(gas, from_c, from_d, to_a):
    odd_i, _, _ = places()
    near = (1 - odd_i) * 112
    for c in range(5):
        at = c * 48
        to_a[at : at + 16, :] = gas[rows(c * OWN + near, 16, 16), :]
        to_a[at + 16 : at + 32, :] = gas[rows(c * OWN + 112 - near, 16, 16), :]
        to_a[at + 32 : at + 40, :] = from_c[c * 8 : c * 8 + 8, :]
        to_a[at + 40 : at + 48, :] = from_d[c * 8 : c * 8 + 8, :]


def pack_b(from_a, from_d, after, to_b):
    del after
    odd_i, _, wrap = places()
    far = (1 - odd_i) * 7
    for c in range(5):
        to_b[c * 24 : c * 24 + 16, :] = from_a[c * 48 + 16 : c * 48 + 32, :]
        to_b[c * 24 + 16 : c * 24 + 24, :] = jnp.zeros((8, 128), F32)
        to_b[c * 24 + 16 : c * 24 + 17, :] = from_a[pl.ds(c * 48 + 32 + far, 1), :]

    def wrapped():
        for c in range(5):
            to_b[c * 24 + 17 : c * 24 + 18, :] = from_d[pl.ds(c * 8 + far, 1), :]

    def inner():
        for c in range(5):
            to_b[c * 24 + 17 : c * 24 + 18, :] = from_a[pl.ds(c * 48 + 40 + far, 1), :]

    choose(wrap, wrapped, inner)


def join_halo(gas, from_c, from_d, from_a, from_b, halo, z_low, z_high):
    odd_i, _, wrap = places()
    near = odd_i * 7
    for c in range(5):
        at = c * HALO
        halo[at : at + 16, :] = from_a[c * 48 : c * 48 + 16, :]
        halo[at + 16 : at + 32, :] = from_b[c * 24 : c * 24 + 16, :]
        halo[at + 32 : at + 40, :] = from_c[c * 8 : c * 8 + 8, :]
        halo[at + 40 : at + 48, :] = jnp.zeros((8, 128), F32)
        halo[at + 40 : at + 41, :] = from_a[pl.ds(c * 48 + 32 + near, 1), :]
        halo[at + 41 : at + 42, :] = from_b[c * 24 + 16 : c * 24 + 17, :]
        halo[at + 56 : at + 64, :] = jnp.zeros((8, 128), F32)
        halo[at + 57 : at + 58, :] = from_b[c * 24 + 17 : c * 24 + 18, :]
    halo[5 * HALO : 384, :] = jnp.zeros((384 - 5 * HALO, 128), F32)

    def wrapped():
        for c in range(5):
            halo[c * HALO + 48 : c * HALO + 56, :] = from_a[c * 48 + 40 : c * 48 + 48, :]
            halo[c * HALO + 56 : c * HALO + 57, :] = from_d[pl.ds(c * 8 + near, 1), :]

    def inner():
        for c in range(5):
            halo[c * HALO + 48 : c * HALO + 56, :] = from_d[c * 8 : c * 8 + 8, :]
            halo[c * HALO + 56 : c * HALO + 57, :] = from_a[pl.ds(c * 48 + 40 + near, 1), :]

    choose(wrap, wrapped, inner)
    for n in range(8):
        part = gas[n * 128 : n * 128 + 128, :] if n < 5 else halo[(n - 5) * 128 : (n - 4) * 128, :]
        turned = part.T
        z_low[n : n + 1, :] = turned[0:1, :]
        z_high[n : n + 1, :] = turned[127:128, :]


def three(place, anchor, offset):
    low = 0.5 * (0.5 - offset) * (0.5 - offset)
    middle = 0.75 - offset * offset
    high = 0.5 * (0.5 + offset) * (0.5 + offset)
    step = place - anchor
    return jnp.where(step == -1, low, jnp.where(step == 0, middle, jnp.where(step == 1, high, 0.0)))


def weigh(gas, cell, shift, frac, after, planar, vertical, part):
    del after
    odd_i, odd_j, _ = places()
    blocks = cell.shape[0]
    near_x, far_x = 8 - 9 * odd_i, 9 * odd_i - 1
    c_y, d_y = 16 - 17 * odd_j, 17 * odd_j - 1
    r = lax.broadcasted_iota(I32, (192, 128), 0)
    q = r & 15
    group = (r >> 4) - 8
    on_y = jnp.where(q < 8, q, jnp.where(q == 8, near_x, jnp.where(q == 9, far_x, FAR_AWAY)))
    place_x = jnp.where(group < 0, r >> 4, jnp.where(group == 0, near_x, jnp.where(group == 1, far_x, on_y)))
    place_y = jnp.where(group == 2, c_y, jnp.where(group == 3, d_y, q))
    s = lax.broadcasted_iota(I32, (144, 128), 0)
    place_z = jnp.where(s < 128, s, jnp.where(s == 128, -1, jnp.where(s == 129, 128, FAR_AWAY)))
    cells = gas[...].astype(BF16)
    for b in range(blocks):
        lanes = slice(b * 128, b * 128 + 128)
        at = cell[b : b + 1, :]
        wx = three(place_x, at >> 10, frac[b : b + 1, :])
        wy = three(place_y, ((at >> 7) & 7) + shift[b : b + 1, :], frac[blocks + b : blocks + b + 1, :])
        wz = three(place_z, at & 127, frac[2 * blocks + b : 2 * blocks + b + 1, :]).astype(BF16)
        flat = (wx * wy).astype(BF16)
        planar[0:192, lanes] = flat
        planar[192:256, lanes] = jnp.zeros((64, 128), BF16)
        vertical[0:144, lanes] = wz
        vertical[144:256, lanes] = jnp.zeros((112, 128), BF16)
        seen = jnp.dot(cells, wz[0:128, :], preferred_element_type=F32)
        own = flat[0:128, :].astype(F32)
        for c in range(5):
            part[c * blocks + b : c * blocks + b + 1, :] = jnp.sum(
                seen[c * OWN : c * OWN + OWN, :] * own, axis=0, keepdims=True
            )


def deposit(
    halo, z_below, z_above, planar, vertical, part, diameter, alive, vel, temp, sums, ghost_low, ghost_high,
    gas_at, source, weighted, total,
):
    blocks = diameter.shape[0]

    def z_rows(ref):
        v = ref[...]
        turned = pltpu.roll(v, 64, 1)
        side = jnp.concatenate(
            [v[5:6], turned[5:6], v[6:7], turned[6:7], v[7:8], jnp.zeros((3, 128), F32)], axis=0
        )
        return jnp.concatenate([v, side], axis=1)

    ends = jnp.concatenate([z_rows(z_below), z_rows(z_above)], axis=0).astype(BF16)
    at_ends = jnp.dot(ends, planar[...], preferred_element_type=F32)
    around = halo[0 : 5 * HALO, :].astype(BF16)
    for b in range(blocks):
        lanes = slice(b * 128, b * 128 + 128)
        seen = jnp.dot(around, vertical[0:128, lanes], preferred_element_type=F32)
        side = planar[128:192, lanes].astype(F32)
        edge = vertical[128:144, lanes].astype(F32)
        ended = at_ends[0:8, lanes] * edge[0:1, :] + at_ends[8:16, lanes] * edge[1:2, :]
        for c in range(5):
            n = c * blocks + b
            gas_at[n : n + 1, :] = (
                part[n : n + 1, :]
                + ended[c : c + 1, :]
                + jnp.sum(seen[c * HALO : c * HALO + HALO, :] * side, axis=0, keepdims=True)
            )
    d = diameter[...]
    live = alive[...]
    warm = gas_at[4 * blocks : 5 * blocks, :] - temp[...]
    soft = jnp.maximum(warm, 0.0) + jnp.log1p(jnp.exp(-jnp.abs(warm)))
    rate = d * jnp.log1p(soft)
    pull = d * gas_at[0:blocks, :]
    source[0:blocks, :] = rate * live
    for m in range(3):
        v = vel[m * blocks : (m + 1) * blocks, :]
        u = gas_at[(m + 1) * blocks : (m + 2) * blocks, :]
        source[(m + 1) * blocks : (m + 2) * blocks, :] = (rate * v - pull * (u - v)) * live
    source[4 * blocks : 5 * blocks, :] = (-(d * warm) - LATENT * rate) * live
    for b in range(blocks):
        lanes = slice(b * 128, b * 128 + 128)
        flat = planar[0:192, lanes].astype(F32)
        for c in range(5):
            scaled = (flat * source[c * blocks + b : c * blocks + b + 1, :]).astype(BF16)
            weighted[c * OWN : c * OWN + OWN, lanes] = scaled[0:128, :]
            weighted[640 + c * HALO : 640 + c * HALO + HALO, lanes] = scaled[128:192, :]
        weighted[960:1024, lanes] = jnp.zeros((64, 128), BF16)
    total[...] = lax.dot_general(
        weighted[...], vertical[...], (((1,), (1,)), ((), ())), preferred_element_type=F32
    )
    sums[...] = total[0:960, 0:128]
    for n in range(8):
        turned = total[n * 128 : n * 128 + 128, 128:256].T
        ghost_low[n : n + 1, :] = turned[0:1, :]
        ghost_high[n : n + 1, :] = turned[1:2, :]


def upright(below, above):
    z = lax.broadcasted_iota(I32, (128, 128), 0)
    return jnp.where(z == 0, below, jnp.where(z == 127, above, 0.0)).T


def fold_z(sums, below, above, own, sides, to_c, to_d):
    for n in range(8):
        extra = upright(below[n : n + 1, :], above[n : n + 1, :])
        if n < 5:
            own[n * OWN : n * OWN + OWN, :] = sums[n * OWN : n * OWN + OWN, :] + extra
            continue
        for half in range(2):
            c = (n - 5) * 2 + half
            if c > 4:
                continue
            at = 640 + c * HALO
            here = sums[at : at + HALO, :] + extra[half * 64 : half * 64 + 64, :]
            sides[c * 32 : c * 32 + 32, :] = here[0:32, :]
            to_c[c * 16 : c * 16 + 16, :] = here[32:48, :]
            to_d[c * 16 : c * 16 + 16, :] = here[48:64, :]


def fold_y(sides, from_c, from_d, to_a):
    _, odd_j, wrap = places()
    keep = jnp.where(wrap, 0.0, 1.0).astype(F32)
    y = lax.broadcasted_iota(I32, (16, 128), 0)
    c_y = 15 - 15 * odd_j
    at_c, at_d = y == c_y, y == 15 - c_y
    for c in range(5):
        for side in range(2):
            row = c * 16 + 8 + side
            to_a[c * 40 + side * 16 : c * 40 + side * 16 + 16, :] = (
                sides[c * 32 + side * 16 : c * 32 + side * 16 + 16, :]
                + jnp.where(at_c, from_c[row : row + 1, :], 0.0)
                + jnp.where(at_d, from_d[row : row + 1, :] * keep, 0.0)
            )
        to_a[c * 40 + 32 : c * 40 + 40, :] = from_d[c * 16 : c * 16 + 8, :]


def relay_b(from_a, from_d, after, to_b):
    del after
    _, odd_j, wrap = places()
    gate = jnp.where(wrap, 1.0, 0.0).astype(F32)
    at_d = lax.broadcasted_iota(I32, (16, 128), 0) == 15 * odd_j
    for c in range(5):
        to_b[c * 16 : c * 16 + 16, :] = from_a[c * 40 + 16 : c * 40 + 32, :] + jnp.where(
            at_d, from_d[c * 16 + 9 : c * 16 + 10, :] * gate, 0.0
        )


def stencil(gas, start, halo, z_below, z_above, own, from_c, from_d, after, out, upper):
    del after
    odd_i, odd_j, wrap = places()
    keep = jnp.where(wrap, 0.0, 1.0).astype(F32)
    y = lax.broadcasted_iota(I32, (16, 128), 0)
    z = lax.broadcasted_iota(I32, (16, 128), 1)
    c_y = 15 - 15 * odd_j
    at_c, at_d = y == c_y, y == 15 - c_y
    near = (1 - odd_i) * 7
    high_x, low_x = 16 * odd_i, 16 - 16 * odd_i
    high_y, low_y = 32 + 16 * odd_j, 48 - 16 * odd_j
    for c in range(5):
        upper[...] = upright(z_below[c : c + 1, :], z_above[c : c + 1, :])
        for x in range(8):
            at = c * OWN + x * 16
            g = gas[at : at + 16, :]
            if x < 7:
                x_up = gas[at + 16 : at + 32, :]
            else:
                x_up = halo[rows(c * HALO + high_x, 16, 16), :]
            if x > 0:
                x_down = gas[at - 16 : at, :]
            else:
                x_down = halo[rows(c * HALO + low_x, 16, 16), :]
            y_up = jnp.where(y == 15, halo[pl.ds(c * HALO + high_y + x, 1), :], pltpu.roll(g, 15, 0))
            y_down = jnp.where(y == 0, halo[pl.ds(c * HALO + low_y + x, 1), :], pltpu.roll(g, 1, 0))
            ends = upper[x * 16 : x * 16 + 16, :]
            z_up = jnp.where(z == 127, ends, pltpu.roll(g, 127, 1))
            z_down = jnp.where(z == 0, ends, pltpu.roll(g, 1, 1))
            laplace = -6.0 * g + (x_up + x_down) + (y_up + y_down) + (z_up + z_down)
            advect = 0.5 * (
                gas[OWN + x * 16 : OWN + x * 16 + 16, :] * (x_up - x_down)
                + gas[2 * OWN + x * 16 : 2 * OWN + x * 16 + 16, :] * (y_up - y_down)
                + gas[3 * OWN + x * 16 : 3 * OWN + x * 16 + 16, :] * (z_up - z_down)
            )
            across = jnp.where(wrap & (near == x), 1.0, 0.0).astype(F32)
            added = (
                own[at : at + 16, :]
                + jnp.where(at_c, from_c[c * 16 + x : c * 16 + x + 1, :], 0.0)
                + jnp.where(
                    at_d,
                    from_d[c * 16 + x : c * 16 + x + 1, :] * keep + from_d[c * 16 + 8 : c * 16 + 9, :] * across,
                    0.0,
                )
            )
            out[at : at + 16, :] = 0.75 * start[at : at + 16, :] + 0.25 * (
                g + TIME_INCREMENT * (VISCOSITY * laplace - advect + added)
            )


def finish(base, from_a, from_b, out):
    odd_i, odd_j, wrap = places()
    near = (1 - odd_i) * 112
    scale = 0.25 * TIME_INCREMENT
    out[...] = base[...]
    for c in range(5):
        at = rows(c * OWN + near, 16, 16)
        out[at, :] = out[at, :] + scale * from_a[c * 40 : c * 40 + 16, :]
        at = rows(c * OWN + 112 - near, 16, 16)
        out[at, :] = out[at, :] + scale * from_b[c * 16 : c * 16 + 16, :]

    def across(y):
        def add():
            for c in range(5):
                at = pl.ds(c * OWN + y, 8, stride=16)
                out[at, :] = out[at, :] + scale * from_a[c * 40 + 32 : c * 40 + 40, :]

        return add

    pl.when(wrap & (odd_j == 0))(across(0))
    pl.when(wrap & (odd_j == 1))(across(15))


def call(body, name, out_shapes, *operands, loose=(), scratch=(), flops=10000):
    whole = pl.BlockSpec(memory_space=pltpu.VMEM)
    anywhere = pl.BlockSpec(memory_space=pl.ANY)
    single = not isinstance(out_shapes, list)
    outs = [out_shapes] if single else out_shapes
    result = pl.pallas_call(
        body,
        name=name,
        out_shape=[jax.ShapeDtypeStruct(s, t) for s, t in outs],
        in_specs=[anywhere if n in loose else whole for n in range(len(operands))],
        out_specs=[whole] * len(outs),
        scratch_shapes=list(scratch),
        compiler_params=pltpu.CompilerParams(vmem_limit_bytes=24 * 1024 * 1024),
        cost_estimate=pl.CostEstimate(flops=flops, bytes_accessed=100000, transcendentals=0),
    )(*operands)
    return result[0] if single else result


def local(gas_state, section_start, drop_cell, block_tile, droplets_per_block, drop_frac, drop_vel, drop_mass, drop_temp):
    shape = tuple(lax.axis_size(a) for a in AXES)
    routes = swaps(shape)

    def send(values, route):
        return lax.ppermute(values, AXES, routes[route])

    blocks = drop_cell.shape[3]
    gas = gas_state.reshape(640, 128)
    start = section_start.reshape(640, 128)
    cell = drop_cell.reshape(blocks, 128)
    frac = drop_frac.reshape(3 * blocks, 128)
    vel = drop_vel.reshape(3 * blocks, 128)
    temp = drop_temp.reshape(blocks, 128)
    diameter = jnp.cbrt(drop_mass.reshape(blocks, 128))
    slots = lax.broadcasted_iota(I32, (blocks, 128), 1)
    alive = jnp.where(slots < droplets_per_block.reshape(blocks, 1), PARCEL, 0.0).astype(F32)
    shift = jnp.broadcast_to(8 * block_tile.reshape(blocks, 1), (blocks, 128)).astype(I32)

    to_c, to_d = call(pack_y, "pack_y", [((40, 128), F32)] * 2, gas)
    gas_c, gas_d = send(to_c, "C"), send(to_d, "D")
    to_a = call(pack_a, "pack_a", ((240, 128), F32), gas, gas_c, gas_d)
    gas_a = send(to_a, "A")
    planar, vertical, part = call(
        weigh,
        "weigh",
        [((256, blocks * 128), BF16), ((256, blocks * 128), BF16), ((5 * blocks, 128), F32)],
        gas, cell, shift, frac, to_a,
        loose=(4,), flops=1 << 32,
    )
    gas_b = send(call(pack_b, "pack_b", ((120, 128), F32), gas_a, gas_d, part, loose=(2,)), "B")
    halo, low, high = call(
        join_halo, "join_halo", [((384, 128), F32), ((8, 128), F32), ((8, 128), F32)],
        gas, gas_c, gas_d, gas_a, gas_b,
    )
    above, below = send(low, "down"), send(high, "up")
    sums, low, high = call(
        deposit, "deposit", [((960, 128), F32), ((8, 128), F32), ((8, 128), F32)],
        halo, below, above, planar, vertical, part, diameter, alive, vel, temp,
        scratch=[
            pltpu.VMEM((5 * blocks, 128), F32),
            pltpu.VMEM((5 * blocks, 128), F32),
            pltpu.VMEM((1024, blocks * 128), BF16),
            pltpu.VMEM((1024, 256), F32),
        ],
    )
    dep_above, dep_below = send(low, "down"), send(high, "up")
    own, sides, to_c, to_d = call(
        fold_z, "fold_z", [((640, 128), F32), ((160, 128), F32), ((80, 128), F32), ((80, 128), F32)],
        sums, dep_below, dep_above,
    )
    dep_c, dep_d = send(to_c, "C"), send(to_d, "D")
    to_a = call(fold_y, "fold_y", ((200, 128), F32), sides, dep_c, dep_d)
    dep_a = send(to_a, "A")
    base = call(
        stencil, "stencil", ((640, 128), F32),
        gas, start, halo, below, above, own, dep_c, dep_d, to_a,
        loose=(8,), scratch=[pltpu.VMEM((128, 128), F32)], flops=1 << 32,
    )
    dep_b = send(call(relay_b, "relay_b", ((80, 128), F32), dep_a, dep_d, base, loose=(2,)), "B")
    out = call(finish, "finish", ((640, 128), F32), base, dep_a, dep_b)
    return out.reshape(gas_state.shape)


def solution(mesh):
    in_specs = (
        P(None, "gx", "gy", "gz"),
        P(None, "gx", "gy", "gz"),
        P("gx", "gy", "gz", None, None),
        P("gx", "gy", "gz", None),
        P("gx", "gy", "gz", None),
        P("gx", "gy", "gz", None, None, None),
        P("gx", "gy", "gz", None, None, None),
        P("gx", "gy", "gz", None, None),
        P("gx", "gy", "gz", None, None),
    )
    return jax.shard_map(local, mesh=mesh, in_specs=in_specs, out_specs=P(None, "gx", "gy", "gz"), check_vma=False)
```

time: 150 us -> 111 us (0.74)
  local copies, waits for them, and re-layouts: 25.5 us -> 1.11 us
  starting transfers between devices: 74 us -> 55.9 us
  waiting for transfers between devices: 33.5 us -> 46.9 us
  matrix products: 8.55 us -> 0 us
  other arithmetic: 7.18 us -> 0.08 us
  Pallas kernels: 0 us -> 6.06 us
    ppermute x12, starting transfers between devices: 74 us -> 55.9 us  [send(): return lax.ppermute(values, AXES, routes[route])]
    ppermute x12, waiting for transfers between devices: 33.5 us -> 46.9 us  [send(): return lax.ppermute(values, AXES, routes[route])]
    scatter-add x4 -> x0, local copies, waits for them, and re-layouts: 11.8 us -> none  [fold_rim(): moved_axis[2:-2].at[0].add(moved_axis[0]).at[-1].add(moved_axis[-1])]
    dot_general x6 -> x0, matrix products: 8.55 us -> none  [the longest x2 5.32 us: deposit_group(): jnp.einsum('bt,bkz->tkz', owners, spread_sources, precision=lax.Precision...]
    pallas_call x0 -> x11, Pallas kernels: none -> 6.06 us  [call(): pl.pallas_call(body, name=name, out_shape=[jax.ShapeDtypeStruct(s, t) for...]
    slice x19 -> x0, local copies, waits for them, and re-layouts: 3.03 us -> none  [the longest x2 1.2 us: with_halo(): head = lax.slice_in_dim(cells, 0, width, axis=dim)]
    transpose x7 -> x0, other arithmetic: 2.64 us -> none  [the longest x3 1.59 us: fold_rim(): moved_axis = jnp.moveaxis(values, dim_index, 0)]
    add x17 -> x0, other arithmetic: 2.28 us -> none  [the longest x1 1.61 us: advance(): 0.75 * section_start]
  transfers between devices with their start and end apart: 12 -> 12, of which waited for: 9 -> 8; matrix products, arithmetic and copies ran while one was open for 3% -> 0% of each run, Pallas kernels for 0% -> 2%
where the time goes in v1:
time: 111 us; the launch traced here: 110 us
  starting transfers between devices  55.9 us (50%)
  waiting for transfers between devices  46.9 us (42%)
  Pallas kernels  6.06 us (5%)
  local copies, waits for them, and re-layouts  1.11 us (1%)
    ppermute x12, starting transfers between devices, send(): return lax.ppermute(values, AXES, routes[route])  55.9 us
    ppermute x12, waiting for transfers between devices, send(): return lax.ppermute(values, AXES, routes[route])  46.9 us
    pallas_call x11, Pallas kernels, call(): pl.pallas_call(body, name=name, out_shape=[jax.ShapeDtypeStruct(s, t) for...  6.06 us
  transfers between devices with their start and end apart: 12, of which 8 were waited for; matrix products, arithmetic and copies ran while one was open for 0% of the time, Pallas kernels for 2%

profile of v1, /device:TPU:6, one launch (start us, length us, event | category | flops | bytes accessed | tf_op | source)
XLA Modules:
  0.0 110.4 jit_solution(18356919364779326546)
XLA Ops:
  0.0 0.0 copy-start
  0.0 1.0 copy-done
  1.0 0.0 copy-start.9
  1.0 1.9 %collective-permute-start = (f32[40,128]{1,0:T(8,128)S(1)}, f32[40,128]{1,0:T(8,128)S(1)}, u32[]{:S(2)}, u32[]{:S(2)}) collective-permute-start(f32[40,128]{1,0:T(8,128)S(1)} %get-tuple-element.20), channel_id=1, source_target_pairs={{0,4},{1,5},{2,6},{3,7},{4,0},{5,1},{6,2},{7,3},{8,12},{9,13},{10,... | collective-permute-start | bytes 61448 | tf_op jit(solution)/shard_map/ppermute | solution.py:398
  2.9 18.3 %collective-permute-start.1 = (f32[40,128]{1,0:T(8,128)S(1)}, f32[40,128]{1,0:T(8,128)S(1)}, u32[]{:S(2)}, u32[]{:S(2)}) collective-permute-start(f32[40,128]{1,0:T(8,128)S(1)} %get-tuple-element.21), channel_id=1, source_target_pairs={{0,124},{1,125},{2,126},{3,127},{4,8},{5,9},{6,10},{7,11},{8,4},{9... | collective-permute-start | bytes 61448 | tf_op jit(solution)/shard_map/ppermute | solution.py:398
  21.3 0.0 copy-done.9
  21.3 0.0 copy-start.5
  21.3 0.0 collective-permute-done.from_c
  21.3 1.4 %collective-permute-done.1.from_d = f32[40,128]{1,0:T(8,128)S(1)} collective-permute-done((f32[40,128]{1,0:T(8,128)S(1)}, f32[40,128]{1,0:T(8,128)S(1)}, u32[]{:S(2)}, u32[]{:S(2)}) %collective-permute-start.1) | collective-permute-done | bytes 20512 | tf_op jit(solution)/shard_map/ppermute | solution.py:398
  22.7 0.0 copy-start.6
  22.8 5.9 %collective-permute-start.2 = (f32[240,128]{1,0:T(8,128)S(1)}, f32[240,128]{1,0:T(8,128)S(1)}, u32[]{:S(2)}, u32[]{:S(2)}) collective-permute-start(f32[240,128]{1,0:T(8,128)S(1)} %pack_a.1.after), channel_id=1, source_target_pairs={{0,64},{1,65},{2,66},{3,67},{4,68},{5,69},{6,70},{7,71},{8,72},{9,... | collective-permute-start | bytes 368648 | tf_op jit(solution)/shard_map/ppermute | solution.py:398
  28.6 0.1 broadcast_in_dim.13.shift
  28.7 0.0 copy-done.5
  28.7 0.0 copy-done.6
  28.7 2.1 %weigh.1 = (bf16[256,2048]{1,0:T(8,128)(2,1)S(1)}, bf16[256,2048]{1,0:T(8,128)(2,1)S(1)}, f32[80,128]{1,0:T(8,128)S(1)}) custom-call(f32[640,128]{1,0:T(8,128)S(1)} %bitcast.14, s32[16,128]{1,0:T(8,128)S(1)} %bitcast.21, s32[16,128]{1,0:T(8,128)S(1)} %broadcast_in_dim.13.shift, f32[48,128]{1,0:T(8,128)S(1)} %bitcast.20, f32[240,128]{1,0:T(8,128)S(1)} %pack_a.1.after), custom_call_target="tpu_custom_call" | custom-call | flops 4294967296 | bytes 100000 | tf_op jit(solution)/shard_map/weigh/pallas_call | solution.py:380
  30.8 9.2 %collective-permute-done.2.from_a = f32[240,128]{1,0:T(8,128)S(1)} collective-permute-done((f32[240,128]{1,0:T(8,128)S(1)}, f32[240,128]{1,0:T(8,128)S(1)}, u32[]{:S(2)}, u32[]{:S(2)}) %collective-permute-start.2) | collective-permute-done | bytes 122912 | tf_op jit(solution)/shard_map/ppermute | solution.py:398
  40.1 3.5 %collective-permute-start.3 = (f32[120,128]{1,0:T(8,128)S(1)}, f32[120,128]{1,0:T(8,128)S(1)}, u32[]{:S(2)}, u32[]{:S(2)}) collective-permute-start(f32[120,128]{1,0:T(8,128)S(1)} %pack_b.1), channel_id=1, source_target_pairs={{0,128},{1,129},{2,130},{3,131},{4,132},{5,133},{6,134},{7,135},{8... | collective-permute-start | bytes 184328 | tf_op jit(solution)/shard_map/ppermute | solution.py:398
  43.5 0.0 copy-done.7
  43.6 4.0 %collective-permute-done.3.from_b = f32[120,128]{1,0:T(8,128)S(1)} collective-permute-done((f32[120,128]{1,0:T(8,128)S(1)}, f32[120,128]{1,0:T(8,128)S(1)}, u32[]{:S(2)}, u32[]{:S(2)}) %collective-permute-start.3) | collective-permute-done | bytes 61472 | tf_op jit(solution)/shard_map/ppermute | solution.py:398
  47.6 0.0 copy-done.1
  47.6 0.2 join_halo.1
  47.8 7.3 %collective-permute-start.4 = (f32[8,128]{1,0:T(8,128)S(1)}, f32[8,128]{1,0:T(8,128)S(1)}, u32[]{:S(2)}, u32[]{:S(2)}) collective-permute-start(f32[8,128]{1,0:T(8,128)S(1)} %get-tuple-element.24), channel_id=1, source_target_pairs={{0,1},{1,2},{2,3},{3,0},{4,5},{5,6},{6,7},{7,4},{8,9},{9,10},{10,1... | collective-permute-start | bytes 12296 | tf_op jit(solution)/shard_map/ppermute | solution.py:398
  55.1 0.0 copy-start.8
  55.1 1.9 %collective-permute-start.5 = (f32[8,128]{1,0:T(8,128)S(1)}, f32[8,128]{1,0:T(8,128)S(1)}, u32[]{:S(2)}, u32[]{:S(2)}) collective-permute-start(f32[8,128]{1,0:T(8,128)S(1)} %get-tuple-element.25), channel_id=1, source_target_pairs={{0,3},{1,0},{2,1},{3,2},{4,7},{5,4},{6,5},{7,6},{8,11},{9,8},{10,9... | collective-permute-start | bytes 12296 | tf_op jit(solution)/shard_map/ppermute | solution.py:398
  57.1 0.0 copy-done.8
  57.1 0.0 copy-start.3
  57.1 0.1 fusion.alive
  57.1 0.0 collective-permute-done.4.z_below
  57.2 4.7 %collective-permute-done.5.z_above = f32[8,128]{1,0:T(8,128)S(1)} collective-permute-done((f32[8,128]{1,0:T(8,128)S(1)}, f32[8,128]{1,0:T(8,128)S(1)}, u32[]{:S(2)}, u32[]{:S(2)}) %collective-permute-start.5) | collective-permute-done | bytes 4128 | tf_op jit(solution)/shard_map/ppermute | solution.py:398
  61.8 0.0 copy-done.2
  61.8 0.0 copy-done.3
  61.8 2.2 %deposit.1 = (f32[960,128]{1,0:T(8,128)S(1)}, f32[8,128]{1,0:T(8,128)S(1)}, f32[8,128]{1,0:T(8,128)S(1)}) custom-call(f32[384,128]{1,0:T(8,128)S(1)} %get-tuple-element.23.halo, f32[8,128]{1,0:T(8,128)S(1)} %collective-permute-done.4.z_below, f32[8,128]{1,0:T(8,128)S(1)} %collective-permute-done.5.z_above, bf16[256,2048]{1,0:T(8,128)(2,1)S(1)} %get-tuple-element.26.planar, ...), custom_call_target="tpu_custom_call" | custom-call | flops 10000 | bytes 100000 | tf_op jit(solution)/shard_map/deposit/pallas_call | solution.py:380
  64.0 1.9 %collective-permute-start.6 = (f32[8,128]{1,0:T(8,128)S(1)}, f32[8,128]{1,0:T(8,128)S(1)}, u32[]{:S(2)}, u32[]{:S(2)}) collective-permute-start(f32[8,128]{1,0:T(8,128)S(1)} %get-tuple-element.29), channel_id=1, source_target_pairs={{0,1},{1,2},{2,3},{3,0},{4,5},{5,6},{6,7},{7,4},{8,9},{9,10},{10,1... | collective-permute-start | bytes 12296 | tf_op jit(solution)/shard_map/ppermute | solution.py:398
  65.9 3.9 %collective-permute-start.7 = (f32[8,128]{1,0:T(8,128)S(1)}, f32[8,128]{1,0:T(8,128)S(1)}, u32[]{:S(2)}, u32[]{:S(2)}) collective-permute-start(f32[8,128]{1,0:T(8,128)S(1)} %get-tuple-element.30), channel_id=1, source_target_pairs={{0,3},{1,0},{2,1},{3,2},{4,7},{5,4},{6,5},{7,6},{8,11},{9,8},{10,9... | collective-permute-start | bytes 12296 | tf_op jit(solution)/shard_map/ppermute | solution.py:398
  69.9 0.0 collective-permute-done.6.below
  69.9 2.8 %collective-permute-done.7.above = f32[8,128]{1,0:T(8,128)S(1)} collective-permute-done((f32[8,128]{1,0:T(8,128)S(1)}, f32[8,128]{1,0:T(8,128)S(1)}, u32[]{:S(2)}, u32[]{:S(2)}) %collective-permute-start.7) | collective-permute-done | bytes 4128 | tf_op jit(solution)/shard_map/ppermute | solution.py:398
  72.6 0.2 fold_z.1
  72.9 1.9 %collective-permute-start.8 = (f32[80,128]{1,0:T(8,128)S(1)}, f32[80,128]{1,0:T(8,128)S(1)}, u32[]{:S(2)}, u32[]{:S(2)}) collective-permute-start(f32[80,128]{1,0:T(8,128)S(1)} %get-tuple-element.32), channel_id=1, source_target_pairs={{0,4},{1,5},{2,6},{3,7},{4,0},{5,1},{6,2},{7,3},{8,12},{9,13},{10,... | collective-permute-start | bytes 122888 | tf_op jit(solution)/shard_map/ppermute | solution.py:398
  74.8 1.9 %collective-permute-start.9 = (f32[80,128]{1,0:T(8,128)S(1)}, f32[80,128]{1,0:T(8,128)S(1)}, u32[]{:S(2)}, u32[]{:S(2)}) collective-permute-start(f32[80,128]{1,0:T(8,128)S(1)} %get-tuple-element.33), channel_id=1, source_target_pairs={{0,124},{1,125},{2,126},{3,127},{4,8},{5,9},{6,10},{7,11},{8,4},{9... | collective-permute-start | bytes 122888 | tf_op jit(solution)/shard_map/ppermute | solution.py:398
  76.7 0.0 collective-permute-done.8.from_c
  76.7 4.6 %collective-permute-done.9.from_d = f32[80,128]{1,0:T(8,128)S(1)} collective-permute-done((f32[80,128]{1,0:T(8,128)S(1)}, f32[80,128]{1,0:T(8,128)S(1)}, u32[]{:S(2)}, u32[]{:S(2)}) %collective-permute-start.9) | collective-permute-done | bytes 40992 | tf_op jit(solution)/shard_map/ppermute | solution.py:398
  81.3 5.5 %collective-permute-start.10 = (f32[200,128]{1,0:T(8,128)S(1)}, f32[200,128]{1,0:T(8,128)S(1)}, u32[]{:S(2)}, u32[]{:S(2)}) collective-permute-start(f32[200,128]{1,0:T(8,128)S(1)} %fold_y.1.after), channel_id=1, source_target_pairs={{0,64},{1,65},{2,66},{3,67},{4,68},{5,69},{6,70},{7,71},{8,72},{9,... | collective-permute-start | bytes 307208 | tf_op jit(solution)/shard_map/ppermute | solution.py:398
  86.9 0.0 copy-done.4
  86.9 0.5 stencil.1.after.base
  87.4 15.0 %collective-permute-done.10.from_a = f32[200,128]{1,0:T(8,128)S(1)} collective-permute-done((f32[200,128]{1,0:T(8,128)S(1)}, f32[200,128]{1,0:T(8,128)S(1)}, u32[]{:S(2)}, u32[]{:S(2)}) %collective-permute-start.10) | collective-permute-done | bytes 102432 | tf_op jit(solution)/shard_map/ppermute | solution.py:398
  102.5 1.9 %collective-permute-start.11 = (f32[80,128]{1,0:T(8,128)S(1)}, f32[80,128]{1,0:T(8,128)S(1)}, u32[]{:S(2)}, u32[]{:S(2)}) collective-permute-start(f32[80,128]{1,0:T(8,128)S(1)} %relay_b.1), channel_id=1, source_target_pairs={{0,128},{1,129},{2,130},{3,131},{4,132},{5,133},{6,134},{7,135},{8... | collective-permute-start | bytes 122888 | tf_op jit(solution)/shard_map/ppermute | solution.py:398
  104.4 5.2 %collective-permute-done.11.from_b = f32[80,128]{1,0:T(8,128)S(1)} collective-permute-done((f32[80,128]{1,0:T(8,128)S(1)}, f32[80,128]{1,0:T(8,128)S(1)}, u32[]{:S(2)}, u32[]{:S(2)}) %collective-permute-start.11) | collective-permute-done | bytes 40992 | tf_op jit(solution)/shard_map/ppermute | solution.py:398
  109.6 0.8 finish.1
  (11 shorter events, 0.1 us)
Async XLA Ops:
  0.0 1.0 copy-start
  1.0 20.3 %copy-start.9 = (s32[1,1,1,16]{3,2,1,0:T(1,128)S(1)}, s32[1,1,1,16]{3,2,1,0:T(1,128)}, u32[]{:S(2)}) copy-start(s32[1,1,1,16]{3,2,1,0:T(1,128)} %param.12) | copy-start | bytes 196
  1.0 20.3 %collective-permute-start = (f32[40,128]{1,0:T(8,128)S(1)}, f32[40,128]{1,0:T(8,128)S(1)}, u32[]{:S(2)}, u32[]{:S(2)}) collective-permute-start(f32[40,128]{1,0:T(8,128)S(1)} %get-tuple-element.20), channel_id=1, source_target_pairs={{0,4},{1,5},{2,6},{3,7},{4,0},{5,1},{6,2},{7,3},{8,12},{9,13},{10,... | collective-permute-start | bytes 61448 | tf_op jit(solution)/shard_map/ppermute | solution.py:398
  2.9 19.8 %collective-permute-start.1 = (f32[40,128]{1,0:T(8,128)S(1)}, f32[40,128]{1,0:T(8,128)S(1)}, u32[]{:S(2)}, u32[]{:S(2)}) collective-permute-start(f32[40,128]{1,0:T(8,128)S(1)} %get-tuple-element.21), channel_id=1, source_target_pairs={{0,124},{1,125},{2,126},{3,127},{4,8},{5,9},{6,10},{7,11},{8,4},{9... | collective-permute-start | bytes 61448 | tf_op jit(solution)/shard_map/ppermute | solution.py:398
  21.3 7.4 %copy-start.5 = (f32[1,1,1,3,16,128]{5,4,3,2,1,0:T(8,128)S(1)}, f32[1,1,1,3,16,128]{5,4,3,2,1,0:T(8,128)}, u32[]{:S(2)}) copy-start(f32[1,1,1,3,16,128]{5,4,3,2,1,0:T(8,128)} %param.14) | copy-start | bytes 73732
  22.7 6.0 %copy-start.6 = (s32[1,1,1,16,128]{4,3,2,1,0:T(8,128)S(1)}, s32[1,1,1,16,128]{4,3,2,1,0:T(8,128)}, u32[]{:S(2)}) copy-start(s32[1,1,1,16,128]{4,3,2,1,0:T(8,128)} %param.11) | copy-start | bytes 24580
  22.8 17.3 %collective-permute-start.2 = (f32[240,128]{1,0:T(8,128)S(1)}, f32[240,128]{1,0:T(8,128)S(1)}, u32[]{:S(2)}, u32[]{:S(2)}) collective-permute-start(f32[240,128]{1,0:T(8,128)S(1)} %pack_a.1.after), channel_id=1, source_target_pairs={{0,64},{1,65},{2,66},{3,67},{4,68},{5,69},{6,70},{7,71},{8,72},{9,... | collective-permute-start | bytes 368648 | tf_op jit(solution)/shard_map/ppermute | solution.py:398
  28.7 18.9 %copy-start.1 = (f32[5,8,16,128]{3,2,1,0:T(8,128)S(1)}, f32[5,8,16,128]{3,2,1,0:T(8,128)}, u32[]{:S(2)}) copy-start(f32[5,8,16,128]{3,2,1,0:T(8,128)} %param.9) | copy-start | bytes 983044
  40.0 3.5 %copy-start.7 = (f32[1,1,1,16,128]{4,3,2,1,0:T(8,128)S(1)}, f32[1,1,1,16,128]{4,3,2,1,0:T(8,128)}, u32[]{:S(2)}) copy-start(f32[1,1,1,16,128]{4,3,2,1,0:T(8,128)} %param.16) | copy-start | bytes 24580
  40.1 7.6 %collective-permute-start.3 = (f32[120,128]{1,0:T(8,128)S(1)}, f32[120,128]{1,0:T(8,128)S(1)}, u32[]{:S(2)}, u32[]{:S(2)}) collective-permute-start(f32[120,128]{1,0:T(8,128)S(1)} %pack_b.1), channel_id=1, source_target_pairs={{0,128},{1,129},{2,130},{3,131},{4,132},{5,133},{6,134},{7,135},{8... | collective-permute-start | bytes 184328 | tf_op jit(solution)/shard_map/ppermute | solution.py:398
  47.6 14.2 %copy-start.2 = (f32[1,1,1,3,16,128]{5,4,3,2,1,0:T(8,128)S(1)}, f32[1,1,1,3,16,128]{5,4,3,2,1,0:T(8,128)}, u32[]{:S(2)}) copy-start(f32[1,1,1,3,16,128]{5,4,3,2,1,0:T(8,128)} %param.15) | copy-start | bytes 73732
  47.8 9.3 %collective-permute-start.4 = (f32[8,128]{1,0:T(8,128)S(1)}, f32[8,128]{1,0:T(8,128)S(1)}, u32[]{:S(2)}, u32[]{:S(2)}) collective-permute-start(f32[8,128]{1,0:T(8,128)S(1)} %get-tuple-element.24), channel_id=1, source_target_pairs={{0,1},{1,2},{2,3},{3,0},{4,5},{5,6},{6,7},{7,4},{8,9},{9,10},{10,1... | collective-permute-start | bytes 12296 | tf_op jit(solution)/shard_map/ppermute | solution.py:398
  55.1 1.9 %copy-start.8 = (s32[1,1,1,16]{3,2,1,0:T(1,128)S(1)}, s32[1,1,1,16]{3,2,1,0:T(1,128)}, u32[]{:S(2)}) copy-start(s32[1,1,1,16]{3,2,1,0:T(1,128)} %param.13) | copy-start | bytes 196
  55.1 6.7 %collective-permute-start.5 = (f32[8,128]{1,0:T(8,128)S(1)}, f32[8,128]{1,0:T(8,128)S(1)}, u32[]{:S(2)}, u32[]{:S(2)}) collective-permute-start(f32[8,128]{1,0:T(8,128)S(1)} %get-tuple-element.25), channel_id=1, source_target_pairs={{0,3},{1,0},{2,1},{3,2},{4,7},{5,4},{6,5},{7,6},{8,11},{9,8},{10,9... | collective-permute-start | bytes 12296 | tf_op jit(solution)/shard_map/ppermute | solution.py:398
  57.1 4.8 %copy-start.3 = (f32[1,1,1,16,128]{4,3,2,1,0:T(8,128)S(1)}, f32[1,1,1,16,128]{4,3,2,1,0:T(8,128)}, u32[]{:S(2)}) copy-start(f32[1,1,1,16,128]{4,3,2,1,0:T(8,128)} %param.17) | copy-start | bytes 24580
  64.0 5.9 %collective-permute-start.6 = (f32[8,128]{1,0:T(8,128)S(1)}, f32[8,128]{1,0:T(8,128)S(1)}, u32[]{:S(2)}, u32[]{:S(2)}) collective-permute-start(f32[8,128]{1,0:T(8,128)S(1)} %get-tuple-element.29), channel_id=1, source_target_pairs={{0,1},{1,2},{2,3},{3,0},{4,5},{5,6},{6,7},{7,4},{8,9},{9,10},{10,1... | collective-permute-start | bytes 12296 | tf_op jit(solution)/shard_map/ppermute | solution.py:398
  65.9 6.7 %collective-permute-start.7 = (f32[8,128]{1,0:T(8,128)S(1)}, f32[8,128]{1,0:T(8,128)S(1)}, u32[]{:S(2)}, u32[]{:S(2)}) collective-permute-start(f32[8,128]{1,0:T(8,128)S(1)} %get-tuple-element.30), channel_id=1, source_target_pairs={{0,3},{1,0},{2,1},{3,2},{4,7},{5,4},{6,5},{7,6},{8,11},{9,8},{10,9... | collective-permute-start | bytes 12296 | tf_op jit(solution)/shard_map/ppermute | solution.py:398
  72.6 14.2 %copy-start.4 = (f32[5,8,16,128]{3,2,1,0:T(8,128)S(1)}, f32[5,8,16,128]{3,2,1,0:T(8,128)}, u32[]{:S(2)}) copy-start(f32[5,8,16,128]{3,2,1,0:T(8,128)} %param.10) | copy-start | bytes 983044
  72.9 3.9 %collective-permute-start.8 = (f32[80,128]{1,0:T(8,128)S(1)}, f32[80,128]{1,0:T(8,128)S(1)}, u32[]{:S(2)}, u32[]{:S(2)}) collective-permute-start(f32[80,128]{1,0:T(8,128)S(1)} %get-tuple-element.32), channel_id=1, source_target_pairs={{0,4},{1,5},{2,6},{3,7},{4,0},{5,1},{6,2},{7,3},{8,12},{9,13},{10,... | collective-permute-start | bytes 122888 | tf_op jit(solution)/shard_map/ppermute | solution.py:398
  74.8 6.5 %collective-permute-start.9 = (f32[80,128]{1,0:T(8,128)S(1)}, f32[80,128]{1,0:T(8,128)S(1)}, u32[]{:S(2)}, u32[]{:S(2)}) collective-permute-start(f32[80,128]{1,0:T(8,128)S(1)} %get-tuple-element.33), channel_id=1, source_target_pairs={{0,124},{1,125},{2,126},{3,127},{4,8},{5,9},{6,10},{7,11},{8,4},{9... | collective-permute-start | bytes 122888 | tf_op jit(solution)/shard_map/ppermute | solution.py:398
  81.3 21.1 %collective-permute-start.10 = (f32[200,128]{1,0:T(8,128)S(1)}, f32[200,128]{1,0:T(8,128)S(1)}, u32[]{:S(2)}, u32[]{:S(2)}) collective-permute-start(f32[200,128]{1,0:T(8,128)S(1)} %fold_y.1.after), channel_id=1, source_target_pairs={{0,64},{1,65},{2,66},{3,67},{4,68},{5,69},{6,70},{7,71},{8,72},{9,... | collective-permute-start | bytes 307208 | tf_op jit(solution)/shard_map/ppermute | solution.py:398
  102.5 7.1 %collective-permute-start.11 = (f32[80,128]{1,0:T(8,128)S(1)}, f32[80,128]{1,0:T(8,128)S(1)}, u32[]{:S(2)}, u32[]{:S(2)}) collective-permute-start(f32[80,128]{1,0:T(8,128)S(1)} %relay_b.1), channel_id=1, source_target_pairs={{0,128},{1,129},{2,130},{3,131},{4,132},{5,133},{6,134},{7,135},{8... | collective-permute-start | bytes 122888 | tf_op jit(solution)/shard_map/ppermute | solution.py:398

commit v2 on v1

--- a/solution.py
+++ b/solution.py
@@ -5,6 +5,7 @@
 from jax.experimental.pallas import tpu as pltpu
 from jax.sharding import PartitionSpec as P
 
+
 PARCEL = 8.0
 LATENT = 0.5
 TIME_INCREMENT = 0.2
@@ -28,8 +29,10 @@
         for i in range(nx):
             for j in range(ny):
                 for k in range(nz):
-                    a, b, c = target(i, j, k)
-                    out.append(((i * ny + j) * nz + k, (a * ny + b) * nz + c))
+                    there = target(i, j, k)
+                    if there is not None:
+                        a, b, c = there
+                        out.append(((i * ny + j) * nz + k, (a * ny + b) * nz + c))
         return out
 
     def d_side(i, j, k):
@@ -39,13 +42,17 @@
             return (i ^ 1, 0, k)
         return (i, ((j - 1) ^ 1) + 1, k)
 
+    def turn(i, j, k):
+        if j in (0, ny - 1):
+            return ((i + 2) % nx if i % 2 == 0 else (i - 2) % nx, j, k)
+        return None
+
     return {
-        "A": pairs(lambda i, j, k: (i ^ 1, j, k)),
-        "B": pairs(lambda i, j, k: ((i + 2) % nx if i % 2 == 0 else (i - 2) % nx, j, k)),
+        "near": pairs(lambda i, j, k: (i ^ 1, j, k)),
+        "far": pairs(lambda i, j, k: ((i - 1) % nx if i % 2 == 0 else (i + 1) % nx, j, k)),
+        "turn": pairs(turn),
         "C": pairs(lambda i, j, k: (i, j ^ 1, k)),
         "D": pairs(d_side),
-        "up": pairs(lambda i, j, k: (i, j, (k + 1) % nz)),
-        "down": pairs(lambda i, j, k: (i, j, (k - 1) % nz)),
     }
 
 
@@ -60,6 +67,22 @@
     return pl.ds(pl.multiple_of(start, unit), size)
 
 
+def post_ends(ref, low, high):
+    k, n = lax.axis_index("gz"), ref.shape[0] // 8
+    ref[...] = jnp.zeros(ref.shape, F32)
+    up, down = lax.rem(k + 1, n) * 8, lax.rem(k + n - 1, n) * 8
+    for row in range(8):
+        ref[pl.ds(up + row, 1), :] = high(row)
+        ref[pl.ds(down + row, 1), :] = low(row)
+
+
+def get_ends(ref):
+    k, n = lax.axis_index("gz"), ref.shape[0] // 8
+    below = ref[rows(lax.rem(k + n - 1, n) * 8, 8, 8), :]
+    above = ref[rows(lax.rem(k + 1, n) * 8, 8, 8), :]
+    return below, above
+
+
 def choose(cond, yes, no):
     pl.when(cond)(yes)
     pl.when(jnp.logical_not(cond))(no)
@@ -83,68 +106,57 @@
     choose(odd_j == 0, even, odd)
 
 
-def pack_a(gas, from_c, from_d, to_a):
+def pack_x(gas, from_c, from_d, to_near, to_far, to_turn):
     odd_i, _, _ = places()
-    near = (1 - odd_i) * 112
+    near = (1 - odd_i) * 7
+    to_near[120:128, :] = jnp.zeros((8, 128), F32)
+    to_far[80:96, :] = jnp.zeros((16, 128), F32)
+    to_turn[...] = jnp.zeros((8, 128), F32)
     for c in range(5):
-        at = c * 48
-        to_a[at : at + 16, :] = gas[rows(c * OWN + near, 16, 16), :]
-        to_a[at + 16 : at + 32, :] = gas[rows(c * OWN + 112 - near, 16, 16), :]
-        to_a[at + 32 : at + 40, :] = from_c[c * 8 : c * 8 + 8, :]
-        to_a[at + 40 : at + 48, :] = from_d[c * 8 : c * 8 + 8, :]
-
-
-def pack_b(from_a, from_d, after, to_b):
+        to_near[c * 24 : c * 24 + 16, :] = gas[rows(c * OWN + near * 16, 16, 16), :]
+        to_near[c * 24 + 16 : c * 24 + 24, :] = from_d[c * 8 : c * 8 + 8, :]
+        to_near[120 + c : 121 + c, :] = from_c[pl.ds(c * 8 + near, 1), :]
+        to_far[c * 16 : c * 16 + 16, :] = gas[rows(c * OWN + 112 - near * 16, 16, 16), :]
+        to_far[80 + c : 81 + c, :] = from_c[pl.ds(c * 8 + 7 - near, 1), :]
+        to_far[88 + c : 89 + c, :] = from_d[pl.ds(c * 8 + 7 - near, 1), :]
+        to_turn[c : c + 1, :] = from_d[pl.ds(c * 8 + near, 1), :]
+
+
+def join_halo(gas, from_c, from_d, from_near, from_far, from_turn, after, halo, ends):
     del after
-    odd_i, _, wrap = places()
-    far = (1 - odd_i) * 7
-    for c in range(5):
-        to_b[c * 24 : c * 24 + 16, :] = from_a[c * 48 + 16 : c * 48 + 32, :]
-        to_b[c * 24 + 16 : c * 24 + 24, :] = jnp.zeros((8, 128), F32)
-        to_b[c * 24 + 16 : c * 24 + 17, :] = from_a[pl.ds(c * 48 + 32 + far, 1), :]
-
-    def wrapped():
-        for c in range(5):
-            to_b[c * 24 + 17 : c * 24 + 18, :] = from_d[pl.ds(c * 8 + far, 1), :]
-
-    def inner():
-        for c in range(5):
-            to_b[c * 24 + 17 : c * 24 + 18, :] = from_a[pl.ds(c * 48 + 40 + far, 1), :]
-
-    choose(wrap, wrapped, inner)
-
-
-def join_halo(gas, from_c, from_d, from_a, from_b, halo, z_low, z_high):
     odd_i, _, wrap = places()
     near = odd_i * 7
     for c in range(5):
         at = c * HALO
-        halo[at : at + 16, :] = from_a[c * 48 : c * 48 + 16, :]
-        halo[at + 16 : at + 32, :] = from_b[c * 24 : c * 24 + 16, :]
+        halo[at : at + 16, :] = from_near[c * 24 : c * 24 + 16, :]
+        halo[at + 16 : at + 32, :] = from_far[c * 16 : c * 16 + 16, :]
         halo[at + 32 : at + 40, :] = from_c[c * 8 : c * 8 + 8, :]
         halo[at + 40 : at + 48, :] = jnp.zeros((8, 128), F32)
-        halo[at + 40 : at + 41, :] = from_a[pl.ds(c * 48 + 32 + near, 1), :]
-        halo[at + 41 : at + 42, :] = from_b[c * 24 + 16 : c * 24 + 17, :]
+        halo[at + 40 : at + 41, :] = from_near[120 + c : 121 + c, :]
+        halo[at + 41 : at + 42, :] = from_far[80 + c : 81 + c, :]
         halo[at + 56 : at + 64, :] = jnp.zeros((8, 128), F32)
-        halo[at + 57 : at + 58, :] = from_b[c * 24 + 17 : c * 24 + 18, :]
     halo[5 * HALO : 384, :] = jnp.zeros((384 - 5 * HALO, 128), F32)
 
     def wrapped():
         for c in range(5):
-            halo[c * HALO + 48 : c * HALO + 56, :] = from_a[c * 48 + 40 : c * 48 + 48, :]
-            halo[c * HALO + 56 : c * HALO + 57, :] = from_d[pl.ds(c * 8 + near, 1), :]
+            at = c * HALO + 48
+            halo[at : at + 8, :] = from_near[c * 24 + 16 : c * 24 + 24, :]
+            halo[at + 8 : at + 9, :] = from_d[pl.ds(c * 8 + near, 1), :]
+            halo[at + 9 : at + 10, :] = from_turn[c : c + 1, :]
 
     def inner():
         for c in range(5):
-            halo[c * HALO + 48 : c * HALO + 56, :] = from_d[c * 8 : c * 8 + 8, :]
-            halo[c * HALO + 56 : c * HALO + 57, :] = from_a[pl.ds(c * 48 + 40 + near, 1), :]
+            at = c * HALO + 48
+            halo[at : at + 8, :] = from_d[c * 8 : c * 8 + 8, :]
+            halo[at + 8 : at + 9, :] = from_near[pl.ds(c * 24 + 16 + near, 1), :]
+            halo[at + 9 : at + 10, :] = from_far[88 + c : 89 + c, :]
 
     choose(wrap, wrapped, inner)
+    turned = []
     for n in range(8):
         part = gas[n * 128 : n * 128 + 128, :] if n < 5 else halo[(n - 5) * 128 : (n - 4) * 128, :]
-        turned = part.T
-        z_low[n : n + 1, :] = turned[0:1, :]
-        z_high[n : n + 1, :] = turned[127:128, :]
+        turned.append(part.T)
+    post_ends(ends, lambda n: turned[n][0:1, :], lambda n: turned[n][127:128, :])
 
 
 def three(place, anchor, offset):
@@ -190,20 +202,21 @@
 
 
 def deposit(
-    halo, z_below, z_above, planar, vertical, part, diameter, alive, vel, temp, sums, ghost_low, ghost_high,
+    halo, z_ends, planar, vertical, part, diameter, alive, vel, temp, sums, ghosts,
     gas_at, source, weighted, total,
 ):
     blocks = diameter.shape[0]
 
-    def z_rows(ref):
-        v = ref[...]
+    below, above = get_ends(z_ends)
+
+    def z_rows(v):
         turned = pltpu.roll(v, 64, 1)
         side = jnp.concatenate(
             [v[5:6], turned[5:6], v[6:7], turned[6:7], v[7:8], jnp.zeros((3, 128), F32)], axis=0
         )
         return jnp.concatenate([v, side], axis=1)
 
-    ends = jnp.concatenate([z_rows(z_below), z_rows(z_above)], axis=0).astype(BF16)
+    ends = jnp.concatenate([z_rows(below), z_rows(above)], axis=0).astype(BF16)
     at_ends = jnp.dot(ends, planar[...], preferred_element_type=F32)
     around = halo[0 : 5 * HALO, :].astype(BF16)
     for b in range(blocks):
@@ -243,10 +256,8 @@
         weighted[...], vertical[...], (((1,), (1,)), ((), ())), preferred_element_type=F32
     )
     sums[...] = total[0:960, 0:128]
-    for n in range(8):
-        turned = total[n * 128 : n * 128 + 128, 128:256].T
-        ghost_low[n : n + 1, :] = turned[0:1, :]
-        ghost_high[n : n + 1, :] = turned[1:2, :]
+    turned = [total[n * 128 : n * 128 + 128, 128:256].T for n in range(8)]
+    post_ends(ghosts, lambda n: turned[n][0:1, :], lambda n: turned[n][1:2, :])
 
 
 def upright(below, above):
@@ -254,7 +265,8 @@
     return jnp.where(z == 0, below, jnp.where(z == 127, above, 0.0)).T
 
 
-def fold_z(sums, below, above, own, sides, to_c, to_d):
+def fold_z(sums, z_ends, own, sides, to_c, to_d):
+    below, above = get_ends(z_ends)
     for n in range(8):
         extra = upright(below[n : n + 1, :], above[n : n + 1, :])
         if n < 5:
@@ -271,36 +283,32 @@
             to_d[c * 16 : c * 16 + 16, :] = here[48:64, :]
 
 
-def fold_y(sides, from_c, from_d, to_a):
+def fold_y(sides, from_c, from_d, to_near, to_far, to_turn):
     _, odd_j, wrap = places()
     keep = jnp.where(wrap, 0.0, 1.0).astype(F32)
     y = lax.broadcasted_iota(I32, (16, 128), 0)
     c_y = 15 - 15 * odd_j
     at_c, at_d = y == c_y, y == 15 - c_y
+    to_turn[...] = jnp.zeros((8, 128), F32)
     for c in range(5):
         for side in range(2):
             row = c * 16 + 8 + side
-            to_a[c * 40 + side * 16 : c * 40 + side * 16 + 16, :] = (
+            folded = (
                 sides[c * 32 + side * 16 : c * 32 + side * 16 + 16, :]
                 + jnp.where(at_c, from_c[row : row + 1, :], 0.0)
                 + jnp.where(at_d, from_d[row : row + 1, :] * keep, 0.0)
             )
-        to_a[c * 40 + 32 : c * 40 + 40, :] = from_d[c * 16 : c * 16 + 8, :]
-
-
-def relay_b(from_a, from_d, after, to_b):
+            if side == 0:
+                to_near[c * 24 : c * 24 + 16, :] = folded
+            else:
+                to_far[c * 16 : c * 16 + 16, :] = folded
+        to_near[c * 24 + 16 : c * 24 + 24, :] = from_d[c * 16 : c * 16 + 8, :]
+        to_turn[c : c + 1, :] = from_d[c * 16 + 9 : c * 16 + 10, :]
+
+
+def stencil(gas, start, halo, z_ends, own, from_c, from_d, after, out, upper):
     del after
-    _, odd_j, wrap = places()
-    gate = jnp.where(wrap, 1.0, 0.0).astype(F32)
-    at_d = lax.broadcasted_iota(I32, (16, 128), 0) == 15 * odd_j
-    for c in range(5):
-        to_b[c * 16 : c * 16 + 16, :] = from_a[c * 40 + 16 : c * 40 + 32, :] + jnp.where(
-            at_d, from_d[c * 16 + 9 : c * 16 + 10, :] * gate, 0.0
-        )
-
-
-def stencil(gas, start, halo, z_below, z_above, own, from_c, from_d, after, out, upper):
-    del after
+    below, above = get_ends(z_ends)
     odd_i, odd_j, wrap = places()
     keep = jnp.where(wrap, 0.0, 1.0).astype(F32)
     y = lax.broadcasted_iota(I32, (16, 128), 0)
@@ -311,7 +319,7 @@
     high_x, low_x = 16 * odd_i, 16 - 16 * odd_i
     high_y, low_y = 32 + 16 * odd_j, 48 - 16 * odd_j
     for c in range(5):
-        upper[...] = upright(z_below[c : c + 1, :], z_above[c : c + 1, :])
+        upper[...] = upright(below[c : c + 1, :], above[c : c + 1, :])
         for x in range(8):
             at = c * OWN + x * 16
             g = gas[at : at + 16, :]
@@ -349,22 +357,25 @@
             )
 
 
-def finish(base, from_a, from_b, out):
+def finish(base, from_near, from_far, from_turn, out):
     odd_i, odd_j, wrap = places()
     near = (1 - odd_i) * 112
     scale = 0.25 * TIME_INCREMENT
+    gate = jnp.where(wrap, scale, 0.0).astype(F32)
+    at_d = lax.broadcasted_iota(I32, (16, 128), 0) == 15 * odd_j
     out[...] = base[...]
     for c in range(5):
         at = rows(c * OWN + near, 16, 16)
-        out[at, :] = out[at, :] + scale * from_a[c * 40 : c * 40 + 16, :]
+        out[at, :] = out[at, :] + scale * from_near[c * 24 : c * 24 + 16, :]
         at = rows(c * OWN + 112 - near, 16, 16)
-        out[at, :] = out[at, :] + scale * from_b[c * 16 : c * 16 + 16, :]
+        turned = jnp.where(at_d, from_turn[c : c + 1, :] * gate, 0.0)
+        out[at, :] = out[at, :] + scale * from_far[c * 16 : c * 16 + 16, :] + turned
 
     def across(y):
         def add():
             for c in range(5):
                 at = pl.ds(c * OWN + y, 8, stride=16)
-                out[at, :] = out[at, :] + scale * from_a[c * 40 + 32 : c * 40 + 40, :]
+                out[at, :] = out[at, :] + scale * from_near[c * 24 + 16 : c * 24 + 24, :]
 
         return add
 
@@ -372,14 +383,13 @@
     pl.when(wrap & (odd_j == 1))(across(15))
 
 
-def call(body, name, out_shapes, *operands, loose=(), scratch=(), flops=10000):
+def call(body, out_shapes, *operands, loose=(), scratch=(), flops=10000):
     whole = pl.BlockSpec(memory_space=pltpu.VMEM)
     anywhere = pl.BlockSpec(memory_space=pl.ANY)
     single = not isinstance(out_shapes, list)
     outs = [out_shapes] if single else out_shapes
     result = pl.pallas_call(
         body,
-        name=name,
         out_shape=[jax.ShapeDtypeStruct(s, t) for s, t in outs],
         in_specs=[anywhere if n in loose else whole for n in range(len(operands))],
         out_specs=[whole] * len(outs),
@@ -397,7 +407,12 @@
     def send(values, route):
         return lax.ppermute(values, AXES, routes[route])
 
+    def swap_ends(values):
+        chunks = values.reshape(shape[2], 8, 128)
+        return lax.all_to_all(chunks, "gz", 0, 0).reshape(values.shape)
+
     blocks = drop_cell.shape[3]
+    ends_shape = ((8 * shape[2], 128), F32)
     gas = gas_state.reshape(640, 128)
     start = section_start.reshape(640, 128)
     cell = drop_cell.reshape(blocks, 128)
@@ -409,26 +424,28 @@
     alive = jnp.where(slots < droplets_per_block.reshape(blocks, 1), PARCEL, 0.0).astype(F32)
     shift = jnp.broadcast_to(8 * block_tile.reshape(blocks, 1), (blocks, 128)).astype(I32)
 
-    to_c, to_d = call(pack_y, "pack_y", [((40, 128), F32)] * 2, gas)
-    gas_c, gas_d = send(to_c, "C"), send(to_d, "D")
-    to_a = call(pack_a, "pack_a", ((240, 128), F32), gas, gas_c, gas_d)
-    gas_a = send(to_a, "A")
+    to_c, to_d = call(pack_y, [((40, 128), F32)] * 2, gas)
+    gas_d, gas_c = send(to_d, "D"), send(to_c, "C")
+    to_near, to_far, to_turn = call(
+        pack_x, [((128, 128), F32), ((96, 128), F32), ((8, 128), F32)], gas, gas_c, gas_d
+    )
+    gas_near, gas_far = send(to_near, "near"), send(to_far, "far")
+    gas_turn = send(to_turn, "turn")
     planar, vertical, part = call(
         weigh,
-        "weigh",
         [((256, blocks * 128), BF16), ((256, blocks * 128), BF16), ((5 * blocks, 128), F32)],
-        gas, cell, shift, frac, to_a,
+        gas, cell, shift, frac, to_near,
         loose=(4,), flops=1 << 32,
     )
-    gas_b = send(call(pack_b, "pack_b", ((120, 128), F32), gas_a, gas_d, part, loose=(2,)), "B")
-    halo, low, high = call(
-        join_halo, "join_halo", [((384, 128), F32), ((8, 128), F32), ((8, 128), F32)],
-        gas, gas_c, gas_d, gas_a, gas_b,
-    )
-    above, below = send(low, "down"), send(high, "up")
-    sums, low, high = call(
-        deposit, "deposit", [((960, 128), F32), ((8, 128), F32), ((8, 128), F32)],
-        halo, below, above, planar, vertical, part, diameter, alive, vel, temp,
+    halo, ends = call(
+        join_halo, [((384, 128), F32), ends_shape],
+        gas, gas_c, gas_d, gas_near, gas_far, gas_turn, part,
+        loose=(6,),
+    )
+    ends = swap_ends(ends)
+    sums, ghosts = call(
+        deposit, [((960, 128), F32), ends_shape],
+        halo, ends, planar, vertical, part, diameter, alive, vel, temp,
         scratch=[
             pltpu.VMEM((5 * blocks, 128), F32),
             pltpu.VMEM((5 * blocks, 128), F32),
@@ -436,21 +453,22 @@
             pltpu.VMEM((1024, 256), F32),
         ],
     )
-    dep_above, dep_below = send(low, "down"), send(high, "up")
     own, sides, to_c, to_d = call(
-        fold_z, "fold_z", [((640, 128), F32), ((160, 128), F32), ((80, 128), F32), ((80, 128), F32)],
-        sums, dep_below, dep_above,
-    )
-    dep_c, dep_d = send(to_c, "C"), send(to_d, "D")
-    to_a = call(fold_y, "fold_y", ((200, 128), F32), sides, dep_c, dep_d)
-    dep_a = send(to_a, "A")
+        fold_z, [((640, 128), F32), ((160, 128), F32), ((80, 128), F32), ((80, 128), F32)],
+        sums, swap_ends(ghosts),
+    )
+    dep_d, dep_c = send(to_d, "D"), send(to_c, "C")
+    to_near, to_far, to_turn = call(
+        fold_y, [((120, 128), F32), ((80, 128), F32), ((8, 128), F32)], sides, dep_c, dep_d
+    )
+    dep_near, dep_far = send(to_near, "near"), send(to_far, "far")
+    dep_turn = send(to_turn, "turn")
     base = call(
-        stencil, "stencil", ((640, 128), F32),
-        gas, start, halo, below, above, own, dep_c, dep_d, to_a,
-        loose=(8,), scratch=[pltpu.VMEM((128, 128), F32)], flops=1 << 32,
-    )
-    dep_b = send(call(relay_b, "relay_b", ((80, 128), F32), dep_a, dep_d, base, loose=(2,)), "B")
-    out = call(finish, "finish", ((640, 128), F32), base, dep_a, dep_b)
+        stencil, ((640, 128), F32),
+        gas, start, halo, ends, own, dep_c, dep_d, to_near,
+        loose=(7,), scratch=[pltpu.VMEM((128, 128), F32)], flops=1 << 32,
+    )
+    out = call(finish, ((640, 128), F32), base, dep_near, dep_far, dep_turn)
     return out.reshape(gas_state.shape)
 
 
@@ -466,4 +484,6 @@
         P("gx", "gy", "gz", None, None),
         P("gx", "gy", "gz", None, None),
     )
-    return jax.shard_map(local, mesh=mesh, in_specs=in_specs, out_specs=P(None, "gx", "gy", "gz"), check_vma=False)
+    return jax.shard_map(
+        local, mesh=mesh, in_specs=in_specs, out_specs=P(None, "gx", "gy", "gz"), check_vma=False
+    )

time: 111 us -> 107 us (0.964)
  the two profiles are of different devices: /device:TPU:6 before, /device:TPU:8 now
where the time goes in v2:
time: 107 us
  starting transfers between devices  66.2 us (62%)
  waiting for transfers between devices  24.2 us (23%)
  blocking collectives  7.71 us (7%)
  Pallas kernels  6.71 us (6%)
  local copies, waits for them, and re-layouts  1.75 us (2%)
    ppermute x10, starting transfers between devices, send(): return lax.ppermute(values, AXES, routes[route])  61.8 us
    ppermute x10, waiting for transfers between devices, send(): return lax.ppermute(values, AXES, routes[route])  19.5 us
    all_to_all x1, blocking collectives, swap_ends(): return lax.all_to_all(chunks, 'gz', 0, 0).reshape(values.shape)  7.71 us
    pallas_call x9, Pallas kernels, call(): pl.pallas_call(body, out_shape=[jax.ShapeDtypeStruct(s, t) for s, t in ou...  6.71 us
    all_to_all x1, waiting for transfers between devices, swap_ends(): return lax.all_to_all(chunks, 'gz', 0, 0).reshape(values.shape)  4.63 us
    all_to_all x1, starting transfers between devices, swap_ends(): return lax.all_to_all(chunks, 'gz', 0, 0).reshape(values.shape)  4.42 us
  transfers between devices with their start and end apart: 11, of which 5 were waited for; matrix products, arithmetic and copies ran while one was open for 0% of the time, Pallas kernels for 3%

profile of v2, /device:TPU:8, one launch (start us, length us, event | category | flops | bytes accessed | tf_op | source)
XLA Modules:
  0.0 106.8 jit_solution(4609252423884083715)
XLA Ops:
  0.0 0.0 copy-start
  0.0 1.0 copy-done
  1.0 0.0 copy-start.7
  1.0 1.9 %collective-permute-start = (f32[40,128]{1,0:T(8,128)S(1)}, f32[40,128]{1,0:T(8,128)S(1)}, u32[]{:S(2)}, u32[]{:S(2)}) collective-permute-start(f32[40,128]{1,0:T(8,128)S(1)} %get-tuple-element.24), channel_id=1, source_target_pairs={{0,4},{1,5},{2,6},{3,7},{4,0},{5,1},{6,2},{7,3},{8,12},{9,13},{10,... | collective-permute-start | bytes 61448 | tf_op jit(solution)/shard_map/ppermute | solution.py:408
  2.9 0.0 copy-start.9
  2.9 18.3 %collective-permute-start.1 = (f32[40,128]{1,0:T(8,128)S(1)}, f32[40,128]{1,0:T(8,128)S(1)}, u32[]{:S(2)}, u32[]{:S(2)}) collective-permute-start(f32[40,128]{1,0:T(8,128)S(1)} %get-tuple-element.25), channel_id=1, source_target_pairs={{0,124},{1,125},{2,126},{3,127},{4,8},{5,9},{6,10},{7,11},{8,4},{9... | collective-permute-start | bytes 61448 | tf_op jit(solution)/shard_map/ppermute | solution.py:408
  21.3 0.0 copy-done.7
  21.3 0.0 copy-done.9
  21.3 0.0 copy-start.5
  21.3 0.0 collective-permute-done.from_c
  21.4 1.4 %collective-permute-done.1.from_d = f32[40,128]{1,0:T(8,128)S(1)} collective-permute-done((f32[40,128]{1,0:T(8,128)S(1)}, f32[40,128]{1,0:T(8,128)S(1)}, u32[]{:S(2)}, u32[]{:S(2)}) %collective-permute-start.1) | collective-permute-done | bytes 20512 | tf_op jit(solution)/shard_map/ppermute | solution.py:408
  22.8 0.0 copy-start.6
  22.8 3.5 %collective-permute-start.4 = (f32[8,128]{1,0:T(8,128)S(1)}, f32[8,128]{1,0:T(8,128)S(1)}, u32[]{:S(2)}, u32[]{:S(2)}) collective-permute-start(f32[8,128]{1,0:T(8,128)S(1)} %get-tuple-element.28), channel_id=1, source_target_pairs={{0,128},{1,129},{2,130},{3,131},{60,188},{61,189},{62,190},{63,191... | collective-permute-start | bytes 12296 | tf_op jit(solution)/shard_map/ppermute | solution.py:408
  26.3 7.7 %collective-permute-start.3 = (f32[96,128]{1,0:T(8,128)S(1)}, f32[96,128]{1,0:T(8,128)S(1)}, u32[]{:S(2)}, u32[]{:S(2)}) collective-permute-start(f32[96,128]{1,0:T(8,128)S(1)} %get-tuple-element.27), channel_id=1, source_target_pairs={{0,960},{1,961},{2,962},{3,963},{4,964},{5,965},{6,966},{7,967},{8... | collective-permute-start | bytes 147464 | tf_op jit(solution)/shard_map/ppermute | solution.py:408
  33.9 7.9 %collective-permute-start.2 = (f32[128,128]{1,0:T(8,128)S(1)}, f32[128,128]{1,0:T(8,128)S(1)}, u32[]{:S(2)}, u32[]{:S(2)}) collective-permute-start(f32[128,128]{1,0:T(8,128)S(1)} %get-tuple-element.26.after), channel_id=1, source_target_pairs={{0,64},{1,65},{2,66},{3,67},{4,68},{5,69},{6,70},{7,71},{8,72},{9,... | collective-permute-start | bytes 196616 | tf_op jit(solution)/shard_map/ppermute | solution.py:408
  41.8 0.1 broadcast_in_dim.13.shift
  41.9 0.0 copy-done.5
  41.9 0.0 copy-done.6
  41.9 2.1 %shard_map.93 = (bf16[256,2048]{1,0:T(8,128)(2,1)S(1)}, bf16[256,2048]{1,0:T(8,128)(2,1)S(1)}, f32[80,128]{1,0:T(8,128)S(1)}) custom-call(f32[640,128]{1,0:T(8,128)S(1)} %bitcast.18, s32[16,128]{1,0:T(8,128)S(1)} %bitcast.29, s32[16,128]{1,0:T(8,128)S(1)} %broadcast_in_dim.13.shift, f32[48,128]{1,0:T(8,128)S(1)} %bitcast.28, ...), custom_call_target="tpu_custom_call" | custom-call | flops 4294967296 | bytes 100000 | tf_op jit(solution)/shard_map/pallas_call | solution.py:391
  44.1 0.0 collective-permute-done.4.from_turn
  44.1 0.0 collective-permute-done.3.from_far
  44.1 4.7 %collective-permute-done.2.from_near = f32[128,128]{1,0:T(8,128)S(1)} collective-permute-done((f32[128,128]{1,0:T(8,128)S(1)}, f32[128,128]{1,0:T(8,128)S(1)}, u32[]{:S(2)}, u32[]{:S(2)}) %collective-permute-start.2) | collective-permute-done | bytes 65568 | tf_op jit(solution)/shard_map/ppermute | solution.py:408
  48.8 0.8 shard_map.94
  49.6 0.0 copy-start.2
  49.6 4.4 %all-to-all-start = ((f32[4,8,128]{2,1,0:T(8,128)}), f32[4,8,128]{2,1,0:T(8,128)S(1)}, u32[]{:S(2)}, u32[]{:S(2)}) async-start(f32[4,8,128]{2,1,0:T(8,128)} %bitcast.5), calls=%async_computation | async-start | bytes 32768 | tf_op jit(solution)/shard_map/all_to_all | solution.py:412
  54.1 0.0 copy-start.8
  54.1 0.7 copy-done.8
  54.7 0.1 fusion.alive
  54.8 4.6 %all-to-all-done = f32[4,8,128]{2,1,0:T(8,128)S(1)} async-done(((f32[4,8,128]{2,1,0:T(8,128)}), f32[4,8,128]{2,1,0:T(8,128)S(1)}, u32[]{:S(2)}, u32[]{:S(2)}) %all-to-all-start) | async-done | bytes 16416 | tf_op jit(solution)/shard_map/all_to_all | solution.py:412
  59.4 0.0 copy-done.2
  59.4 0.0 copy-done.3
  59.4 2.1 %shard_map.95 = (f32[960,128]{1,0:T(8,128)S(1)}, f32[32,128]{1,0:T(8,128)S(1)}) custom-call(f32[384,128]{1,0:T(8,128)S(1)} %get-tuple-element.30.halo, f32[32,128]{1,0:T(8,128)S(1)} %bitcast.21, bf16[256,2048]{1,0:T(8,128)(2,1)S(1)} %get-tuple-element.32.planar, bf16[256,2048]{1,0:T(8,128)(2,1)S(1)} %get-tuple-element.33.vertical, ...), custom_call_target="tpu_custom_call" | custom-call | flops 10000 | bytes 100000 | tf_op jit(solution)/shard_map/pallas_call | solution.py:391
  61.6 7.7 %all_to_all.10 = f32[4,8,128]{2,1,0:T(8,128)S(1)} all-to-all(f32[4,8,128]{2,1,0:T(8,128)S(1)} %bitcast.25), channel_id=1, replica_groups=mesh['gx'=16,'gy'=16,'gz'=4] {'gz'}, dimensions={0} | all-to-all | bytes 32768 | tf_op jit(solution)/shard_map/all_to_all | solution.py:412
  69.3 0.2 shard_map.96
  69.5 1.9 %collective-permute-start.5 = (f32[80,128]{1,0:T(8,128)S(1)}, f32[80,128]{1,0:T(8,128)S(1)}, u32[]{:S(2)}, u32[]{:S(2)}) collective-permute-start(f32[80,128]{1,0:T(8,128)S(1)} %get-tuple-element.37), channel_id=1, source_target_pairs={{0,4},{1,5},{2,6},{3,7},{4,0},{5,1},{6,2},{7,3},{8,12},{9,13},{10,... | collective-permute-start | bytes 122888 | tf_op jit(solution)/shard_map/ppermute | solution.py:408
  71.4 1.9 %collective-permute-start.6 = (f32[80,128]{1,0:T(8,128)S(1)}, f32[80,128]{1,0:T(8,128)S(1)}, u32[]{:S(2)}, u32[]{:S(2)}) collective-permute-start(f32[80,128]{1,0:T(8,128)S(1)} %get-tuple-element.38), channel_id=1, source_target_pairs={{0,124},{1,125},{2,126},{3,127},{4,8},{5,9},{6,10},{7,11},{8,4},{9... | collective-permute-start | bytes 122888 | tf_op jit(solution)/shard_map/ppermute | solution.py:408
  73.3 0.0 collective-permute-done.5.from_c
  73.4 4.6 %collective-permute-done.6.from_d = f32[80,128]{1,0:T(8,128)S(1)} collective-permute-done((f32[80,128]{1,0:T(8,128)S(1)}, f32[80,128]{1,0:T(8,128)S(1)}, u32[]{:S(2)}, u32[]{:S(2)}) %collective-permute-start.6) | collective-permute-done | bytes 40992 | tf_op jit(solution)/shard_map/ppermute | solution.py:408
  78.0 2.6 %collective-permute-start.9 = (f32[8,128]{1,0:T(8,128)S(1)}, f32[8,128]{1,0:T(8,128)S(1)}, u32[]{:S(2)}, u32[]{:S(2)}) collective-permute-start(f32[8,128]{1,0:T(8,128)S(1)} %get-tuple-element.42), channel_id=1, source_target_pairs={{0,128},{1,129},{2,130},{3,131},{60,188},{61,189},{62,190},{63,191... | collective-permute-start | bytes 12296 | tf_op jit(solution)/shard_map/ppermute | solution.py:408
  80.6 10.2 %collective-permute-start.8 = (f32[80,128]{1,0:T(8,128)S(1)}, f32[80,128]{1,0:T(8,128)S(1)}, u32[]{:S(2)}, u32[]{:S(2)}) collective-permute-start(f32[80,128]{1,0:T(8,128)S(1)} %get-tuple-element.41), channel_id=1, source_target_pairs={{0,960},{1,961},{2,962},{3,963},{4,964},{5,965},{6,966},{7,967},{8... | collective-permute-start | bytes 122888 | tf_op jit(solution)/shard_map/ppermute | solution.py:408
  90.8 5.9 %collective-permute-start.7 = (f32[120,128]{1,0:T(8,128)S(1)}, f32[120,128]{1,0:T(8,128)S(1)}, u32[]{:S(2)}, u32[]{:S(2)}) collective-permute-start(f32[120,128]{1,0:T(8,128)S(1)} %get-tuple-element.40.after), channel_id=1, source_target_pairs={{0,64},{1,65},{2,66},{3,67},{4,68},{5,69},{6,70},{7,71},{8,72},{9,... | collective-permute-start | bytes 184328 | tf_op jit(solution)/shard_map/ppermute | solution.py:408
  96.7 0.0 copy-done.1
  96.7 0.0 copy-done.4
  96.7 0.6 shard_map.98.base
  97.2 0.0 collective-permute-done.9.from_turn
  97.2 0.0 collective-permute-done.8.from_far
  97.2 8.8 %collective-permute-done.7.from_near = f32[120,128]{1,0:T(8,128)S(1)} collective-permute-done((f32[120,128]{1,0:T(8,128)S(1)}, f32[120,128]{1,0:T(8,128)S(1)}, u32[]{:S(2)}, u32[]{:S(2)}) %collective-permute-start.7) | collective-permute-done | bytes 61472 | tf_op jit(solution)/shard_map/ppermute | solution.py:408
  106.1 0.8 shard_map.99
  (8 shorter events, 0.1 us)
Async XLA Ops:
  0.0 1.0 copy-start
  1.0 20.3 %copy-start.7 = (f32[1,1,1,16,128]{4,3,2,1,0:T(8,128)S(1)}, f32[1,1,1,16,128]{4,3,2,1,0:T(8,128)}, u32[]{:S(2)}) copy-start(f32[1,1,1,16,128]{4,3,2,1,0:T(8,128)} %param.16) | copy-start | bytes 24580
  1.0 20.3 %collective-permute-start = (f32[40,128]{1,0:T(8,128)S(1)}, f32[40,128]{1,0:T(8,128)S(1)}, u32[]{:S(2)}, u32[]{:S(2)}) collective-permute-start(f32[40,128]{1,0:T(8,128)S(1)} %get-tuple-element.24), channel_id=1, source_target_pairs={{0,4},{1,5},{2,6},{3,7},{4,0},{5,1},{6,2},{7,3},{8,12},{9,13},{10,... | collective-permute-start | bytes 61448 | tf_op jit(solution)/shard_map/ppermute | solution.py:408
  2.9 18.4 %copy-start.9 = (s32[1,1,1,16]{3,2,1,0:T(1,128)S(1)}, s32[1,1,1,16]{3,2,1,0:T(1,128)}, u32[]{:S(2)}) copy-start(s32[1,1,1,16]{3,2,1,0:T(1,128)} %param.12) | copy-start | bytes 196
  2.9 19.8 %collective-permute-start.1 = (f32[40,128]{1,0:T(8,128)S(1)}, f32[40,128]{1,0:T(8,128)S(1)}, u32[]{:S(2)}, u32[]{:S(2)}) collective-permute-start(f32[40,128]{1,0:T(8,128)S(1)} %get-tuple-element.25), channel_id=1, source_target_pairs={{0,124},{1,125},{2,126},{3,127},{4,8},{5,9},{6,10},{7,11},{8,4},{9... | collective-permute-start | bytes 61448 | tf_op jit(solution)/shard_map/ppermute | solution.py:408
  21.3 20.6 %copy-start.5 = (f32[1,1,1,3,16,128]{5,4,3,2,1,0:T(8,128)S(1)}, f32[1,1,1,3,16,128]{5,4,3,2,1,0:T(8,128)}, u32[]{:S(2)}) copy-start(f32[1,1,1,3,16,128]{5,4,3,2,1,0:T(8,128)} %param.14) | copy-start | bytes 73732
  22.8 19.2 %copy-start.6 = (s32[1,1,1,16,128]{4,3,2,1,0:T(8,128)S(1)}, s32[1,1,1,16,128]{4,3,2,1,0:T(8,128)}, u32[]{:S(2)}) copy-start(s32[1,1,1,16,128]{4,3,2,1,0:T(8,128)} %param.11) | copy-start | bytes 24580
  22.8 21.3 %collective-permute-start.4 = (f32[8,128]{1,0:T(8,128)S(1)}, f32[8,128]{1,0:T(8,128)S(1)}, u32[]{:S(2)}, u32[]{:S(2)}) collective-permute-start(f32[8,128]{1,0:T(8,128)S(1)} %get-tuple-element.28), channel_id=1, source_target_pairs={{0,128},{1,129},{2,130},{3,131},{60,188},{61,189},{62,190},{63,191... | collective-permute-start | bytes 12296 | tf_op jit(solution)/shard_map/ppermute | solution.py:408
  26.3 17.8 %collective-permute-start.3 = (f32[96,128]{1,0:T(8,128)S(1)}, f32[96,128]{1,0:T(8,128)S(1)}, u32[]{:S(2)}, u32[]{:S(2)}) collective-permute-start(f32[96,128]{1,0:T(8,128)S(1)} %get-tuple-element.27), channel_id=1, source_target_pairs={{0,960},{1,961},{2,962},{3,963},{4,964},{5,965},{6,966},{7,967},{8... | collective-permute-start | bytes 147464 | tf_op jit(solution)/shard_map/ppermute | solution.py:408
  33.9 14.9 %collective-permute-start.2 = (f32[128,128]{1,0:T(8,128)S(1)}, f32[128,128]{1,0:T(8,128)S(1)}, u32[]{:S(2)}, u32[]{:S(2)}) collective-permute-start(f32[128,128]{1,0:T(8,128)S(1)} %get-tuple-element.26.after), channel_id=1, source_target_pairs={{0,64},{1,65},{2,66},{3,67},{4,68},{5,69},{6,70},{7,71},{8,72},{9,... | collective-permute-start | bytes 196616 | tf_op jit(solution)/shard_map/ppermute | solution.py:408
  49.6 9.8 %copy-start.2 = (f32[1,1,1,3,16,128]{5,4,3,2,1,0:T(8,128)S(1)}, f32[1,1,1,3,16,128]{5,4,3,2,1,0:T(8,128)}, u32[]{:S(2)}) copy-start(f32[1,1,1,3,16,128]{5,4,3,2,1,0:T(8,128)} %param.15) | copy-start | bytes 73732
  49.6 9.8 %all-to-all-start = ((f32[4,8,128]{2,1,0:T(8,128)}), f32[4,8,128]{2,1,0:T(8,128)S(1)}, u32[]{:S(2)}, u32[]{:S(2)}) async-start(f32[4,8,128]{2,1,0:T(8,128)} %bitcast.5), calls=%async_computation | async-start | bytes 32768 | tf_op jit(solution)/shard_map/all_to_all | solution.py:412
  54.1 0.7 copy-start.8
  54.7 4.7 %copy-start.3 = (f32[1,1,1,16,128]{4,3,2,1,0:T(8,128)S(1)}, f32[1,1,1,16,128]{4,3,2,1,0:T(8,128)}, u32[]{:S(2)}) copy-start(f32[1,1,1,16,128]{4,3,2,1,0:T(8,128)} %param.17) | copy-start | bytes 24580
  69.3 27.4 %copy-start.1 = (f32[5,8,16,128]{3,2,1,0:T(8,128)S(1)}, f32[5,8,16,128]{3,2,1,0:T(8,128)}, u32[]{:S(2)}) copy-start(f32[5,8,16,128]{3,2,1,0:T(8,128)} %param.9) | copy-start | bytes 983044
  69.3 27.4 %copy-start.4 = (f32[5,8,16,128]{3,2,1,0:T(8,128)S(1)}, f32[5,8,16,128]{3,2,1,0:T(8,128)}, u32[]{:S(2)}) copy-start(f32[5,8,16,128]{3,2,1,0:T(8,128)} %param.10) | copy-start | bytes 983044
  69.5 3.9 %collective-permute-start.5 = (f32[80,128]{1,0:T(8,128)S(1)}, f32[80,128]{1,0:T(8,128)S(1)}, u32[]{:S(2)}, u32[]{:S(2)}) collective-permute-start(f32[80,128]{1,0:T(8,128)S(1)} %get-tuple-element.37), channel_id=1, source_target_pairs={{0,4},{1,5},{2,6},{3,7},{4,0},{5,1},{6,2},{7,3},{8,12},{9,13},{10,... | collective-permute-start | bytes 122888 | tf_op jit(solution)/shard_map/ppermute | solution.py:408
  71.4 6.5 %collective-permute-start.6 = (f32[80,128]{1,0:T(8,128)S(1)}, f32[80,128]{1,0:T(8,128)S(1)}, u32[]{:S(2)}, u32[]{:S(2)}) collective-permute-start(f32[80,128]{1,0:T(8,128)S(1)} %get-tuple-element.38), channel_id=1, source_target_pairs={{0,124},{1,125},{2,126},{3,127},{4,8},{5,9},{6,10},{7,11},{8,4},{9... | collective-permute-start | bytes 122888 | tf_op jit(solution)/shard_map/ppermute | solution.py:408
  78.0 19.3 %collective-permute-start.9 = (f32[8,128]{1,0:T(8,128)S(1)}, f32[8,128]{1,0:T(8,128)S(1)}, u32[]{:S(2)}, u32[]{:S(2)}) collective-permute-start(f32[8,128]{1,0:T(8,128)S(1)} %get-tuple-element.42), channel_id=1, source_target_pairs={{0,128},{1,129},{2,130},{3,131},{60,188},{61,189},{62,190},{63,191... | collective-permute-start | bytes 12296 | tf_op jit(solution)/shard_map/ppermute | solution.py:408
  80.6 16.7 %collective-permute-start.8 = (f32[80,128]{1,0:T(8,128)S(1)}, f32[80,128]{1,0:T(8,128)S(1)}, u32[]{:S(2)}, u32[]{:S(2)}) collective-permute-start(f32[80,128]{1,0:T(8,128)S(1)} %get-tuple-element.41), channel_id=1, source_target_pairs={{0,960},{1,961},{2,962},{3,963},{4,964},{5,965},{6,966},{7,967},{8... | collective-permute-start | bytes 122888 | tf_op jit(solution)/shard_map/ppermute | solution.py:408
  90.8 15.3 %collective-permute-start.7 = (f32[120,128]{1,0:T(8,128)S(1)}, f32[120,128]{1,0:T(8,128)S(1)}, u32[]{:S(2)}, u32[]{:S(2)}) collective-permute-start(f32[120,128]{1,0:T(8,128)S(1)} %get-tuple-element.40.after), channel_id=1, source_target_pairs={{0,64},{1,65},{2,66},{3,67},{4,68},{5,69},{6,70},{7,71},{8,72},{9,... | collective-permute-start | bytes 184328 | tf_op jit(solution)/shard_map/ppermute | solution.py:408

commit v3 on v2

--- a/solution.py
+++ b/solution.py
@@ -70,10 +70,8 @@
 def post_ends(ref, low, high):
     k, n = lax.axis_index("gz"), ref.shape[0] // 8
     ref[...] = jnp.zeros(ref.shape, F32)
-    up, down = lax.rem(k + 1, n) * 8, lax.rem(k + n - 1, n) * 8
-    for row in range(8):
-        ref[pl.ds(up + row, 1), :] = high(row)
-        ref[pl.ds(down + row, 1), :] = low(row)
+    ref[rows(lax.rem(k + 1, n) * 8, 8, 8), :] = jnp.concatenate(high, axis=0)
+    ref[rows(lax.rem(k + n - 1, n) * 8, 8, 8), :] = jnp.concatenate(low, axis=0)
 
 
 def get_ends(ref):
@@ -156,7 +154,7 @@
     for n in range(8):
         part = gas[n * 128 : n * 128 + 128, :] if n < 5 else halo[(n - 5) * 128 : (n - 4) * 128, :]
         turned.append(part.T)
-    post_ends(ends, lambda n: turned[n][0:1, :], lambda n: turned[n][127:128, :])
+    post_ends(ends, [t[0:1, :] for t in turned], [t[127:128, :] for t in turned])
 
 
 def three(place, anchor, offset):
@@ -167,10 +165,16 @@
     return jnp.where(step == -1, low, jnp.where(step == 0, middle, jnp.where(step == 1, high, 0.0)))
 
 
-def weigh(gas, cell, shift, frac, after, planar, vertical, part):
+def weigh(
+    gas, cell, tile, count, frac, mass, vel, temp, after, planar, vertical, across, part, drops
+):
     del after
     odd_i, odd_j, _ = places()
     blocks = cell.shape[0]
+    drops[0:blocks, :] = jnp.exp(jnp.log(mass[...]) * (1.0 / 3.0))
+    slot = lax.broadcasted_iota(I32, (1, 128), 1)
+    drops[2 * blocks : 5 * blocks, :] = vel[...]
+    drops[5 * blocks : 6 * blocks, :] = temp[...]
     near_x, far_x = 8 - 9 * odd_i, 9 * odd_i - 1
     c_y, d_y = 16 - 17 * odd_j, 17 * odd_j - 1
     r = lax.broadcasted_iota(I32, (192, 128), 0)
@@ -179,21 +183,22 @@
     on_y = jnp.where(q < 8, q, jnp.where(q == 8, near_x, jnp.where(q == 9, far_x, FAR_AWAY)))
     place_x = jnp.where(group < 0, r >> 4, jnp.where(group == 0, near_x, jnp.where(group == 1, far_x, on_y)))
     place_y = jnp.where(group == 2, c_y, jnp.where(group == 3, d_y, q))
-    s = lax.broadcasted_iota(I32, (144, 128), 0)
+    s = lax.broadcasted_iota(I32, (256, 128), 0)
     place_z = jnp.where(s < 128, s, jnp.where(s == 128, -1, jnp.where(s == 129, 128, FAR_AWAY)))
     cells = gas[...].astype(BF16)
     for b in range(blocks):
         lanes = slice(b * 128, b * 128 + 128)
         at = cell[b : b + 1, :]
         wx = three(place_x, at >> 10, frac[b : b + 1, :])
-        wy = three(place_y, ((at >> 7) & 7) + shift[b : b + 1, :], frac[blocks + b : blocks + b + 1, :])
-        wz = three(place_z, at & 127, frac[2 * blocks + b : 2 * blocks + b + 1, :]).astype(BF16)
+        drops[blocks + b : blocks + b + 1, :] = jnp.where(slot < count[0:1, b : b + 1], PARCEL, 0.0).astype(F32)
+        wy = three(place_y, ((at >> 7) & 7) + 8 * tile[0:1, b : b + 1], frac[blocks + b : blocks + b + 1, :])
+        wz = three(place_z, at & 127, frac[2 * blocks + b : 2 * blocks + b + 1, :])
         flat = (wx * wy).astype(BF16)
         planar[0:192, lanes] = flat
         planar[192:256, lanes] = jnp.zeros((64, 128), BF16)
-        vertical[0:144, lanes] = wz
-        vertical[144:256, lanes] = jnp.zeros((112, 128), BF16)
-        seen = jnp.dot(cells, wz[0:128, :], preferred_element_type=F32)
+        vertical[:, lanes] = wz[0:144, :].astype(BF16)
+        across[lanes, :] = jnp.concatenate([wz[0:128, :].T, wz[128:256, :].T], axis=1).astype(BF16)
+        seen = jnp.dot(cells, wz[0:128, :].astype(BF16), preferred_element_type=F32)
         own = flat[0:128, :].astype(F32)
         for c in range(5):
             part[c * blocks + b : c * blocks + b + 1, :] = jnp.sum(
@@ -201,12 +206,8 @@
             )
 
 
-def deposit(
-    halo, z_ends, planar, vertical, part, diameter, alive, vel, temp, sums, ghosts,
-    gas_at, source, weighted, total,
-):
-    blocks = diameter.shape[0]
-
+def deposit(halo, z_ends, planar, vertical, across, part, drops, sums, ghosts, gas_at, source, weighted):
+    blocks = drops.shape[0] // 6
     below, above = get_ends(z_ends)
 
     def z_rows(v):
@@ -219,30 +220,28 @@
     ends = jnp.concatenate([z_rows(below), z_rows(above)], axis=0).astype(BF16)
     at_ends = jnp.dot(ends, planar[...], preferred_element_type=F32)
     around = halo[0 : 5 * HALO, :].astype(BF16)
-    for b in range(blocks):
-        lanes = slice(b * 128, b * 128 + 128)
+    for b in range(0, blocks, 2):
+        lanes = slice(b * 128, b * 128 + 256)
         seen = jnp.dot(around, vertical[0:128, lanes], preferred_element_type=F32)
         side = planar[128:192, lanes].astype(F32)
         edge = vertical[128:144, lanes].astype(F32)
         ended = at_ends[0:8, lanes] * edge[0:1, :] + at_ends[8:16, lanes] * edge[1:2, :]
         for c in range(5):
             n = c * blocks + b
-            gas_at[n : n + 1, :] = (
-                part[n : n + 1, :]
-                + ended[c : c + 1, :]
-                + jnp.sum(seen[c * HALO : c * HALO + HALO, :] * side, axis=0, keepdims=True)
-            )
-    d = diameter[...]
-    live = alive[...]
-    warm = gas_at[4 * blocks : 5 * blocks, :] - temp[...]
+            row = ended[c : c + 1, :] + jnp.sum(seen[c * HALO : c * HALO + HALO, :] * side, axis=0, keepdims=True)
+            gas_at[n : n + 1, :] = part[n : n + 1, :] + row[:, 0:128]
+            gas_at[n + 1 : n + 2, :] = part[n + 1 : n + 2, :] + row[:, 128:256]
+    d = drops[0:blocks, :]
+    live = drops[blocks : 2 * blocks, :]
+    warm = gas_at[4 * blocks : 5 * blocks, :] - drops[5 * blocks : 6 * blocks, :]
     soft = jnp.maximum(warm, 0.0) + jnp.log1p(jnp.exp(-jnp.abs(warm)))
     rate = d * jnp.log1p(soft)
     pull = d * gas_at[0:blocks, :]
     source[0:blocks, :] = rate * live
-    for m in range(3):
-        v = vel[m * blocks : (m + 1) * blocks, :]
-        u = gas_at[(m + 1) * blocks : (m + 2) * blocks, :]
-        source[(m + 1) * blocks : (m + 2) * blocks, :] = (rate * v - pull * (u - v)) * live
+    for m in range(1, 4):
+        v = drops[(m + 1) * blocks : (m + 2) * blocks, :]
+        u = gas_at[m * blocks : (m + 1) * blocks, :]
+        source[m * blocks : (m + 1) * blocks, :] = (rate * v - pull * (u - v)) * live
     source[4 * blocks : 5 * blocks, :] = (-(d * warm) - LATENT * rate) * live
     for b in range(blocks):
         lanes = slice(b * 128, b * 128 + 128)
@@ -251,13 +250,18 @@
             scaled = (flat * source[c * blocks + b : c * blocks + b + 1, :]).astype(BF16)
             weighted[c * OWN : c * OWN + OWN, lanes] = scaled[0:128, :]
             weighted[640 + c * HALO : 640 + c * HALO + HALO, lanes] = scaled[128:192, :]
-        weighted[960:1024, lanes] = jnp.zeros((64, 128), BF16)
-    total[...] = lax.dot_general(
-        weighted[...], vertical[...], (((1,), (1,)), ((), ())), preferred_element_type=F32
-    )
-    sums[...] = total[0:960, 0:128]
-    turned = [total[n * 128 : n * 128 + 128, 128:256].T for n in range(8)]
-    post_ends(ghosts, lambda n: turned[n][0:1, :], lambda n: turned[n][1:2, :])
+    low, high = [], []
+    for n in range(8):
+        size = 128 if n < 7 else 64
+        total = jnp.dot(weighted[n * 128 : n * 128 + size, :], across[...], preferred_element_type=F32)
+        sums[n * 128 : n * 128 + size, :] = total[:, 0:128]
+        ends = total[:, 128:256]
+        if size < 128:
+            ends = jnp.concatenate([ends, jnp.zeros((128 - size, 128), F32)], axis=0)
+        turned = ends.T
+        low.append(turned[0:1, :])
+        high.append(turned[1:2, :])
+    post_ends(ghosts, low, high)
 
 
 def upright(below, above):
@@ -419,23 +423,26 @@
     frac = drop_frac.reshape(3 * blocks, 128)
     vel = drop_vel.reshape(3 * blocks, 128)
     temp = drop_temp.reshape(blocks, 128)
-    diameter = jnp.cbrt(drop_mass.reshape(blocks, 128))
-    slots = lax.broadcasted_iota(I32, (blocks, 128), 1)
-    alive = jnp.where(slots < droplets_per_block.reshape(blocks, 1), PARCEL, 0.0).astype(F32)
-    shift = jnp.broadcast_to(8 * block_tile.reshape(blocks, 1), (blocks, 128)).astype(I32)
+    mass = drop_mass.reshape(blocks, 128)
+    count = droplets_per_block.reshape(1, blocks)
+    tile = block_tile.reshape(1, blocks)
 
     to_c, to_d = call(pack_y, [((40, 128), F32)] * 2, gas)
     gas_d, gas_c = send(to_d, "D"), send(to_c, "C")
-    to_near, to_far, to_turn = call(
-        pack_x, [((128, 128), F32), ((96, 128), F32), ((8, 128), F32)], gas, gas_c, gas_d
-    )
+    to_near, to_far, to_turn = call(pack_x, [((128, 128), F32), ((96, 128), F32), ((8, 128), F32)], gas, gas_c, gas_d)
     gas_near, gas_far = send(to_near, "near"), send(to_far, "far")
     gas_turn = send(to_turn, "turn")
-    planar, vertical, part = call(
+    planar, vertical, across, part, drops = call(
         weigh,
-        [((256, blocks * 128), BF16), ((256, blocks * 128), BF16), ((5 * blocks, 128), F32)],
-        gas, cell, shift, frac, to_near,
-        loose=(4,), flops=1 << 32,
+        [
+            ((256, blocks * 128), BF16),
+            ((144, blocks * 128), BF16),
+            ((blocks * 128, 256), BF16),
+            ((5 * blocks, 128), F32),
+            ((6 * blocks, 128), F32),
+        ],
+        gas, cell, tile, count, frac, mass, vel, temp, to_near,
+        loose=(8,), flops=1 << 32,
     )
     halo, ends = call(
         join_halo, [((384, 128), F32), ends_shape],
@@ -445,12 +452,11 @@
     ends = swap_ends(ends)
     sums, ghosts = call(
         deposit, [((960, 128), F32), ends_shape],
-        halo, ends, planar, vertical, part, diameter, alive, vel, temp,
+        halo, ends, planar, vertical, across, part, drops,
         scratch=[
             pltpu.VMEM((5 * blocks, 128), F32),
             pltpu.VMEM((5 * blocks, 128), F32),
-            pltpu.VMEM((1024, blocks * 128), BF16),
-            pltpu.VMEM((1024, 256), F32),
+            pltpu.VMEM((960, blocks * 128), BF16),
         ],
     )
     own, sides, to_c, to_d = call(
@@ -458,9 +464,7 @@
         sums, swap_ends(ghosts),
     )
     dep_d, dep_c = send(to_d, "D"), send(to_c, "C")
-    to_near, to_far, to_turn = call(
-        fold_y, [((120, 128), F32), ((80, 128), F32), ((8, 128), F32)], sides, dep_c, dep_d
-    )
+    to_near, to_far, to_turn = call(fold_y, [((120, 128), F32), ((80, 128), F32), ((8, 128), F32)], sides, dep_c, dep_d)
     dep_near, dep_far = send(to_near, "near"), send(to_far, "far")
     dep_turn = send(to_turn, "turn")
     base = call(

time: 107 us -> 107 us (level)
  the two profiles are of different devices: /device:TPU:8 before, /device:TPU:1 now
where the time goes in v3:
time: 107 us; the launch traced here: 106 us
  starting transfers between devices  56.2 us (53%)
  waiting for transfers between devices  27.3 us (26%)
  blocking collectives  14.6 us (14%)
  Pallas kernels  6.34 us (6%)
  local copies, waits for them, and re-layouts  1.62 us (2%)
    ppermute x10, starting transfers between devices, send(): return lax.ppermute(values, AXES, routes[route])  56.2 us
    ppermute x10, waiting for transfers between devices, send(): return lax.ppermute(values, AXES, routes[route])  27.3 us
    all_to_all x2, blocking collectives, swap_ends(): return lax.all_to_all(chunks, 'gz', 0, 0).reshape(values.shape)  14.6 us
    pallas_call x9, Pallas kernels, call(): pl.pallas_call(body, out_shape=[jax.ShapeDtypeStruct(s, t) for s, t in ou...  6.34 us
  transfers between devices with their start and end apart: 10, of which 6 were waited for; matrix products, arithmetic and copies ran while one was open for 0% of the time, Pallas kernels for 3%

profile of v3, /device:TPU:1, one launch (start us, length us, event | category | flops | bytes accessed | tf_op | source)
XLA Modules:
  0.0 106.3 jit_solution(11059356550971216204)
XLA Ops:
  0.0 0.0 copy-start
  0.0 1.0 copy-done
  1.0 16.0 %collective-permute-start = (f32[40,128]{1,0:T(8,128)S(1)}, f32[40,128]{1,0:T(8,128)S(1)}, u32[]{:S(2)}, u32[]{:S(2)}) collective-permute-start(f32[40,128]{1,0:T(8,128)S(1)} %get-tuple-element.26), channel_id=1, source_target_pairs={{0,4},{1,5},{2,6},{3,7},{4,0},{5,1},{6,2},{7,3},{8,12},{9,13},{10,... | collective-permute-start | bytes 61448 | tf_op jit(solution)/shard_map/ppermute | solution.py:412
  17.0 0.0 copy-start.3
  17.0 0.0 copy-start.4
  17.1 1.9 %collective-permute-start.1 = (f32[40,128]{1,0:T(8,128)S(1)}, f32[40,128]{1,0:T(8,128)S(1)}, u32[]{:S(2)}, u32[]{:S(2)}) collective-permute-start(f32[40,128]{1,0:T(8,128)S(1)} %get-tuple-element.27), channel_id=1, source_target_pairs={{0,124},{1,125},{2,126},{3,127},{4,8},{5,9},{6,10},{7,11},{8,4},{9... | collective-permute-start | bytes 61448 | tf_op jit(solution)/shard_map/ppermute | solution.py:412
  19.0 0.0 collective-permute-done.from_c
  19.0 3.2 %collective-permute-done.1.from_d = f32[40,128]{1,0:T(8,128)S(1)} collective-permute-done((f32[40,128]{1,0:T(8,128)S(1)}, f32[40,128]{1,0:T(8,128)S(1)}, u32[]{:S(2)}, u32[]{:S(2)}) %collective-permute-start.1) | collective-permute-done | bytes 20512 | tf_op jit(solution)/shard_map/ppermute | solution.py:412
  22.2 0.0 copy-start.7
  22.2 0.7 collective-permute-start.4
  22.8 0.0 copy-start.6
  22.9 0.0 copy-start.5
  22.9 9.7 %collective-permute-start.3 = (f32[96,128]{1,0:T(8,128)S(1)}, f32[96,128]{1,0:T(8,128)S(1)}, u32[]{:S(2)}, u32[]{:S(2)}) collective-permute-start(f32[96,128]{1,0:T(8,128)S(1)} %get-tuple-element.29), channel_id=1, source_target_pairs={{0,960},{1,961},{2,962},{3,963},{4,964},{5,965},{6,966},{7,967},{8... | collective-permute-start | bytes 147464 | tf_op jit(solution)/shard_map/ppermute | solution.py:412
  32.5 1.9 %collective-permute-start.2 = (f32[128,128]{1,0:T(8,128)S(1)}, f32[128,128]{1,0:T(8,128)S(1)}, u32[]{:S(2)}, u32[]{:S(2)}) collective-permute-start(f32[128,128]{1,0:T(8,128)S(1)} %get-tuple-element.28.after), channel_id=1, source_target_pairs={{0,64},{1,65},{2,66},{3,67},{4,68},{5,69},{6,70},{7,71},{8,72},{9,... | collective-permute-start | bytes 196616 | tf_op jit(solution)/shard_map/ppermute | solution.py:412
  34.5 0.0 copy-start.8
  34.5 0.0 copy-start.9
  34.5 0.0 copy-done.3
  34.5 0.0 copy-done.4
  34.5 0.0 copy-done.7
  34.5 0.0 copy-done.6
  34.5 0.0 copy-done.5
  34.5 0.6 copy-done.8
  35.1 0.0 copy-done.9
  35.1 2.2 %shard_map.93 = (bf16[256,2048]{1,0:T(8,128)(2,1)S(1)}, bf16[144,2048]{1,0:T(8,128)(2,1)S(1)}, bf16[2048,256]{1,0:T(8,128)(2,1)S(1)}, f32[80,128]{1,0:T(8,128)S(1)}, f32[96,128]{1,0:T(8,128)S(1)}) custom-call(f32[640,128]{1,0:T(8,128)S(1)} %bitcast.16, s32[16,128]{1,0:T(8,128)S(1)} %bitcast.27, s32[1,16]{1,0:T(1,128)S(1)} %bitcast.30, s32[1,16]{1,0:T(1,128)S(1)} %bitcast.31, ...), custom_call_target="tpu_custom_call" | custom-call | flops 4294967296 | bytes 100000 | tf_op jit(solution)/shard_map/pallas_call | solution.py:395
  37.4 0.0 collective-permute-done.4.from_turn
  37.4 1.2 %collective-permute-done.3.from_far = f32[96,128]{1,0:T(8,128)S(1)} collective-permute-done((f32[96,128]{1,0:T(8,128)S(1)}, f32[96,128]{1,0:T(8,128)S(1)}, u32[]{:S(2)}, u32[]{:S(2)}) %collective-permute-start.3) | collective-permute-done | bytes 49184 | tf_op jit(solution)/shard_map/ppermute | solution.py:412
  38.5 7.9 %collective-permute-done.2.from_near = f32[128,128]{1,0:T(8,128)S(1)} collective-permute-done((f32[128,128]{1,0:T(8,128)S(1)}, f32[128,128]{1,0:T(8,128)S(1)}, u32[]{:S(2)}, u32[]{:S(2)}) %collective-permute-start.2) | collective-permute-done | bytes 65568 | tf_op jit(solution)/shard_map/ppermute | solution.py:412
  46.4 0.2 shard_map.94
  46.6 8.0 %all_to_all.10 = f32[4,8,128]{2,1,0:T(8,128)S(1)} all-to-all(f32[4,8,128]{2,1,0:T(8,128)S(1)} %bitcast.22), channel_id=1, replica_groups=mesh['gx'=16,'gy'=16,'gz'=4] {'gz'}, dimensions={0} | all-to-all | bytes 32768 | tf_op jit(solution)/shard_map/all_to_all | solution.py:416
  54.6 2.3 %shard_map.95 = (f32[960,128]{1,0:T(8,128)S(1)}, f32[32,128]{1,0:T(8,128)S(1)}) custom-call(f32[384,128]{1,0:T(8,128)S(1)} %get-tuple-element.32.halo, f32[32,128]{1,0:T(8,128)S(1)} %bitcast.19, bf16[256,2048]{1,0:T(8,128)(2,1)S(1)} %get-tuple-element.34.planar, bf16[144,2048]{1,0:T(8,128)(2,1)S(1)} %get-tuple-element.35.vertical, ...), custom_call_target="tpu_custom_call" | custom-call | flops 10000 | bytes 100000 | tf_op jit(solution)/shard_map/pallas_call | solution.py:395
  57.0 6.6 %all_to_all.11 = f32[4,8,128]{2,1,0:T(8,128)S(1)} all-to-all(f32[4,8,128]{2,1,0:T(8,128)S(1)} %bitcast.23), channel_id=1, replica_groups=mesh['gx'=16,'gy'=16,'gz'=4] {'gz'}, dimensions={0} | all-to-all | bytes 32768 | tf_op jit(solution)/shard_map/all_to_all | solution.py:416
  63.5 0.0 copy-start.1
  63.5 0.0 copy-start.2
  63.5 0.2 shard_map.96
  63.7 10.5 %collective-permute-start.5 = (f32[80,128]{1,0:T(8,128)S(1)}, f32[80,128]{1,0:T(8,128)S(1)}, u32[]{:S(2)}, u32[]{:S(2)}) collective-permute-start(f32[80,128]{1,0:T(8,128)S(1)} %get-tuple-element.41), channel_id=1, source_target_pairs={{0,4},{1,5},{2,6},{3,7},{4,0},{5,1},{6,2},{7,3},{8,12},{9,13},{10,... | collective-permute-start | bytes 122888 | tf_op jit(solution)/shard_map/ppermute | solution.py:412
  74.3 1.9 %collective-permute-start.6 = (f32[80,128]{1,0:T(8,128)S(1)}, f32[80,128]{1,0:T(8,128)S(1)}, u32[]{:S(2)}, u32[]{:S(2)}) collective-permute-start(f32[80,128]{1,0:T(8,128)S(1)} %get-tuple-element.42), channel_id=1, source_target_pairs={{0,124},{1,125},{2,126},{3,127},{4,8},{5,9},{6,10},{7,11},{8,4},{9... | collective-permute-start | bytes 122888 | tf_op jit(solution)/shard_map/ppermute | solution.py:412
  76.2 0.0 collective-permute-done.5.from_c
  76.2 3.7 %collective-permute-done.6.from_d = f32[80,128]{1,0:T(8,128)S(1)} collective-permute-done((f32[80,128]{1,0:T(8,128)S(1)}, f32[80,128]{1,0:T(8,128)S(1)}, u32[]{:S(2)}, u32[]{:S(2)}) %collective-permute-start.6) | collective-permute-done | bytes 40992 | tf_op jit(solution)/shard_map/ppermute | solution.py:412
  79.9 0.7 collective-permute-start.9
  80.6 7.4 %collective-permute-start.8 = (f32[80,128]{1,0:T(8,128)S(1)}, f32[80,128]{1,0:T(8,128)S(1)}, u32[]{:S(2)}, u32[]{:S(2)}) collective-permute-start(f32[80,128]{1,0:T(8,128)S(1)} %get-tuple-element.45), channel_id=1, source_target_pairs={{0,960},{1,961},{2,962},{3,963},{4,964},{5,965},{6,966},{7,967},{8... | collective-permute-start | bytes 122888 | tf_op jit(solution)/shard_map/ppermute | solution.py:412
  88.0 5.4 %collective-permute-start.7 = (f32[120,128]{1,0:T(8,128)S(1)}, f32[120,128]{1,0:T(8,128)S(1)}, u32[]{:S(2)}, u32[]{:S(2)}) collective-permute-start(f32[120,128]{1,0:T(8,128)S(1)} %get-tuple-element.44.after), channel_id=1, source_target_pairs={{0,64},{1,65},{2,66},{3,67},{4,68},{5,69},{6,70},{7,71},{8,72},{9,... | collective-permute-start | bytes 184328 | tf_op jit(solution)/shard_map/ppermute | solution.py:412
  93.5 0.0 copy-done.1
  93.5 0.0 copy-done.2
  93.5 0.5 shard_map.98.base
  94.1 0.0 collective-permute-done.9.from_turn
  94.1 2.4 %collective-permute-done.8.from_far = f32[80,128]{1,0:T(8,128)S(1)} collective-permute-done((f32[80,128]{1,0:T(8,128)S(1)}, f32[80,128]{1,0:T(8,128)S(1)}, u32[]{:S(2)}, u32[]{:S(2)}) %collective-permute-start.8) | collective-permute-done | bytes 40992 | tf_op jit(solution)/shard_map/ppermute | solution.py:412
  96.5 9.0 %collective-permute-done.7.from_near = f32[120,128]{1,0:T(8,128)S(1)} collective-permute-done((f32[120,128]{1,0:T(8,128)S(1)}, f32[120,128]{1,0:T(8,128)S(1)}, u32[]{:S(2)}, u32[]{:S(2)}) %collective-permute-start.7) | collective-permute-done | bytes 61472 | tf_op jit(solution)/shard_map/ppermute | solution.py:412
  105.5 0.8 shard_map.99
  (3 shorter events, 0.1 us)
Async XLA Ops:
  0.0 1.0 copy-start
  1.0 18.0 %collective-permute-start = (f32[40,128]{1,0:T(8,128)S(1)}, f32[40,128]{1,0:T(8,128)S(1)}, u32[]{:S(2)}, u32[]{:S(2)}) collective-permute-start(f32[40,128]{1,0:T(8,128)S(1)} %get-tuple-element.26), channel_id=1, source_target_pairs={{0,4},{1,5},{2,6},{3,7},{4,0},{5,1},{6,2},{7,3},{8,12},{9,13},{10,... | collective-permute-start | bytes 61448 | tf_op jit(solution)/shard_map/ppermute | solution.py:412
  17.0 17.5 %copy-start.3 = (f32[1,1,1,3,16,128]{5,4,3,2,1,0:T(8,128)S(1)}, f32[1,1,1,3,16,128]{5,4,3,2,1,0:T(8,128)}, u32[]{:S(2)}) copy-start(f32[1,1,1,3,16,128]{5,4,3,2,1,0:T(8,128)} %param.14) | copy-start | bytes 73732
  17.0 17.5 %copy-start.4 = (f32[1,1,1,3,16,128]{5,4,3,2,1,0:T(8,128)S(1)}, f32[1,1,1,3,16,128]{5,4,3,2,1,0:T(8,128)}, u32[]{:S(2)}) copy-start(f32[1,1,1,3,16,128]{5,4,3,2,1,0:T(8,128)} %param.15) | copy-start | bytes 73732
  17.1 5.1 %collective-permute-start.1 = (f32[40,128]{1,0:T(8,128)S(1)}, f32[40,128]{1,0:T(8,128)S(1)}, u32[]{:S(2)}, u32[]{:S(2)}) collective-permute-start(f32[40,128]{1,0:T(8,128)S(1)} %get-tuple-element.27), channel_id=1, source_target_pairs={{0,124},{1,125},{2,126},{3,127},{4,8},{5,9},{6,10},{7,11},{8,4},{9... | collective-permute-start | bytes 61448 | tf_op jit(solution)/shard_map/ppermute | solution.py:412
  22.2 12.4 %copy-start.7 = (f32[1,1,1,16,128]{4,3,2,1,0:T(8,128)S(1)}, f32[1,1,1,16,128]{4,3,2,1,0:T(8,128)}, u32[]{:S(2)}) copy-start(f32[1,1,1,16,128]{4,3,2,1,0:T(8,128)} %param.17) | copy-start | bytes 24580
  22.2 15.2 %collective-permute-start.4 = (f32[8,128]{1,0:T(8,128)S(1)}, f32[8,128]{1,0:T(8,128)S(1)}, u32[]{:S(2)}, u32[]{:S(2)}) collective-permute-start(f32[8,128]{1,0:T(8,128)S(1)} %get-tuple-element.30), channel_id=1, source_target_pairs={{0,128},{1,129},{2,130},{3,131},{60,188},{61,189},{62,190},{63,191... | collective-permute-start | bytes 12296 | tf_op jit(solution)/shard_map/ppermute | solution.py:412
  22.8 11.7 %copy-start.6 = (f32[1,1,1,16,128]{4,3,2,1,0:T(8,128)S(1)}, f32[1,1,1,16,128]{4,3,2,1,0:T(8,128)}, u32[]{:S(2)}) copy-start(f32[1,1,1,16,128]{4,3,2,1,0:T(8,128)} %param.16) | copy-start | bytes 24580
  22.9 11.7 %copy-start.5 = (s32[1,1,1,16,128]{4,3,2,1,0:T(8,128)S(1)}, s32[1,1,1,16,128]{4,3,2,1,0:T(8,128)}, u32[]{:S(2)}) copy-start(s32[1,1,1,16,128]{4,3,2,1,0:T(8,128)} %param.11) | copy-start | bytes 24580
  22.9 15.7 %collective-permute-start.3 = (f32[96,128]{1,0:T(8,128)S(1)}, f32[96,128]{1,0:T(8,128)S(1)}, u32[]{:S(2)}, u32[]{:S(2)}) collective-permute-start(f32[96,128]{1,0:T(8,128)S(1)} %get-tuple-element.29), channel_id=1, source_target_pairs={{0,960},{1,961},{2,962},{3,963},{4,964},{5,965},{6,966},{7,967},{8... | collective-permute-start | bytes 147464 | tf_op jit(solution)/shard_map/ppermute | solution.py:412
  32.5 13.9 %collective-permute-start.2 = (f32[128,128]{1,0:T(8,128)S(1)}, f32[128,128]{1,0:T(8,128)S(1)}, u32[]{:S(2)}, u32[]{:S(2)}) collective-permute-start(f32[128,128]{1,0:T(8,128)S(1)} %get-tuple-element.28.after), channel_id=1, source_target_pairs={{0,64},{1,65},{2,66},{3,67},{4,68},{5,69},{6,70},{7,71},{8,72},{9,... | collective-permute-start | bytes 196616 | tf_op jit(solution)/shard_map/ppermute | solution.py:412
  34.5 0.7 copy-start.8
  34.5 0.7 copy-start.9
  63.5 30.0 %copy-start.1 = (f32[5,8,16,128]{3,2,1,0:T(8,128)S(1)}, f32[5,8,16,128]{3,2,1,0:T(8,128)}, u32[]{:S(2)}) copy-start(f32[5,8,16,128]{3,2,1,0:T(8,128)} %param.9) | copy-start | bytes 983044
  63.5 30.0 %copy-start.2 = (f32[5,8,16,128]{3,2,1,0:T(8,128)S(1)}, f32[5,8,16,128]{3,2,1,0:T(8,128)}, u32[]{:S(2)}) copy-start(f32[5,8,16,128]{3,2,1,0:T(8,128)} %param.10) | copy-start | bytes 983044
  63.7 12.5 %collective-permute-start.5 = (f32[80,128]{1,0:T(8,128)S(1)}, f32[80,128]{1,0:T(8,128)S(1)}, u32[]{:S(2)}, u32[]{:S(2)}) collective-permute-start(f32[80,128]{1,0:T(8,128)S(1)} %get-tuple-element.41), channel_id=1, source_target_pairs={{0,4},{1,5},{2,6},{3,7},{4,0},{5,1},{6,2},{7,3},{8,12},{9,13},{10,... | collective-permute-start | bytes 122888 | tf_op jit(solution)/shard_map/ppermute | solution.py:412
  74.3 5.6 %collective-permute-start.6 = (f32[80,128]{1,0:T(8,128)S(1)}, f32[80,128]{1,0:T(8,128)S(1)}, u32[]{:S(2)}, u32[]{:S(2)}) collective-permute-start(f32[80,128]{1,0:T(8,128)S(1)} %get-tuple-element.42), channel_id=1, source_target_pairs={{0,124},{1,125},{2,126},{3,127},{4,8},{5,9},{6,10},{7,11},{8,4},{9... | collective-permute-start | bytes 122888 | tf_op jit(solution)/shard_map/ppermute | solution.py:412
  79.9 14.1 %collective-permute-start.9 = (f32[8,128]{1,0:T(8,128)S(1)}, f32[8,128]{1,0:T(8,128)S(1)}, u32[]{:S(2)}, u32[]{:S(2)}) collective-permute-start(f32[8,128]{1,0:T(8,128)S(1)} %get-tuple-element.46), channel_id=1, source_target_pairs={{0,128},{1,129},{2,130},{3,131},{60,188},{61,189},{62,190},{63,191... | collective-permute-start | bytes 12296 | tf_op jit(solution)/shard_map/ppermute | solution.py:412
  80.6 15.9 %collective-permute-start.8 = (f32[80,128]{1,0:T(8,128)S(1)}, f32[80,128]{1,0:T(8,128)S(1)}, u32[]{:S(2)}, u32[]{:S(2)}) collective-permute-start(f32[80,128]{1,0:T(8,128)S(1)} %get-tuple-element.45), channel_id=1, source_target_pairs={{0,960},{1,961},{2,962},{3,963},{4,964},{5,965},{6,966},{7,967},{8... | collective-permute-start | bytes 122888 | tf_op jit(solution)/shard_map/ppermute | solution.py:412
  88.0 17.5 %collective-permute-start.7 = (f32[120,128]{1,0:T(8,128)S(1)}, f32[120,128]{1,0:T(8,128)S(1)}, u32[]{:S(2)}, u32[]{:S(2)}) collective-permute-start(f32[120,128]{1,0:T(8,128)S(1)} %get-tuple-element.44.after), channel_id=1, source_target_pairs={{0,64},{1,65},{2,66},{3,67},{4,68},{5,69},{6,70},{7,71},{8,72},{9,... | collective-permute-start | bytes 184328 | tf_op jit(solution)/shard_map/ppermute | solution.py:412

commit v4 on v3

--- a/solution.py
+++ b/solution.py
@@ -48,7 +48,8 @@
         return None
 
     return {
-        "near": pairs(lambda i, j, k: (i ^ 1, j, k)),
+        "near": pairs(lambda i, j, k: (i ^ 1, j, k) if 0 < j < ny - 1 else None),
+        "carry": pairs(lambda i, j, k: (i ^ 1, j, k) if j in (0, ny - 1) else None),
         "far": pairs(lambda i, j, k: ((i - 1) % nx if i % 2 == 0 else (i + 1) % nx, j, k)),
         "turn": pairs(turn),
         "C": pairs(lambda i, j, k: (i, j ^ 1, k)),
@@ -104,50 +105,58 @@
     choose(odd_j == 0, even, odd)
 
 
-def pack_x(gas, from_c, from_d, to_near, to_far, to_turn):
+def pack_x(gas, from_c, from_d, to_near, to_carry, to_far, to_turn):
     odd_i, _, _ = places()
     near = (1 - odd_i) * 7
-    to_near[120:128, :] = jnp.zeros((8, 128), F32)
+    to_turn[...] = jnp.zeros((8, 128), F32)
     to_far[80:96, :] = jnp.zeros((16, 128), F32)
-    to_turn[...] = jnp.zeros((8, 128), F32)
     for c in range(5):
-        to_near[c * 24 : c * 24 + 16, :] = gas[rows(c * OWN + near * 16, 16, 16), :]
-        to_near[c * 24 + 16 : c * 24 + 24, :] = from_d[c * 8 : c * 8 + 8, :]
-        to_near[120 + c : 121 + c, :] = from_c[pl.ds(c * 8 + near, 1), :]
         to_far[c * 16 : c * 16 + 16, :] = gas[rows(c * OWN + 112 - near * 16, 16, 16), :]
         to_far[80 + c : 81 + c, :] = from_c[pl.ds(c * 8 + 7 - near, 1), :]
         to_far[88 + c : 89 + c, :] = from_d[pl.ds(c * 8 + 7 - near, 1), :]
         to_turn[c : c + 1, :] = from_d[pl.ds(c * 8 + near, 1), :]
-
-
-def join_halo(gas, from_c, from_d, from_near, from_far, from_turn, after, halo, ends):
+    to_near[80:96, :] = jnp.zeros((16, 128), F32)
+    to_carry[120:128, :] = jnp.zeros((8, 128), F32)
+    for c in range(5):
+        face = gas[rows(c * OWN + near * 16, 16, 16), :]
+        to_near[c * 16 : c * 16 + 16, :] = face
+        to_near[80 + c : 81 + c, :] = from_c[pl.ds(c * 8 + near, 1), :]
+        to_near[88 + c : 89 + c, :] = from_d[pl.ds(c * 8 + near, 1), :]
+        to_carry[c * 24 : c * 24 + 16, :] = face
+        to_carry[c * 24 + 16 : c * 24 + 24, :] = from_d[c * 8 : c * 8 + 8, :]
+        to_carry[120 + c : 121 + c, :] = from_c[pl.ds(c * 8 + near, 1), :]
+
+
+def join_halo(gas, from_c, from_d, from_near, from_carry, from_far, from_turn, after, halo, ends):
     del after
     odd_i, _, wrap = places()
     near = odd_i * 7
     for c in range(5):
         at = c * HALO
-        halo[at : at + 16, :] = from_near[c * 24 : c * 24 + 16, :]
         halo[at + 16 : at + 32, :] = from_far[c * 16 : c * 16 + 16, :]
         halo[at + 32 : at + 40, :] = from_c[c * 8 : c * 8 + 8, :]
         halo[at + 40 : at + 48, :] = jnp.zeros((8, 128), F32)
-        halo[at + 40 : at + 41, :] = from_near[120 + c : 121 + c, :]
         halo[at + 41 : at + 42, :] = from_far[80 + c : 81 + c, :]
         halo[at + 56 : at + 64, :] = jnp.zeros((8, 128), F32)
     halo[5 * HALO : 384, :] = jnp.zeros((384 - 5 * HALO, 128), F32)
 
     def wrapped():
         for c in range(5):
-            at = c * HALO + 48
-            halo[at : at + 8, :] = from_near[c * 24 + 16 : c * 24 + 24, :]
-            halo[at + 8 : at + 9, :] = from_d[pl.ds(c * 8 + near, 1), :]
-            halo[at + 9 : at + 10, :] = from_turn[c : c + 1, :]
+            at = c * HALO
+            halo[at : at + 16, :] = from_carry[c * 24 : c * 24 + 16, :]
+            halo[at + 40 : at + 41, :] = from_carry[120 + c : 121 + c, :]
+            halo[at + 48 : at + 56, :] = from_carry[c * 24 + 16 : c * 24 + 24, :]
+            halo[at + 56 : at + 57, :] = from_d[pl.ds(c * 8 + near, 1), :]
+            halo[at + 57 : at + 58, :] = from_turn[c : c + 1, :]
 
     def inner():
         for c in range(5):
-            at = c * HALO + 48
-            halo[at : at + 8, :] = from_d[c * 8 : c * 8 + 8, :]
-            halo[at + 8 : at + 9, :] = from_near[pl.ds(c * 24 + 16 + near, 1), :]
-            halo[at + 9 : at + 10, :] = from_far[88 + c : 89 + c, :]
+            at = c * HALO
+            halo[at : at + 16, :] = from_near[c * 16 : c * 16 + 16, :]
+            halo[at + 40 : at + 41, :] = from_near[80 + c : 81 + c, :]
+            halo[at + 48 : at + 56, :] = from_d[c * 8 : c * 8 + 8, :]
+            halo[at + 56 : at + 57, :] = from_near[88 + c : 89 + c, :]
+            halo[at + 57 : at + 58, :] = from_far[88 + c : 89 + c, :]
 
     choose(wrap, wrapped, inner)
     turned = []
@@ -287,7 +296,7 @@
             to_d[c * 16 : c * 16 + 16, :] = here[48:64, :]
 
 
-def fold_y(sides, from_c, from_d, to_near, to_far, to_turn):
+def fold_y(sides, from_c, from_d, to_near, to_carry, to_far, to_turn):
     _, odd_j, wrap = places()
     keep = jnp.where(wrap, 0.0, 1.0).astype(F32)
     y = lax.broadcasted_iota(I32, (16, 128), 0)
@@ -303,10 +312,11 @@
                 + jnp.where(at_d, from_d[row : row + 1, :] * keep, 0.0)
             )
             if side == 0:
-                to_near[c * 24 : c * 24 + 16, :] = folded
+                to_near[c * 16 : c * 16 + 16, :] = folded
+                to_carry[c * 24 : c * 24 + 16, :] = folded
             else:
                 to_far[c * 16 : c * 16 + 16, :] = folded
-        to_near[c * 24 + 16 : c * 24 + 24, :] = from_d[c * 16 : c * 16 + 8, :]
+        to_carry[c * 24 + 16 : c * 24 + 24, :] = from_d[c * 16 : c * 16 + 8, :]
         to_turn[c : c + 1, :] = from_d[c * 16 + 9 : c * 16 + 10, :]
 
 
@@ -361,7 +371,7 @@
             )
 
 
-def finish(base, from_near, from_far, from_turn, out):
+def finish(base, from_near, from_carry, from_far, from_turn, out):
     odd_i, odd_j, wrap = places()
     near = (1 - odd_i) * 112
     scale = 0.25 * TIME_INCREMENT
@@ -370,7 +380,9 @@
     out[...] = base[...]
     for c in range(5):
         at = rows(c * OWN + near, 16, 16)
-        out[at, :] = out[at, :] + scale * from_near[c * 24 : c * 24 + 16, :]
+        out[at, :] = out[at, :] + scale * (
+            from_near[c * 16 : c * 16 + 16, :] + from_carry[c * 24 : c * 24 + 16, :]
+        )
         at = rows(c * OWN + 112 - near, 16, 16)
         turned = jnp.where(at_d, from_turn[c : c + 1, :] * gate, 0.0)
         out[at, :] = out[at, :] + scale * from_far[c * 16 : c * 16 + 16, :] + turned
@@ -379,7 +391,7 @@
         def add():
             for c in range(5):
                 at = pl.ds(c * OWN + y, 8, stride=16)
-                out[at, :] = out[at, :] + scale * from_near[c * 24 + 16 : c * 24 + 24, :]
+                out[at, :] = out[at, :] + scale * from_carry[c * 24 + 16 : c * 24 + 24, :]
 
         return add
 
@@ -429,8 +441,12 @@
 
     to_c, to_d = call(pack_y, [((40, 128), F32)] * 2, gas)
     gas_d, gas_c = send(to_d, "D"), send(to_c, "C")
-    to_near, to_far, to_turn = call(pack_x, [((128, 128), F32), ((96, 128), F32), ((8, 128), F32)], gas, gas_c, gas_d)
+    to_near, to_carry, to_far, to_turn = call(
+        pack_x, [((96, 128), F32), ((128, 128), F32), ((96, 128), F32), ((8, 128), F32)],
+        gas, gas_c, gas_d,
+    )
     gas_near, gas_far = send(to_near, "near"), send(to_far, "far")
+    gas_carry = send(to_carry, "carry")
     gas_turn = send(to_turn, "turn")
     planar, vertical, across, part, drops = call(
         weigh,
@@ -446,8 +462,8 @@
     )
     halo, ends = call(
         join_halo, [((384, 128), F32), ends_shape],
-        gas, gas_c, gas_d, gas_near, gas_far, gas_turn, part,
-        loose=(6,),
+        gas, gas_c, gas_d, gas_near, gas_carry, gas_far, gas_turn, part,
+        loose=(7,),
     )
     ends = swap_ends(ends)
     sums, ghosts = call(
@@ -464,15 +480,19 @@
         sums, swap_ends(ghosts),
     )
     dep_d, dep_c = send(to_d, "D"), send(to_c, "C")
-    to_near, to_far, to_turn = call(fold_y, [((120, 128), F32), ((80, 128), F32), ((8, 128), F32)], sides, dep_c, dep_d)
+    to_near, to_carry, to_far, to_turn = call(
+        fold_y, [((80, 128), F32), ((120, 128), F32), ((80, 128), F32), ((8, 128), F32)],
+        sides, dep_c, dep_d,
+    )
     dep_near, dep_far = send(to_near, "near"), send(to_far, "far")
+    dep_carry = send(to_carry, "carry")
     dep_turn = send(to_turn, "turn")
     base = call(
         stencil, ((640, 128), F32),
         gas, start, halo, ends, own, dep_c, dep_d, to_near,
         loose=(7,), scratch=[pltpu.VMEM((128, 128), F32)], flops=1 << 32,
     )
-    out = call(finish, ((640, 128), F32), base, dep_near, dep_far, dep_turn)
+    out = call(finish, ((640, 128), F32), base, dep_near, dep_carry, dep_far, dep_turn)
     return out.reshape(gas_state.shape)
 
 

time: 107 us -> 108 us (level)
  the two profiles are of different devices: /device:TPU:1 before, /device:TPU:6 now
where the time goes in v4:
time: 108 us; the launch traced here: 107 us
  starting transfers between devices  61.1 us (57%)
  waiting for transfers between devices  21.9 us (20%)
  blocking collectives  15.6 us (14%)
  Pallas kernels  6.34 us (6%)
  local copies, waits for them, and re-layouts  1.62 us (2%)
    ppermute x12, starting transfers between devices, send(): return lax.ppermute(values, AXES, routes[route])  61.1 us
    ppermute x12, waiting for transfers between devices, send(): return lax.ppermute(values, AXES, routes[route])  21.9 us
    all_to_all x2, blocking collectives, swap_ends(): return lax.all_to_all(chunks, 'gz', 0, 0).reshape(values.shape)  15.6 us
    pallas_call x9, Pallas kernels, call(): pl.pallas_call(body, out_shape=[jax.ShapeDtypeStruct(s, t) for s, t in ou...  6.34 us
  transfers between devices with their start and end apart: 12, of which 5 were waited for; matrix products, arithmetic and copies ran while one was open for 0% of the time, Pallas kernels for 3%

profile of v4, /device:TPU:6, one launch (start us, length us, event | category | flops | bytes accessed | tf_op | source)
XLA Modules:
  0.0 106.8 jit_solution(17439495433651813443)
XLA Ops:
  0.0 1.0 copy-done
  1.0 1.9 %collective-permute-start = (f32[40,128]{1,0:T(8,128)S(1)}, f32[40,128]{1,0:T(8,128)S(1)}, u32[]{:S(2)}, u32[]{:S(2)}) collective-permute-start(f32[40,128]{1,0:T(8,128)S(1)} %get-tuple-element.28), channel_id=1, source_target_pairs={{0,4},{1,5},{2,6},{3,7},{4,0},{5,1},{6,2},{7,3},{8,12},{9,13},{10,... | collective-permute-start | bytes 61448 | tf_op jit(solution)/shard_map/ppermute | solution.py:424
  2.9 0.0 copy-start.3
  2.9 0.0 copy-start.4
  2.9 18.3 %collective-permute-start.1 = (f32[40,128]{1,0:T(8,128)S(1)}, f32[40,128]{1,0:T(8,128)S(1)}, u32[]{:S(2)}, u32[]{:S(2)}) collective-permute-start(f32[40,128]{1,0:T(8,128)S(1)} %get-tuple-element.29), channel_id=1, source_target_pairs={{0,124},{1,125},{2,126},{3,127},{4,8},{5,9},{6,10},{7,11},{8,4},{9... | collective-permute-start | bytes 61448 | tf_op jit(solution)/shard_map/ppermute | solution.py:424
  21.3 0.0 collective-permute-done.from_c
  21.3 1.4 %collective-permute-done.1.from_d = f32[40,128]{1,0:T(8,128)S(1)} collective-permute-done((f32[40,128]{1,0:T(8,128)S(1)}, f32[40,128]{1,0:T(8,128)S(1)}, u32[]{:S(2)}, u32[]{:S(2)}) %collective-permute-start.1) | collective-permute-done | bytes 20512 | tf_op jit(solution)/shard_map/ppermute | solution.py:424
  22.8 3.5 %collective-permute-start.5 = (f32[8,128]{1,0:T(8,128)S(1)}, f32[8,128]{1,0:T(8,128)S(1)}, u32[]{:S(2)}, u32[]{:S(2)}) collective-permute-start(f32[8,128]{1,0:T(8,128)S(1)} %get-tuple-element.33), channel_id=1, source_target_pairs={{0,128},{1,129},{2,130},{3,131},{60,188},{61,189},{62,190},{63,191... | collective-permute-start | bytes 12296 | tf_op jit(solution)/shard_map/ppermute | solution.py:424
  26.3 8.6 %collective-permute-start.4 = (f32[96,128]{1,0:T(8,128)S(1)}, f32[96,128]{1,0:T(8,128)S(1)}, u32[]{:S(2)}, u32[]{:S(2)}) collective-permute-start(f32[96,128]{1,0:T(8,128)S(1)} %get-tuple-element.32), channel_id=1, source_target_pairs={{0,960},{1,961},{2,962},{3,963},{4,964},{5,965},{6,966},{7,967},{8... | collective-permute-start | bytes 147464 | tf_op jit(solution)/shard_map/ppermute | solution.py:424
  34.8 0.0 copy-start.6
  34.8 0.0 copy-start.5
  34.9 0.7 collective-permute-start.2
  35.5 7.0 %collective-permute-start.3 = (f32[128,128]{1,0:T(8,128)S(1)}, f32[128,128]{1,0:T(8,128)S(1)}, u32[]{:S(2)}, u32[]{:S(2)}) collective-permute-start(f32[128,128]{1,0:T(8,128)S(1)} %get-tuple-element.31), channel_id=1, source_target_pairs={{0,64},{1,65},{2,66},{3,67},{60,124},{61,125},{62,126},{63,127},{6... | collective-permute-start | bytes 196616 | tf_op jit(solution)/shard_map/ppermute | solution.py:424
  42.5 0.0 copy-start.8
  42.6 0.0 copy-start.9
  42.6 0.0 copy-done.3
  42.6 0.0 copy-done.4
  42.6 0.0 copy-done.7
  42.6 0.0 copy-done.6
  42.6 0.0 copy-done.5
  42.6 0.6 copy-done.8
  43.2 0.0 copy-done.9
  43.2 2.2 %shard_map.93 = (bf16[256,2048]{1,0:T(8,128)(2,1)S(1)}, bf16[144,2048]{1,0:T(8,128)(2,1)S(1)}, bf16[2048,256]{1,0:T(8,128)(2,1)S(1)}, f32[80,128]{1,0:T(8,128)S(1)}, f32[96,128]{1,0:T(8,128)S(1)}) custom-call(f32[640,128]{1,0:T(8,128)S(1)} %bitcast.16, s32[16,128]{1,0:T(8,128)S(1)} %bitcast.27, s32[1,16]{1,0:T(1,128)S(1)} %bitcast.30, s32[1,16]{1,0:T(1,128)S(1)} %bitcast.31, ...), custom_call_target="tpu_custom_call" | custom-call | flops 4294967296 | bytes 100000 | tf_op jit(solution)/shard_map/pallas_call | solution.py:407
  45.4 0.0 collective-permute-done.5.from_turn
  45.4 0.0 collective-permute-done.4.from_far
  45.5 0.0 collective-permute-done.2.from_near
  45.5 4.9 %collective-permute-done.3.from_carry = f32[128,128]{1,0:T(8,128)S(1)} collective-permute-done((f32[128,128]{1,0:T(8,128)S(1)}, f32[128,128]{1,0:T(8,128)S(1)}, u32[]{:S(2)}, u32[]{:S(2)}) %collective-permute-start.3) | collective-permute-done | bytes 65568 | tf_op jit(solution)/shard_map/ppermute | solution.py:424
  50.4 0.2 shard_map.94
  50.6 7.9 %all_to_all.10 = f32[4,8,128]{2,1,0:T(8,128)S(1)} all-to-all(f32[4,8,128]{2,1,0:T(8,128)S(1)} %bitcast.22), channel_id=1, replica_groups=mesh['gx'=16,'gy'=16,'gz'=4] {'gz'}, dimensions={0} | all-to-all | bytes 32768 | tf_op jit(solution)/shard_map/all_to_all | solution.py:428
  58.5 2.3 %shard_map.95 = (f32[960,128]{1,0:T(8,128)S(1)}, f32[32,128]{1,0:T(8,128)S(1)}) custom-call(f32[384,128]{1,0:T(8,128)S(1)} %get-tuple-element.35.halo, f32[32,128]{1,0:T(8,128)S(1)} %bitcast.19, bf16[256,2048]{1,0:T(8,128)(2,1)S(1)} %get-tuple-element.37.planar, bf16[144,2048]{1,0:T(8,128)(2,1)S(1)} %get-tuple-element.38.vertical, ...), custom_call_target="tpu_custom_call" | custom-call | flops 10000 | bytes 100000 | tf_op jit(solution)/shard_map/pallas_call | solution.py:407
  60.8 7.7 %all_to_all.11 = f32[4,8,128]{2,1,0:T(8,128)S(1)} all-to-all(f32[4,8,128]{2,1,0:T(8,128)S(1)} %bitcast.23), channel_id=1, replica_groups=mesh['gx'=16,'gy'=16,'gz'=4] {'gz'}, dimensions={0} | all-to-all | bytes 32768 | tf_op jit(solution)/shard_map/all_to_all | solution.py:428
  68.5 0.2 shard_map.96
  68.7 1.9 %collective-permute-start.6 = (f32[80,128]{1,0:T(8,128)S(1)}, f32[80,128]{1,0:T(8,128)S(1)}, u32[]{:S(2)}, u32[]{:S(2)}) collective-permute-start(f32[80,128]{1,0:T(8,128)S(1)} %get-tuple-element.44), channel_id=1, source_target_pairs={{0,4},{1,5},{2,6},{3,7},{4,0},{5,1},{6,2},{7,3},{8,12},{9,13},{10,... | collective-permute-start | bytes 122888 | tf_op jit(solution)/shard_map/ppermute | solution.py:424
  70.7 1.9 %collective-permute-start.7 = (f32[80,128]{1,0:T(8,128)S(1)}, f32[80,128]{1,0:T(8,128)S(1)}, u32[]{:S(2)}, u32[]{:S(2)}) collective-permute-start(f32[80,128]{1,0:T(8,128)S(1)} %get-tuple-element.45), channel_id=1, source_target_pairs={{0,124},{1,125},{2,126},{3,127},{4,8},{5,9},{6,10},{7,11},{8,4},{9... | collective-permute-start | bytes 122888 | tf_op jit(solution)/shard_map/ppermute | solution.py:424
  72.6 0.0 collective-permute-done.6.from_c
  72.6 4.6 %collective-permute-done.7.from_d = f32[80,128]{1,0:T(8,128)S(1)} collective-permute-done((f32[80,128]{1,0:T(8,128)S(1)}, f32[80,128]{1,0:T(8,128)S(1)}, u32[]{:S(2)}, u32[]{:S(2)}) %collective-permute-start.7) | collective-permute-done | bytes 40992 | tf_op jit(solution)/shard_map/ppermute | solution.py:424
  77.2 2.6 %collective-permute-start.11 = (f32[8,128]{1,0:T(8,128)S(1)}, f32[8,128]{1,0:T(8,128)S(1)}, u32[]{:S(2)}, u32[]{:S(2)}) collective-permute-start(f32[8,128]{1,0:T(8,128)S(1)} %get-tuple-element.50), channel_id=1, source_target_pairs={{0,128},{1,129},{2,130},{3,131},{60,188},{61,189},{62,190},{63,191... | collective-permute-start | bytes 12296 | tf_op jit(solution)/shard_map/ppermute | solution.py:424
  79.8 10.7 %collective-permute-start.10 = (f32[80,128]{1,0:T(8,128)S(1)}, f32[80,128]{1,0:T(8,128)S(1)}, u32[]{:S(2)}, u32[]{:S(2)}) collective-permute-start(f32[80,128]{1,0:T(8,128)S(1)} %get-tuple-element.49), channel_id=1, source_target_pairs={{0,960},{1,961},{2,962},{3,963},{4,964},{5,965},{6,966},{7,967},{8... | collective-permute-start | bytes 122888 | tf_op jit(solution)/shard_map/ppermute | solution.py:424
  90.5 0.7 collective-permute-start.8
  91.2 3.3 %collective-permute-start.9 = (f32[120,128]{1,0:T(8,128)S(1)}, f32[120,128]{1,0:T(8,128)S(1)}, u32[]{:S(2)}, u32[]{:S(2)}) collective-permute-start(f32[120,128]{1,0:T(8,128)S(1)} %get-tuple-element.48), channel_id=1, source_target_pairs={{0,64},{1,65},{2,66},{3,67},{60,124},{61,125},{62,126},{63,127},{6... | collective-permute-start | bytes 184328 | tf_op jit(solution)/shard_map/ppermute | solution.py:424
  94.5 0.0 copy-done.1
  94.5 0.0 copy-done.2
  94.5 0.5 shard_map.98.base
  95.1 0.0 collective-permute-done.11.from_turn
  95.1 1.5 %collective-permute-done.10.from_far = f32[80,128]{1,0:T(8,128)S(1)} collective-permute-done((f32[80,128]{1,0:T(8,128)S(1)}, f32[80,128]{1,0:T(8,128)S(1)}, u32[]{:S(2)}, u32[]{:S(2)}) %collective-permute-start.10) | collective-permute-done | bytes 40992 | tf_op jit(solution)/shard_map/ppermute | solution.py:424
  96.5 0.0 collective-permute-done.8.from_near
  96.5 9.5 %collective-permute-done.9.from_carry = f32[120,128]{1,0:T(8,128)S(1)} collective-permute-done((f32[120,128]{1,0:T(8,128)S(1)}, f32[120,128]{1,0:T(8,128)S(1)}, u32[]{:S(2)}, u32[]{:S(2)}) %collective-permute-start.9) | collective-permute-done | bytes 61472 | tf_op jit(solution)/shard_map/ppermute | solution.py:424
  106.0 0.8 shard_map.99
  (7 shorter events, 0.1 us)
Async XLA Ops:
  0.0 1.0 copy-start
  1.0 20.3 %collective-permute-start = (f32[40,128]{1,0:T(8,128)S(1)}, f32[40,128]{1,0:T(8,128)S(1)}, u32[]{:S(2)}, u32[]{:S(2)}) collective-permute-start(f32[40,128]{1,0:T(8,128)S(1)} %get-tuple-element.28), channel_id=1, source_target_pairs={{0,4},{1,5},{2,6},{3,7},{4,0},{5,1},{6,2},{7,3},{8,12},{9,13},{10,... | collective-permute-start | bytes 61448 | tf_op jit(solution)/shard_map/ppermute | solution.py:424
  2.9 39.6 %copy-start.3 = (f32[1,1,1,3,16,128]{5,4,3,2,1,0:T(8,128)S(1)}, f32[1,1,1,3,16,128]{5,4,3,2,1,0:T(8,128)}, u32[]{:S(2)}) copy-start(f32[1,1,1,3,16,128]{5,4,3,2,1,0:T(8,128)} %param.14) | copy-start | bytes 73732
  2.9 39.6 %copy-start.4 = (f32[1,1,1,3,16,128]{5,4,3,2,1,0:T(8,128)S(1)}, f32[1,1,1,3,16,128]{5,4,3,2,1,0:T(8,128)}, u32[]{:S(2)}) copy-start(f32[1,1,1,3,16,128]{5,4,3,2,1,0:T(8,128)} %param.15) | copy-start | bytes 73732
  2.9 19.8 %collective-permute-start.1 = (f32[40,128]{1,0:T(8,128)S(1)}, f32[40,128]{1,0:T(8,128)S(1)}, u32[]{:S(2)}, u32[]{:S(2)}) collective-permute-start(f32[40,128]{1,0:T(8,128)S(1)} %get-tuple-element.29), channel_id=1, source_target_pairs={{0,124},{1,125},{2,126},{3,127},{4,8},{5,9},{6,10},{7,11},{8,4},{9... | collective-permute-start | bytes 61448 | tf_op jit(solution)/shard_map/ppermute | solution.py:424
  22.7 19.8 %copy-start.7 = (f32[1,1,1,16,128]{4,3,2,1,0:T(8,128)S(1)}, f32[1,1,1,16,128]{4,3,2,1,0:T(8,128)}, u32[]{:S(2)}) copy-start(f32[1,1,1,16,128]{4,3,2,1,0:T(8,128)} %param.17) | copy-start | bytes 24580
  22.8 22.7 %collective-permute-start.5 = (f32[8,128]{1,0:T(8,128)S(1)}, f32[8,128]{1,0:T(8,128)S(1)}, u32[]{:S(2)}, u32[]{:S(2)}) collective-permute-start(f32[8,128]{1,0:T(8,128)S(1)} %get-tuple-element.33), channel_id=1, source_target_pairs={{0,128},{1,129},{2,130},{3,131},{60,188},{61,189},{62,190},{63,191... | collective-permute-start | bytes 12296 | tf_op jit(solution)/shard_map/ppermute | solution.py:424
  26.3 19.2 %collective-permute-start.4 = (f32[96,128]{1,0:T(8,128)S(1)}, f32[96,128]{1,0:T(8,128)S(1)}, u32[]{:S(2)}, u32[]{:S(2)}) collective-permute-start(f32[96,128]{1,0:T(8,128)S(1)} %get-tuple-element.32), channel_id=1, source_target_pairs={{0,960},{1,961},{2,962},{3,963},{4,964},{5,965},{6,966},{7,967},{8... | collective-permute-start | bytes 147464 | tf_op jit(solution)/shard_map/ppermute | solution.py:424
  34.8 7.8 %copy-start.6 = (f32[1,1,1,16,128]{4,3,2,1,0:T(8,128)S(1)}, f32[1,1,1,16,128]{4,3,2,1,0:T(8,128)}, u32[]{:S(2)}) copy-start(f32[1,1,1,16,128]{4,3,2,1,0:T(8,128)} %param.16) | copy-start | bytes 24580
  34.8 7.8 %copy-start.5 = (s32[1,1,1,16,128]{4,3,2,1,0:T(8,128)S(1)}, s32[1,1,1,16,128]{4,3,2,1,0:T(8,128)}, u32[]{:S(2)}) copy-start(s32[1,1,1,16,128]{4,3,2,1,0:T(8,128)} %param.11) | copy-start | bytes 24580
  34.9 10.6 %collective-permute-start.2 = (f32[96,128]{1,0:T(8,128)S(1)}, f32[96,128]{1,0:T(8,128)S(1)}, u32[]{:S(2)}, u32[]{:S(2)}) collective-permute-start(f32[96,128]{1,0:T(8,128)S(1)} %get-tuple-element.30.after), channel_id=1, source_target_pairs={{4,68},{5,69},{6,70},{7,71},{8,72},{9,73},{10,74},{11,75},{12,76},... | collective-permute-start | bytes 147464 | tf_op jit(solution)/shard_map/ppermute | solution.py:424
  35.5 14.9 %collective-permute-start.3 = (f32[128,128]{1,0:T(8,128)S(1)}, f32[128,128]{1,0:T(8,128)S(1)}, u32[]{:S(2)}, u32[]{:S(2)}) collective-permute-start(f32[128,128]{1,0:T(8,128)S(1)} %get-tuple-element.31), channel_id=1, source_target_pairs={{0,64},{1,65},{2,66},{3,67},{60,124},{61,125},{62,126},{63,127},{6... | collective-permute-start | bytes 196616 | tf_op jit(solution)/shard_map/ppermute | solution.py:424
  42.5 0.7 copy-start.8
  42.6 0.7 copy-start.9
  68.5 26.0 %copy-start.1 = (f32[5,8,16,128]{3,2,1,0:T(8,128)S(1)}, f32[5,8,16,128]{3,2,1,0:T(8,128)}, u32[]{:S(2)}) copy-start(f32[5,8,16,128]{3,2,1,0:T(8,128)} %param.9) | copy-start | bytes 983044
  68.5 26.0 %copy-start.2 = (f32[5,8,16,128]{3,2,1,0:T(8,128)S(1)}, f32[5,8,16,128]{3,2,1,0:T(8,128)}, u32[]{:S(2)}) copy-start(f32[5,8,16,128]{3,2,1,0:T(8,128)} %param.10) | copy-start | bytes 983044
  68.7 3.9 %collective-permute-start.6 = (f32[80,128]{1,0:T(8,128)S(1)}, f32[80,128]{1,0:T(8,128)S(1)}, u32[]{:S(2)}, u32[]{:S(2)}) collective-permute-start(f32[80,128]{1,0:T(8,128)S(1)} %get-tuple-element.44), channel_id=1, source_target_pairs={{0,4},{1,5},{2,6},{3,7},{4,0},{5,1},{6,2},{7,3},{8,12},{9,13},{10,... | collective-permute-start | bytes 122888 | tf_op jit(solution)/shard_map/ppermute | solution.py:424
  70.7 6.5 %collective-permute-start.7 = (f32[80,128]{1,0:T(8,128)S(1)}, f32[80,128]{1,0:T(8,128)S(1)}, u32[]{:S(2)}, u32[]{:S(2)}) collective-permute-start(f32[80,128]{1,0:T(8,128)S(1)} %get-tuple-element.45), channel_id=1, source_target_pairs={{0,124},{1,125},{2,126},{3,127},{4,8},{5,9},{6,10},{7,11},{8,4},{9... | collective-permute-start | bytes 122888 | tf_op jit(solution)/shard_map/ppermute | solution.py:424
  77.2 17.9 %collective-permute-start.11 = (f32[8,128]{1,0:T(8,128)S(1)}, f32[8,128]{1,0:T(8,128)S(1)}, u32[]{:S(2)}, u32[]{:S(2)}) collective-permute-start(f32[8,128]{1,0:T(8,128)S(1)} %get-tuple-element.50), channel_id=1, source_target_pairs={{0,128},{1,129},{2,130},{3,131},{60,188},{61,189},{62,190},{63,191... | collective-permute-start | bytes 12296 | tf_op jit(solution)/shard_map/ppermute | solution.py:424
  79.8 16.7 %collective-permute-start.10 = (f32[80,128]{1,0:T(8,128)S(1)}, f32[80,128]{1,0:T(8,128)S(1)}, u32[]{:S(2)}, u32[]{:S(2)}) collective-permute-start(f32[80,128]{1,0:T(8,128)S(1)} %get-tuple-element.49), channel_id=1, source_target_pairs={{0,960},{1,961},{2,962},{3,963},{4,964},{5,965},{6,966},{7,967},{8... | collective-permute-start | bytes 122888 | tf_op jit(solution)/shard_map/ppermute | solution.py:424
  90.5 6.0 %collective-permute-start.8 = (f32[80,128]{1,0:T(8,128)S(1)}, f32[80,128]{1,0:T(8,128)S(1)}, u32[]{:S(2)}, u32[]{:S(2)}) collective-permute-start(f32[80,128]{1,0:T(8,128)S(1)} %get-tuple-element.47.after), channel_id=1, source_target_pairs={{4,68},{5,69},{6,70},{7,71},{8,72},{9,73},{10,74},{11,75},{12,76},... | collective-permute-start | bytes 122888 | tf_op jit(solution)/shard_map/ppermute | solution.py:424
  91.2 14.8 %collective-permute-start.9 = (f32[120,128]{1,0:T(8,128)S(1)}, f32[120,128]{1,0:T(8,128)S(1)}, u32[]{:S(2)}, u32[]{:S(2)}) collective-permute-start(f32[120,128]{1,0:T(8,128)S(1)} %get-tuple-element.48), channel_id=1, source_target_pairs={{0,64},{1,65},{2,66},{3,67},{60,124},{61,125},{62,126},{63,127},{6... | collective-permute-start | bytes 184328 | tf_op jit(solution)/shard_map/ppermute | solution.py:424

commit v5 on v4

--- a/solution.py
+++ b/solution.py
@@ -87,25 +87,16 @@
     pl.when(jnp.logical_not(cond))(no)
 
 
-def pack_y(gas, to_c, to_d):
-    _, odd_j, _ = places()
-
-    def put(ref, y):
-        for c in range(5):
-            ref[c * 8 : c * 8 + 8, :] = gas[pl.ds(c * OWN + y, 8, stride=16), :]
-
-    def even():
-        put(to_c, 15)
-        put(to_d, 0)
-
-    def odd():
-        put(to_c, 0)
-        put(to_d, 15)
-
-    choose(odd_j == 0, even, odd)
-
-
-def pack_x(gas, from_c, from_d, to_near, to_carry, to_far, to_turn):
+def own_ends(gas, low_high):
+    low_high[...] = jnp.zeros((16, 128), F32)
+    for c in range(5):
+        turned = gas[c * OWN : c * OWN + OWN, :].T
+        low_high[c : c + 1, :] = turned[0:1, :]
+        low_high[8 + c : 9 + c, :] = turned[127:128, :]
+
+
+def pack_x(gas, from_c, from_d, after, to_near, to_carry, to_far, to_turn):
+    del after
     odd_i, _, _ = places()
     near = (1 - odd_i) * 7
     to_turn[...] = jnp.zeros((8, 128), F32)
@@ -127,7 +118,7 @@
         to_carry[120 + c : 121 + c, :] = from_c[pl.ds(c * 8 + near, 1), :]
 
 
-def join_halo(gas, from_c, from_d, from_near, from_carry, from_far, from_turn, after, halo, ends):
+def join_halo(own, from_c, from_d, from_near, from_carry, from_far, from_turn, after, halo, ends):
     del after
     odd_i, _, wrap = places()
     near = odd_i * 7
@@ -159,11 +150,12 @@
             halo[at + 57 : at + 58, :] = from_far[88 + c : 89 + c, :]
 
     choose(wrap, wrapped, inner)
-    turned = []
-    for n in range(8):
-        part = gas[n * 128 : n * 128 + 128, :] if n < 5 else halo[(n - 5) * 128 : (n - 4) * 128, :]
-        turned.append(part.T)
-    post_ends(ends, [t[0:1, :] for t in turned], [t[127:128, :] for t in turned])
+    turned = [halo[n * 128 : n * 128 + 128, :].T for n in range(3)]
+    post_ends(
+        ends,
+        [own[0:5, :]] + [t[0:1, :] for t in turned],
+        [own[8:13, :]] + [t[127:128, :] for t in turned],
+    )
 
 
 def three(place, anchor, offset):
@@ -439,11 +431,15 @@
     count = droplets_per_block.reshape(1, blocks)
     tile = block_tile.reshape(1, blocks)
 
-    to_c, to_d = call(pack_y, [((40, 128), F32)] * 2, gas)
+    odd_j = lax.rem(lax.axis_index("gy"), 2)
+    low, high = gas_state[:, :, 0, :].reshape(40, 128), gas_state[:, :, 15, :].reshape(40, 128)
+    to_c, to_d = jnp.where(odd_j == 0, high, low), jnp.where(odd_j == 0, low, high)
+    own_z = call(own_ends, ((16, 128), F32), gas, flops=1 << 32)
     gas_d, gas_c = send(to_d, "D"), send(to_c, "C")
     to_near, to_carry, to_far, to_turn = call(
         pack_x, [((96, 128), F32), ((128, 128), F32), ((96, 128), F32), ((8, 128), F32)],
-        gas, gas_c, gas_d,
+        gas, gas_c, gas_d, own_z,
+        loose=(3,),
     )
     gas_near, gas_far = send(to_near, "near"), send(to_far, "far")
     gas_carry = send(to_carry, "carry")
@@ -462,7 +458,7 @@
     )
     halo, ends = call(
         join_halo, [((384, 128), F32), ends_shape],
-        gas, gas_c, gas_d, gas_near, gas_carry, gas_far, gas_turn, part,
+        own_z, gas_c, gas_d, gas_near, gas_carry, gas_far, gas_turn, part,
         loose=(7,),
     )
     ends = swap_ends(ends)

time: 108 us -> 108 us (level)
  waiting for transfers between devices: 21.9 us -> 20.7 us
    ppermute x12, waiting for transfers between devices: 21.9 us -> 20.7 us  [send(): return lax.ppermute(values, AXES, routes[route])]
where the time goes in v5:
time: 108 us; the launch traced here: 107 us
  starting transfers between devices  61.1 us (57%)
  waiting for transfers between devices  20.7 us (19%)
  blocking collectives  15.6 us (14%)
  Pallas kernels  6.4 us (6%)
  local copies, waits for them, and re-layouts  1.61 us (1%)
    ppermute x12, starting transfers between devices, send(): return lax.ppermute(values, AXES, routes[route])  61.1 us
    ppermute x12, waiting for transfers between devices, send(): return lax.ppermute(values, AXES, routes[route])  20.7 us
    all_to_all x2, blocking collectives, swap_ends(): return lax.all_to_all(chunks, 'gz', 0, 0).reshape(values.shape)  15.6 us
    pallas_call x9, Pallas kernels, call(): pl.pallas_call(body, out_shape=[jax.ShapeDtypeStruct(s, t) for s, t in ou...  6.4 us
  transfers between devices with their start and end apart: 12, of which 5 were waited for; matrix products, arithmetic and copies ran while one was open for 0% of the time, Pallas kernels for 3%

profile of v5, /device:TPU:6, one launch (start us, length us, event | category | flops | bytes accessed | tf_op | source)
XLA Modules:
  0.0 106.7 jit_solution(3597390726993374267)
XLA Ops:
  0.0 1.0 broadcast_select_fusion
  1.0 1.9 %collective-permute-start = (f32[40,128]{1,0:T(8,128)S(1)}, f32[40,128]{1,0:T(8,128)S(1)}, u32[]{:S(2)}, u32[]{:S(2)}) collective-permute-start(f32[40,128]{1,0:T(8,128)S(1)} %bitcast.34), channel_id=1, source_target_pairs={{0,4},{1,5},{2,6},{3,7},{4,0},{5,1},{6,2},{7,3},{8,12},{9,13},{10,... | collective-permute-start | bytes 61448 | tf_op jit(solution)/shard_map/ppermute | solution.py:416
  3.0 18.3 %collective-permute-start.1 = (f32[40,128]{1,0:T(8,128)S(1)}, f32[40,128]{1,0:T(8,128)S(1)}, u32[]{:S(2)}, u32[]{:S(2)}) collective-permute-start(f32[40,128]{1,0:T(8,128)S(1)} %bitcast.33), channel_id=1, source_target_pairs={{0,124},{1,125},{2,126},{3,127},{4,8},{5,9},{6,10},{7,11},{8,4},{9... | collective-permute-start | bytes 61448 | tf_op jit(solution)/shard_map/ppermute | solution.py:416
  21.3 0.0 copy-start
  21.3 1.0 copy-done
  22.3 0.1 shard_map.91.after.own
  22.4 0.0 copy-start.3
  22.4 0.0 copy-start.4
  22.4 0.0 collective-permute-done.from_c
  22.5 0.3 collective-permute-done.1.from_d
  22.8 3.5 %collective-permute-start.5 = (f32[8,128]{1,0:T(8,128)S(1)}, f32[8,128]{1,0:T(8,128)S(1)}, u32[]{:S(2)}, u32[]{:S(2)}) collective-permute-start(f32[8,128]{1,0:T(8,128)S(1)} %get-tuple-element.29), channel_id=1, source_target_pairs={{0,128},{1,129},{2,130},{3,131},{60,188},{61,189},{62,190},{63,191... | collective-permute-start | bytes 12296 | tf_op jit(solution)/shard_map/ppermute | solution.py:416
  26.3 8.6 %collective-permute-start.4 = (f32[96,128]{1,0:T(8,128)S(1)}, f32[96,128]{1,0:T(8,128)S(1)}, u32[]{:S(2)}, u32[]{:S(2)}) collective-permute-start(f32[96,128]{1,0:T(8,128)S(1)} %get-tuple-element.28), channel_id=1, source_target_pairs={{0,960},{1,961},{2,962},{3,963},{4,964},{5,965},{6,966},{7,967},{8... | collective-permute-start | bytes 147464 | tf_op jit(solution)/shard_map/ppermute | solution.py:416
  34.8 0.0 copy-start.6
  34.8 0.0 copy-start.5
  34.9 0.7 collective-permute-start.2
  35.5 7.0 %collective-permute-start.3 = (f32[128,128]{1,0:T(8,128)S(1)}, f32[128,128]{1,0:T(8,128)S(1)}, u32[]{:S(2)}, u32[]{:S(2)}) collective-permute-start(f32[128,128]{1,0:T(8,128)S(1)} %get-tuple-element.27), channel_id=1, source_target_pairs={{0,64},{1,65},{2,66},{3,67},{60,124},{61,125},{62,126},{63,127},{6... | collective-permute-start | bytes 196616 | tf_op jit(solution)/shard_map/ppermute | solution.py:416
  42.6 0.0 copy-start.8
  42.6 0.0 copy-start.9
  42.6 0.0 copy-done.3
  42.6 0.0 copy-done.4
  42.6 0.6 copy-done.8
  43.2 0.0 copy-done.9
  43.2 2.2 %shard_map.93 = (bf16[256,2048]{1,0:T(8,128)(2,1)S(1)}, bf16[144,2048]{1,0:T(8,128)(2,1)S(1)}, bf16[2048,256]{1,0:T(8,128)(2,1)S(1)}, f32[80,128]{1,0:T(8,128)S(1)}, f32[96,128]{1,0:T(8,128)S(1)}) custom-call(f32[640,128]{1,0:T(8,128)S(1)} %bitcast.18, s32[16,128]{1,0:T(8,128)S(1)} %bitcast.28, s32[1,16]{1,0:T(1,128)S(1)} %bitcast.31, s32[1,16]{1,0:T(1,128)S(1)} %bitcast.32, ...), custom_call_target="tpu_custom_call" | custom-call | flops 4294967296 | bytes 100000 | tf_op jit(solution)/shard_map/pallas_call | solution.py:399
  45.4 0.0 collective-permute-done.5.from_turn
  45.5 0.0 collective-permute-done.4.from_far
  45.5 0.0 collective-permute-done.2.from_near
  45.5 4.9 %collective-permute-done.3.from_carry = f32[128,128]{1,0:T(8,128)S(1)} collective-permute-done((f32[128,128]{1,0:T(8,128)S(1)}, f32[128,128]{1,0:T(8,128)S(1)}, u32[]{:S(2)}, u32[]{:S(2)}) %collective-permute-start.3) | collective-permute-done | bytes 65568 | tf_op jit(solution)/shard_map/ppermute | solution.py:416
  50.4 0.1 shard_map.94
  50.5 7.9 %all_to_all.10 = f32[4,8,128]{2,1,0:T(8,128)S(1)} all-to-all(f32[4,8,128]{2,1,0:T(8,128)S(1)} %bitcast.23), channel_id=1, replica_groups=mesh['gx'=16,'gy'=16,'gz'=4] {'gz'}, dimensions={0} | all-to-all | bytes 32768 | tf_op jit(solution)/shard_map/all_to_all | solution.py:420
  58.4 2.3 %shard_map.95 = (f32[960,128]{1,0:T(8,128)S(1)}, f32[32,128]{1,0:T(8,128)S(1)}) custom-call(f32[384,128]{1,0:T(8,128)S(1)} %get-tuple-element.31.halo, f32[32,128]{1,0:T(8,128)S(1)} %bitcast.20, bf16[256,2048]{1,0:T(8,128)(2,1)S(1)} %get-tuple-element.33.planar, bf16[144,2048]{1,0:T(8,128)(2,1)S(1)} %get-tuple-element.34.vertical, ...), custom_call_target="tpu_custom_call" | custom-call | flops 10000 | bytes 100000 | tf_op jit(solution)/shard_map/pallas_call | solution.py:399
  60.7 7.7 %all_to_all.11 = f32[4,8,128]{2,1,0:T(8,128)S(1)} all-to-all(f32[4,8,128]{2,1,0:T(8,128)S(1)} %bitcast.24), channel_id=1, replica_groups=mesh['gx'=16,'gy'=16,'gz'=4] {'gz'}, dimensions={0} | all-to-all | bytes 32768 | tf_op jit(solution)/shard_map/all_to_all | solution.py:420
  68.5 0.2 shard_map.96
  68.7 1.9 %collective-permute-start.6 = (f32[80,128]{1,0:T(8,128)S(1)}, f32[80,128]{1,0:T(8,128)S(1)}, u32[]{:S(2)}, u32[]{:S(2)}) collective-permute-start(f32[80,128]{1,0:T(8,128)S(1)} %get-tuple-element.40), channel_id=1, source_target_pairs={{0,4},{1,5},{2,6},{3,7},{4,0},{5,1},{6,2},{7,3},{8,12},{9,13},{10,... | collective-permute-start | bytes 122888 | tf_op jit(solution)/shard_map/ppermute | solution.py:416
  70.6 1.9 %collective-permute-start.7 = (f32[80,128]{1,0:T(8,128)S(1)}, f32[80,128]{1,0:T(8,128)S(1)}, u32[]{:S(2)}, u32[]{:S(2)}) collective-permute-start(f32[80,128]{1,0:T(8,128)S(1)} %get-tuple-element.41), channel_id=1, source_target_pairs={{0,124},{1,125},{2,126},{3,127},{4,8},{5,9},{6,10},{7,11},{8,4},{9... | collective-permute-start | bytes 122888 | tf_op jit(solution)/shard_map/ppermute | solution.py:416
  72.5 0.0 collective-permute-done.6.from_c
  72.5 4.6 %collective-permute-done.7.from_d = f32[80,128]{1,0:T(8,128)S(1)} collective-permute-done((f32[80,128]{1,0:T(8,128)S(1)}, f32[80,128]{1,0:T(8,128)S(1)}, u32[]{:S(2)}, u32[]{:S(2)}) %collective-permute-start.7) | collective-permute-done | bytes 40992 | tf_op jit(solution)/shard_map/ppermute | solution.py:416
  77.2 2.6 %collective-permute-start.11 = (f32[8,128]{1,0:T(8,128)S(1)}, f32[8,128]{1,0:T(8,128)S(1)}, u32[]{:S(2)}, u32[]{:S(2)}) collective-permute-start(f32[8,128]{1,0:T(8,128)S(1)} %get-tuple-element.46), channel_id=1, source_target_pairs={{0,128},{1,129},{2,130},{3,131},{60,188},{61,189},{62,190},{63,191... | collective-permute-start | bytes 12296 | tf_op jit(solution)/shard_map/ppermute | solution.py:416
  79.7 10.7 %collective-permute-start.10 = (f32[80,128]{1,0:T(8,128)S(1)}, f32[80,128]{1,0:T(8,128)S(1)}, u32[]{:S(2)}, u32[]{:S(2)}) collective-permute-start(f32[80,128]{1,0:T(8,128)S(1)} %get-tuple-element.45), channel_id=1, source_target_pairs={{0,960},{1,961},{2,962},{3,963},{4,964},{5,965},{6,966},{7,967},{8... | collective-permute-start | bytes 122888 | tf_op jit(solution)/shard_map/ppermute | solution.py:416
  90.4 0.7 collective-permute-start.8
  91.1 3.3 %collective-permute-start.9 = (f32[120,128]{1,0:T(8,128)S(1)}, f32[120,128]{1,0:T(8,128)S(1)}, u32[]{:S(2)}, u32[]{:S(2)}) collective-permute-start(f32[120,128]{1,0:T(8,128)S(1)} %get-tuple-element.44), channel_id=1, source_target_pairs={{0,64},{1,65},{2,66},{3,67},{60,124},{61,125},{62,126},{63,127},{6... | collective-permute-start | bytes 184328 | tf_op jit(solution)/shard_map/ppermute | solution.py:416
  94.4 0.0 copy-done.1
  94.4 0.0 copy-done.2
  94.5 0.5 shard_map.98.base
  95.0 0.0 collective-permute-done.11.from_turn
  95.0 1.4 %collective-permute-done.10.from_far = f32[80,128]{1,0:T(8,128)S(1)} collective-permute-done((f32[80,128]{1,0:T(8,128)S(1)}, f32[80,128]{1,0:T(8,128)S(1)}, u32[]{:S(2)}, u32[]{:S(2)}) %collective-permute-start.10) | collective-permute-done | bytes 40992 | tf_op jit(solution)/shard_map/ppermute | solution.py:416
  96.5 0.0 collective-permute-done.8.from_near
  96.5 9.5 %collective-permute-done.9.from_carry = f32[120,128]{1,0:T(8,128)S(1)} collective-permute-done((f32[120,128]{1,0:T(8,128)S(1)}, f32[120,128]{1,0:T(8,128)S(1)}, u32[]{:S(2)}, u32[]{:S(2)}) %collective-permute-start.9) | collective-permute-done | bytes 61472 | tf_op jit(solution)/shard_map/ppermute | solution.py:416
  105.9 0.8 shard_map.99
  (8 shorter events, 0.1 us)
Async XLA Ops:
  1.0 21.4 %collective-permute-start = (f32[40,128]{1,0:T(8,128)S(1)}, f32[40,128]{1,0:T(8,128)S(1)}, u32[]{:S(2)}, u32[]{:S(2)}) collective-permute-start(f32[40,128]{1,0:T(8,128)S(1)} %bitcast.34), channel_id=1, source_target_pairs={{0,4},{1,5},{2,6},{3,7},{4,0},{5,1},{6,2},{7,3},{8,12},{9,13},{10,... | collective-permute-start | bytes 61448 | tf_op jit(solution)/shard_map/ppermute | solution.py:416
  3.0 19.8 %collective-permute-start.1 = (f32[40,128]{1,0:T(8,128)S(1)}, f32[40,128]{1,0:T(8,128)S(1)}, u32[]{:S(2)}, u32[]{:S(2)}) collective-permute-start(f32[40,128]{1,0:T(8,128)S(1)} %bitcast.33), channel_id=1, source_target_pairs={{0,124},{1,125},{2,126},{3,127},{4,8},{5,9},{6,10},{7,11},{8,4},{9... | collective-permute-start | bytes 61448 | tf_op jit(solution)/shard_map/ppermute | solution.py:416
  21.3 1.0 copy-start
  22.4 20.2 %copy-start.3 = (f32[1,1,1,3,16,128]{5,4,3,2,1,0:T(8,128)S(1)}, f32[1,1,1,3,16,128]{5,4,3,2,1,0:T(8,128)}, u32[]{:S(2)}) copy-start(f32[1,1,1,3,16,128]{5,4,3,2,1,0:T(8,128)} %param.14) | copy-start | bytes 73732
  22.4 20.2 %copy-start.4 = (f32[1,1,1,3,16,128]{5,4,3,2,1,0:T(8,128)S(1)}, f32[1,1,1,3,16,128]{5,4,3,2,1,0:T(8,128)}, u32[]{:S(2)}) copy-start(f32[1,1,1,3,16,128]{5,4,3,2,1,0:T(8,128)} %param.15) | copy-start | bytes 73732
  22.8 19.8 %copy-start.7 = (f32[1,1,1,16,128]{4,3,2,1,0:T(8,128)S(1)}, f32[1,1,1,16,128]{4,3,2,1,0:T(8,128)}, u32[]{:S(2)}) copy-start(f32[1,1,1,16,128]{4,3,2,1,0:T(8,128)} %param.17) | copy-start | bytes 24580
  22.8 22.7 %collective-permute-start.5 = (f32[8,128]{1,0:T(8,128)S(1)}, f32[8,128]{1,0:T(8,128)S(1)}, u32[]{:S(2)}, u32[]{:S(2)}) collective-permute-start(f32[8,128]{1,0:T(8,128)S(1)} %get-tuple-element.29), channel_id=1, source_target_pairs={{0,128},{1,129},{2,130},{3,131},{60,188},{61,189},{62,190},{63,191... | collective-permute-start | bytes 12296 | tf_op jit(solution)/shard_map/ppermute | solution.py:416
  26.3 19.2 %collective-permute-start.4 = (f32[96,128]{1,0:T(8,128)S(1)}, f32[96,128]{1,0:T(8,128)S(1)}, u32[]{:S(2)}, u32[]{:S(2)}) collective-permute-start(f32[96,128]{1,0:T(8,128)S(1)} %get-tuple-element.28), channel_id=1, source_target_pairs={{0,960},{1,961},{2,962},{3,963},{4,964},{5,965},{6,966},{7,967},{8... | collective-permute-start | bytes 147464 | tf_op jit(solution)/shard_map/ppermute | solution.py:416
  34.8 7.8 %copy-start.6 = (f32[1,1,1,16,128]{4,3,2,1,0:T(8,128)S(1)}, f32[1,1,1,16,128]{4,3,2,1,0:T(8,128)}, u32[]{:S(2)}) copy-start(f32[1,1,1,16,128]{4,3,2,1,0:T(8,128)} %param.16) | copy-start | bytes 24580
  34.8 7.8 %copy-start.5 = (s32[1,1,1,16,128]{4,3,2,1,0:T(8,128)S(1)}, s32[1,1,1,16,128]{4,3,2,1,0:T(8,128)}, u32[]{:S(2)}) copy-start(s32[1,1,1,16,128]{4,3,2,1,0:T(8,128)} %param.11) | copy-start | bytes 24580
  34.9 10.6 %collective-permute-start.2 = (f32[96,128]{1,0:T(8,128)S(1)}, f32[96,128]{1,0:T(8,128)S(1)}, u32[]{:S(2)}, u32[]{:S(2)}) collective-permute-start(f32[96,128]{1,0:T(8,128)S(1)} %get-tuple-element.26.after), channel_id=1, source_target_pairs={{4,68},{5,69},{6,70},{7,71},{8,72},{9,73},{10,74},{11,75},{12,76},... | collective-permute-start | bytes 147464 | tf_op jit(solution)/shard_map/ppermute | solution.py:416
  35.5 14.9 %collective-permute-start.3 = (f32[128,128]{1,0:T(8,128)S(1)}, f32[128,128]{1,0:T(8,128)S(1)}, u32[]{:S(2)}, u32[]{:S(2)}) collective-permute-start(f32[128,128]{1,0:T(8,128)S(1)} %get-tuple-element.27), channel_id=1, source_target_pairs={{0,64},{1,65},{2,66},{3,67},{60,124},{61,125},{62,126},{63,127},{6... | collective-permute-start | bytes 196616 | tf_op jit(solution)/shard_map/ppermute | solution.py:416
  42.6 0.7 copy-start.8
  42.6 0.7 copy-start.9
  68.4 26.0 %copy-start.1 = (f32[5,8,16,128]{3,2,1,0:T(8,128)S(1)}, f32[5,8,16,128]{3,2,1,0:T(8,128)}, u32[]{:S(2)}) copy-start(f32[5,8,16,128]{3,2,1,0:T(8,128)} %param.9) | copy-start | bytes 983044
  68.5 26.0 %copy-start.2 = (f32[5,8,16,128]{3,2,1,0:T(8,128)S(1)}, f32[5,8,16,128]{3,2,1,0:T(8,128)}, u32[]{:S(2)}) copy-start(f32[5,8,16,128]{3,2,1,0:T(8,128)} %param.10) | copy-start | bytes 983044
  68.7 3.9 %collective-permute-start.6 = (f32[80,128]{1,0:T(8,128)S(1)}, f32[80,128]{1,0:T(8,128)S(1)}, u32[]{:S(2)}, u32[]{:S(2)}) collective-permute-start(f32[80,128]{1,0:T(8,128)S(1)} %get-tuple-element.40), channel_id=1, source_target_pairs={{0,4},{1,5},{2,6},{3,7},{4,0},{5,1},{6,2},{7,3},{8,12},{9,13},{10,... | collective-permute-start | bytes 122888 | tf_op jit(solution)/shard_map/ppermute | solution.py:416
  70.6 6.5 %collective-permute-start.7 = (f32[80,128]{1,0:T(8,128)S(1)}, f32[80,128]{1,0:T(8,128)S(1)}, u32[]{:S(2)}, u32[]{:S(2)}) collective-permute-start(f32[80,128]{1,0:T(8,128)S(1)} %get-tuple-element.41), channel_id=1, source_target_pairs={{0,124},{1,125},{2,126},{3,127},{4,8},{5,9},{6,10},{7,11},{8,4},{9... | collective-permute-start | bytes 122888 | tf_op jit(solution)/shard_map/ppermute | solution.py:416
  77.2 17.9 %collective-permute-start.11 = (f32[8,128]{1,0:T(8,128)S(1)}, f32[8,128]{1,0:T(8,128)S(1)}, u32[]{:S(2)}, u32[]{:S(2)}) collective-permute-start(f32[8,128]{1,0:T(8,128)S(1)} %get-tuple-element.46), channel_id=1, source_target_pairs={{0,128},{1,129},{2,130},{3,131},{60,188},{61,189},{62,190},{63,191... | collective-permute-start | bytes 12296 | tf_op jit(solution)/shard_map/ppermute | solution.py:416
  79.7 16.7 %collective-permute-start.10 = (f32[80,128]{1,0:T(8,128)S(1)}, f32[80,128]{1,0:T(8,128)S(1)}, u32[]{:S(2)}, u32[]{:S(2)}) collective-permute-start(f32[80,128]{1,0:T(8,128)S(1)} %get-tuple-element.45), channel_id=1, source_target_pairs={{0,960},{1,961},{2,962},{3,963},{4,964},{5,965},{6,966},{7,967},{8... | collective-permute-start | bytes 122888 | tf_op jit(solution)/shard_map/ppermute | solution.py:416
  90.4 6.0 %collective-permute-start.8 = (f32[80,128]{1,0:T(8,128)S(1)}, f32[80,128]{1,0:T(8,128)S(1)}, u32[]{:S(2)}, u32[]{:S(2)}) collective-permute-start(f32[80,128]{1,0:T(8,128)S(1)} %get-tuple-element.43.after), channel_id=1, source_target_pairs={{4,68},{5,69},{6,70},{7,71},{8,72},{9,73},{10,74},{11,75},{12,76},... | collective-permute-start | bytes 122888 | tf_op jit(solution)/shard_map/ppermute | solution.py:416
  91.1 14.8 %collective-permute-start.9 = (f32[120,128]{1,0:T(8,128)S(1)}, f32[120,128]{1,0:T(8,128)S(1)}, u32[]{:S(2)}, u32[]{:S(2)}) collective-permute-start(f32[120,128]{1,0:T(8,128)S(1)} %get-tuple-element.44), channel_id=1, source_target_pairs={{0,64},{1,65},{2,66},{3,67},{60,124},{61,125},{62,126},{63,127},{6... | collective-permute-start | bytes 184328 | tf_op jit(solution)/shard_map/ppermute | solution.py:416
